TPU v7x, 32 devices: a whole 2x2x4 slice. The times are simulated.
32 devices in a mesh: view: 8 (over z, y), head: 4 (over x, core).
Axes of the slice: x: 2, y: 2, z: 4, core: 2. Of those that a mesh axis runs over, the one named last changes fastest.
Arguments:
- query_rows: bfloat16 [8192, 1024], P('view', 'head'), may hold values from -20 to 20
- key_rows: bfloat16 [8192, 1024], P('view', 'head'), may hold values from -6 to 6
- value_rows: bfloat16 [8192, 1024], P('view', 'head'), may hold values from -12 to 12
- out_weight: bfloat16 [1024, 1024], replicated, may hold values from -0.1875 to 0.1875
- out_grad: bfloat16 [8192, 1024], P('view', 'head'), may hold values from -12 to 12
- source_view: int32 [8, 16], replicated, may hold values from 0 to 7, as said below
- source_block: int32 [8, 16], replicated, may hold values from 0 to 7
Outputs:
- mixed_out: bfloat16 [8192, 1024], P('view', 'head')
- query_grad: bfloat16 [8192, 1024], P('view', 'head')
- key_grad: bfloat16 [8192, 1024], P('view', 'head')
- value_grad: bfloat16 [8192, 1024], P('view', 'head')
Inputs may be any that keep to these rules, and one draw needn't show every extreme that they name: `source_view`: for each query view the 16 slots name distinct pairs of source view and block. No source view is named by more than 4 slots of one query view, and for every query view some source view is named by exactly 4 of its slots.
All inputs are finite; a program needn't handle non-finite values.
Results may differ from a plain program's by a relative error of at most 0.014.
Values may be sent and summed in bfloat16 or wider, within the bound.
No kernel may reach another device: no remote copies, remote signals or barrier semaphores. Data moves between devices by JAX's collectives and lax.ppermute only.
A program may use at most 128 MiB of HBM per device.

v0:
```python
import jax
import jax.numpy as jnp
from jax import lax
from jax.sharding import PartitionSpec as P

HEAD_DIM = 64
BLOCK_TOKENS = 128


def score_rows(query_part, key_heads, score_scale):
    return (
        jnp.einsum("qhd,khd->hqk", query_part, key_heads, preferred_element_type=jnp.float32)
        * score_scale
    )


def body(query_rows, key_rows, value_rows, out_weight, out_grad, source_view, source_block):
    tokens = query_rows.shape[0]
    columns = query_rows.shape[1]
    heads_here = columns // HEAD_DIM
    slot_count = source_view.shape[1]
    key_count = slot_count * BLOCK_TOKENS
    peer_count = lax.axis_size("view")
    capacity = max(1, 2 * slot_count // peer_count)
    block_count = tokens // BLOCK_TOKENS
    view_index = lax.axis_index("view")
    head_index = lax.axis_index("head")
    score_scale = HEAD_DIM ** (-0.5)
    slot_order = jnp.arange(slot_count, dtype=jnp.int32)
    same_view = source_view[:, :, None] == source_view[:, None, :]
    earlier = slot_order[None, :] < slot_order[:, None]
    slot_rank = jnp.sum((same_view & earlier[None]).astype(jnp.int32), axis=2)
    copy_order = jnp.arange(capacity, dtype=jnp.int32)
    matched = (source_view == view_index)[:, :, None] & (
        slot_rank[:, :, None] == copy_order[None, None, :]
    )
    filled = jnp.any(matched, axis=1)
    chosen = jnp.sum(jnp.where(matched, source_block[:, :, None], 0), axis=1)
    own_view = lax.dynamic_index_in_dim(source_view, view_index, 0, keepdims=False)
    own_rank = lax.dynamic_index_in_dim(slot_rank, view_index, 0, keepdims=False)
    landing = own_view * capacity + own_rank
    joined = jnp.concatenate([key_rows, value_rows], axis=1)
    outgoing = jnp.take(
        joined.reshape(block_count, BLOCK_TOKENS, 2 * columns), chosen.reshape(-1), axis=0
    )
    outgoing = outgoing.reshape(peer_count, capacity, BLOCK_TOKENS, 2 * columns)
    incoming = lax.all_to_all(outgoing, "view", split_axis=0, concat_axis=0, tiled=True)
    fetched = jnp.take(
        incoming.reshape(peer_count * capacity, BLOCK_TOKENS, 2 * columns), landing, axis=0
    )
    fetched = fetched.reshape(key_count, 2 * columns)
    query_block = min(512, tokens)
    block_total = tokens // query_block
    key_heads = fetched[:, :columns].reshape(key_count, heads_here, HEAD_DIM)
    value_heads = fetched[:, columns:].reshape(key_count, heads_here, HEAD_DIM)
    query_heads = query_rows.reshape(block_total, query_block, heads_here, HEAD_DIM)

    def forward_step(query_part):
        scores = score_rows(query_part, key_heads, score_scale)
        row_top = jnp.max(scores, axis=-1, keepdims=True)
        shifted = jnp.exp(scores - row_top)
        row_total = jnp.sum(shifted, axis=-1, keepdims=True)
        weights = (shifted / row_total).astype(jnp.bfloat16)
        out_part = jnp.einsum(
            "hqk,khd->qhd", weights, value_heads, preferred_element_type=jnp.float32
        )
        return (out_part.astype(jnp.bfloat16), row_top, row_total)

    attended, row_tops, row_totals = lax.map(forward_step, query_heads)
    attended_rows = attended.reshape(tokens, columns)
    own_rows = lax.dynamic_slice_in_dim(out_weight, head_index * columns, columns, 0)
    part_weight = own_rows
    summed_rows = lax.psum_scatter(
        lax.dot_general(
            part_weight, attended_rows, (((0,), (1,)), ((), ())), preferred_element_type=jnp.float32
        ).astype(jnp.bfloat16),
        "head",
        scatter_dimension=0,
        tiled=True,
    ).astype(jnp.float32)
    mixed_out = summed_rows.T.astype(jnp.bfloat16)
    part_weight = own_rows
    attended_grad = lax.dot_general(
        lax.all_gather(out_grad, "head", axis=1, tiled=True),
        part_weight,
        (((1,), (1,)), ((), ())),
        preferred_element_type=jnp.float32,
    )
    grad_heads = attended_grad.astype(jnp.bfloat16).reshape(
        block_total, query_block, heads_here, HEAD_DIM
    )

    def backward_step(totals, inputs):
        key_total, value_total = totals
        query_part, out_part, grad_part, row_top, row_total = inputs
        scores = score_rows(query_part, key_heads, score_scale)
        probability = jnp.exp(scores - row_top) / row_total
        weights = probability.astype(jnp.bfloat16)
        grad_prob = jnp.einsum(
            "qhd,khd->hqk", grad_part, value_heads, preferred_element_type=jnp.float32
        )
        row_delta = jnp.einsum(
            "qhd,qhd->hq", out_part, grad_part, preferred_element_type=jnp.float32
        )[:, :, None]
        grad_scores = (probability * (grad_prob - row_delta)).astype(jnp.bfloat16)
        query_part_grad = (
            jnp.einsum("hqk,khd->qhd", grad_scores, key_heads, preferred_element_type=jnp.float32)
            * score_scale
        )
        key_total = (
            key_total
            + jnp.einsum(
                "hqk,qhd->khd", grad_scores, query_part, preferred_element_type=jnp.float32
            )
            * score_scale
        )
        value_total = value_total + jnp.einsum(
            "hqk,qhd->khd", weights, grad_part, preferred_element_type=jnp.float32
        )
        return ((key_total, value_total), query_part_grad.astype(jnp.bfloat16))

    zero_keys = jnp.zeros((key_count, heads_here, HEAD_DIM), jnp.float32)
    (key_total, value_total), query_grads = lax.scan(
        backward_step,
        (zero_keys, zero_keys),
        (query_heads, attended, grad_heads, row_tops, row_totals),
    )
    query_grad = query_grads.reshape(tokens, columns)
    slot_grads = jnp.concatenate(
        [key_total.reshape(key_count, columns), value_total.reshape(key_count, columns)], axis=1
    )
    slot_grads = slot_grads.reshape(slot_count, BLOCK_TOKENS * 2 * columns)
    placing = (
        landing[None, :] == jnp.arange(peer_count * capacity, dtype=jnp.int32)[:, None]
    ).astype(jnp.float32)
    outgoing_grads = jnp.dot(placing, slot_grads, precision=lax.Precision.HIGHEST).reshape(
        peer_count, capacity, BLOCK_TOKENS, 2 * columns
    )
    returned = lax.all_to_all(
        outgoing_grads.astype(jnp.bfloat16), "view", split_axis=0, concat_axis=0, tiled=True
    ).astype(outgoing_grads.dtype)
    gathering = (
        chosen.reshape(-1)[None, :] == jnp.arange(block_count, dtype=jnp.int32)[:, None]
    ) & filled.reshape(-1)[None, :]
    summed = jnp.dot(
        gathering.astype(jnp.float32),
        returned.reshape(peer_count * capacity, BLOCK_TOKENS * 2 * columns),
        precision=lax.Precision.HIGHEST,
    )
    summed = summed.reshape(tokens, 2 * columns)
    key_grad = summed[:, :columns].astype(jnp.bfloat16)
    value_grad = summed[:, columns:].astype(jnp.bfloat16)
    return (mixed_out, query_grad, key_grad, value_grad)


def solution(mesh):
    placed = (
        P("view", "head"),
        P("view", "head"),
        P("view", "head"),
        P(),
        P("view", "head"),
        P(),
        P(),
    )
    return jax.shard_map(
        body,
        mesh=mesh,
        in_specs=placed,
        out_specs=(P("view", "head"), P("view", "head"), P("view", "head"), P("view", "head")),
        check_vma=False,
    )
```

profile of v0, /device:TPU:0, one launch (start us, length us, event | category | flops | bytes accessed | tf_op | source)
XLA Modules:
  0.0 368.4 jit_solution(16471732138422702483)
XLA Ops:
  14.7 4.6 %broadcast_select_fusion = bf16[8,4,128,512]{3,2,1,0:T(8,128)(2,1)} fusion(bf16[8,4,128,512]{3,2,1,0:T(8,128)(2,1)} %bitcast.152, pred[8,4]{1,0:T(8,128)(4,1)S(1)} %copy.46), kind=kLoop, calls=%fused_computation.52 | loop fusion | flops 2097152 | bytes 8388640 | tf_op jit(solution)/shard_map/jit(_take)/select_n | solution.py:43
  19.3 7.3 %all-to-all-start = ((bf16[8,4,128,512]{3,2,1,0:T(8,128)(2,1)}), bf16[8,4,128,512]{3,2,1,0:T(8,128)(2,1)}, u32[]{:S(2)}, u32[]{:S(2)}) async-start(bf16[8,4,128,512]{3,2,1,0:T(8,128)(2,1)} %broadcast_select_fusion), calls=%async_computation | async-start | bytes 8388608 | tf_op jit(solution)/shard_map/all_to_all | solution.py:47
  32.1 21.1 %all-gather.2.cloned.1.call-done = bf16[1024,1024]{1,0:T(8,128)(2,1)} async-done(((bf16[1024,256]{1,0:T(8,128)(2,1)}), bf16[1024,1024]{1,0:T(8,128)(2,1)}) %all-gather.2.cloned.1.call-update) | async-done | bytes 2097168 | tf_op jit(solution)/shard_map/all_gather | solution.py:84
  56.8 63.1 %all-to-all-done = bf16[8,4,128,512]{3,2,1,0:T(8,128)(2,1)} async-done(((bf16[8,4,128,512]{3,2,1,0:T(8,128)(2,1)}), bf16[8,4,128,512]{3,2,1,0:T(8,128)(2,1)}, u32[]{:S(2)}, u32[]{:S(2)}) %all-to-all-start) | async-done | bytes 4194336 | tf_op jit(solution)/shard_map/all_to_all | solution.py:47
  119.9 4.2 %gather_fusion.1 = bf16[16,128,512]{2,1,0:T(8,128)(2,1)} fusion(bf16[32,128,512]{2,1,0:T(8,128)(2,1)} %bitcast.12, s32[1024]{0:T(1024)S(1)} %pad_clamp_fusion), kind=kCustom, calls=%fused_computation.1 | custom fusion | bytes 4194368 | tf_op jit(solution)/shard_map/jit(_take)/gather | solution.py:48
  131.5 25.6 %while.29 = (s32[]{:T(128)}, bf16[2,512,4,64]{1,3,2,0:T(8,128)(2,1)}, f32[2,4,512,1]{2,1,3,0:T(4,128)S(1)}, f32[2,4,512,1]{2,1,3,0:T(4,128)S(1)}, bf16[2,512,4,6...) while((s32[]{:T(128)}, ...), condition=%wide.region_5.6_spmd, body=%wide.region_2.5_spmd.sunk | while | flops 1111617536 | bytes 53026920 | solution.py:69
  131.5 3.8 %multiply_reduce_fusion.4 = (f32[4,512]{1,0:T(4,128)S(1)}, f32[4,512,2048]{2,1,0:T(8,128)S(1)}) fusion(bf16[2048,4,64]{0,2,1:T(8,128)(2,1)} %get-tuple-element.416, bf16[2,512,4,64]{1,3,2,0:T(8,128)(2,1)} %get-tuple-element.415, s32[]{:T(128)S(6)} %copy.97), kind=kOutput, calls=%fused_computation.4.clone.1 | convolution fusion | flops 545257472 | bytes 18096132 | tf_op jit(solution)/shard_map/while/body/eval_jaxpr/qhd,khd->hqk/dot_general | solution.py:12
  135.3 3.3 fusion.89
  138.5 5.8 %fusion.90 = bf16[2,512,4,64]{1,3,2,0:T(8,128)(2,1)} fusion(bf16[2,512,4,64]{1,3,2,0:T(8,128)(2,1)} %get-tuple-element.404, s32[]{:T(128)S(6)} %copy.97, bf16[2048,4,64]{0,2,1:T(8,128)(2,1)} %get-tuple-element.417, f32[4,512,2048]{2,1,0:T(8,128)S(1)} %get-tuple-element.378, f32[4,512]{1,0:T(4,128)S(1)} %fusion.89, f32[4,512]{1,0:T(4,128)S(1)} %get-tuple-element.379), kind=kOutput, calls=%fused_computation.9.clone.1 | convolution fusion | flops 553779200 | bytes 18104324 | tf_op jit(solution)/shard_map/while/body/eval_jaxpr/hqk,khd->qhd/dot_general | solution.py:64
  144.3 3.8 %multiply_reduce_fusion.4 = (f32[4,512]{1,0:T(4,128)S(1)}, f32[4,512,2048]{2,1,0:T(8,128)S(1)}) fusion(bf16[2048,4,64]{0,2,1:T(8,128)(2,1)} %get-tuple-element.416, bf16[2,512,4,64]{1,3,2,0:T(8,128)(2,1)} %get-tuple-element.415, s32[]{:T(128)S(6)} %copy.97), kind=kOutput, calls=%fused_computation.4.clone.1 | convolution fusion | flops 545257472 | bytes 18096132 | tf_op jit(solution)/shard_map/while/body/eval_jaxpr/qhd,khd->hqk/dot_general | solution.py:12
  148.1 3.3 fusion.89
  151.3 5.8 %fusion.90 = bf16[2,512,4,64]{1,3,2,0:T(8,128)(2,1)} fusion(bf16[2,512,4,64]{1,3,2,0:T(8,128)(2,1)} %get-tuple-element.404, s32[]{:T(128)S(6)} %copy.97, bf16[2048,4,64]{0,2,1:T(8,128)(2,1)} %get-tuple-element.417, f32[4,512,2048]{2,1,0:T(8,128)S(1)} %get-tuple-element.378, f32[4,512]{1,0:T(4,128)S(1)} %fusion.89, f32[4,512]{1,0:T(4,128)S(1)} %get-tuple-element.379), kind=kOutput, calls=%fused_computation.9.clone.1 | convolution fusion | flops 553779200 | bytes 18104324 | tf_op jit(solution)/shard_map/while/body/eval_jaxpr/hqk,khd->qhd/dot_general | solution.py:64
  157.9 73.0 %while.30 = (s32[]{:T(128)}, f32[2048,4,64]{0,2,1:T(8,128)}, f32[2048,4,64]{0,2,1:T(8,128)}, bf16[2,512,4,64]{1,3,2,0:T(8,128)(2,1)}, bf16[2,512,4,64]{1,3,2,0:T...) while((s32[]{:T(128)}, f32[2048,4,64]{0,2,1:T(8,128)}, ...), condition=%wide.region_8.9_spmd.clone, body=%wide.region_7.8_spmd.clone.sunk | while | flops 2717120512 | bytes 178061584 | solution.py:123
  163.5 5.1 %exponential_divide_fusion.2 = f32[4,512,2048]{2,1,0:T(8,128)S(1)} fusion(f32[4,512]{1,0:T(4,128)S(1)} %get-tuple-element.393, f32[4,512]{1,0:T(4,128)S(1)} %get-tuple-element.394, bf16[2048,4,64]{0,2,1:T(8,128)(2,1)} %get-tuple-element.450, bf16[2,512,4,64]{1,3,2,0:T(8,128)(2,1)} %get-tuple-element.449, s32[]{:T(128)S(6)} %copy.109), kind=kOutput, calls=%fused_computation.18.clone.1 | convolution fusion | flops 549453824 | bytes 18104324 | tf_op jit(solution)/shard_map/while/body/eval_jaxpr/qhd,khd->hqk/dot_general | solution.py:12
  168.6 5.7 %copy-done.1 = f32[4,512,2048]{2,1,0:T(8,128)} copy-done((f32[4,512,2048]{2,1,0:T(8,128)}, f32[4,512,2048]{2,1,0:T(8,128)S(1)}, u32[]{:S(2)}) %copy-start.1) | copy-done | bytes 16777240 | tf_op jit(solution)/shard_map/while
  174.3 3.0 fusion.102
  177.3 7.4 %multiply_convert_fusion.2 = bf16[4,512,2048]{2,1,0:T(8,128)(2,1)S(1)} fusion(f32[4,512,2048]{2,1,0:T(8,128)} %copy-done.1, f32[4,512]{1,0:T(4,128)S(1)} %multiply_reduce_fusion.5, bf16[2048,4,64]{0,2,1:T(8,128)(2,1)} %get-tuple-element.454, bf16[2,512,4,64]{1,3,2,0:T(8,128)(2,1)S(1)} %copy-done.4, s32[]{:T(128)S(6)} %copy.109), kind=kOutput, calls=%fused_computation.17.clone.1 | convolution fusion | flops 549453824 | bytes 26484740 | tf_op jit(solution)/shard_map/while/body/eval_jaxpr/qhd,khd->hqk/dot_general | solution.py:99
  184.7 4.8 %fusion.103 = bf16[2,512,4,64]{1,3,2,0:T(8,128)(2,1)} fusion(bf16[2,512,4,64]{1,3,2,0:T(8,128)(2,1)} %get-tuple-element.435, s32[]{:T(128)S(6)} %copy.109, bf16[4,512,2048]{2,1,0:T(8,128)(2,1)S(1)} %multiply_convert_fusion.2, bf16[2048,4,64]{0,2,1:T(8,128)(2,1)} %get-tuple-element.450), kind=kOutput, calls=%fused_computation.29.clone.1 | convolution fusion | flops 537133056 | bytes 9699332 | tf_op jit(solution)/shard_map/while/body/eval_jaxpr/hqk,khd->qhd/dot_general | solution.py:107
  199.2 5.1 %exponential_divide_fusion.2 = f32[4,512,2048]{2,1,0:T(8,128)S(1)} fusion(f32[4,512]{1,0:T(4,128)S(1)} %get-tuple-element.393, f32[4,512]{1,0:T(4,128)S(1)} %get-tuple-element.394, bf16[2048,4,64]{0,2,1:T(8,128)(2,1)} %get-tuple-element.450, bf16[2,512,4,64]{1,3,2,0:T(8,128)(2,1)} %get-tuple-element.449, s32[]{:T(128)S(6)} %copy.109), kind=kOutput, calls=%fused_computation.18.clone.1 | convolution fusion | flops 549453824 | bytes 18104324 | tf_op jit(solution)/shard_map/while/body/eval_jaxpr/qhd,khd->hqk/dot_general | solution.py:12
  204.3 5.7 %copy-done.1 = f32[4,512,2048]{2,1,0:T(8,128)} copy-done((f32[4,512,2048]{2,1,0:T(8,128)}, f32[4,512,2048]{2,1,0:T(8,128)S(1)}, u32[]{:S(2)}) %copy-start.1) | copy-done | bytes 16777240 | tf_op jit(solution)/shard_map/while
  210.0 4.6 %fusion.102 = f32[2048,4,64]{0,2,1:T(8,128)} fusion(f32[4,512,2048]{2,1,0:T(8,128)S(1)} %exponential_divide_fusion.2, f32[2048,4,64]{0,2,1:T(8,128)} %get-tuple-element.434, pred[]{:T(512)S(6)} %compare.3, bf16[2,512,4,64]{1,3,2,0:T(8,128)(2,1)S(1)} %copy-done.4, s32[]{:T(128)S(6)} %copy.109), kind=kOutput, calls=%fused_computation.25.clone.1 | convolution fusion | flops 542113792 | bytes 21233668 | tf_op jit(solution)/shard_map/while/body/eval_jaxpr/hqk,qhd->khd/dot_general | solution.py:117
  214.5 7.4 %multiply_convert_fusion.2 = bf16[4,512,2048]{2,1,0:T(8,128)(2,1)S(1)} fusion(f32[4,512,2048]{2,1,0:T(8,128)} %copy-done.1, f32[4,512]{1,0:T(4,128)S(1)} %multiply_reduce_fusion.5, bf16[2048,4,64]{0,2,1:T(8,128)(2,1)} %get-tuple-element.454, bf16[2,512,4,64]{1,3,2,0:T(8,128)(2,1)S(1)} %copy-done.4, s32[]{:T(128)S(6)} %copy.109), kind=kOutput, calls=%fused_computation.17.clone.1 | convolution fusion | flops 549453824 | bytes 26484740 | tf_op jit(solution)/shard_map/while/body/eval_jaxpr/qhd,khd->hqk/dot_general | solution.py:99
  222.0 4.8 %fusion.103 = bf16[2,512,4,64]{1,3,2,0:T(8,128)(2,1)} fusion(bf16[2,512,4,64]{1,3,2,0:T(8,128)(2,1)} %get-tuple-element.435, s32[]{:T(128)S(6)} %copy.109, bf16[4,512,2048]{2,1,0:T(8,128)(2,1)S(1)} %multiply_convert_fusion.2, bf16[2048,4,64]{0,2,1:T(8,128)(2,1)} %get-tuple-element.450), kind=kOutput, calls=%fused_computation.29.clone.1 | convolution fusion | flops 537133056 | bytes 9699332 | tf_op jit(solution)/shard_map/while/body/eval_jaxpr/hqk,khd->qhd/dot_general | solution.py:107
  233.8 2.9 copy.59
  236.7 4.7 %pad_maximum_fusion = f32[2048,512]{1,0:T(8,128)} fusion(f32[2048,256]{1,0:T(8,128)} %copy.59, f32[2048,256]{1,0:T(8,128)} %copy.58), kind=kLoop, calls=%fused_computation.51 | loop fusion | flops 1048576 | bytes 8388608 | tf_op jit(solution)/shard_map/concatenate | solution.py:129
  241.5 3.9 %reshape.193 = f32[16,65536]{1,0:T(8,128)} reshape(f32[2048,512]{1,0:T(8,128)} %pad_maximum_fusion) | data formatting | bytes 8388608 | tf_op jit(solution)/shard_map/reshape | solution.py:132
  245.4 6.6 %fusion.37 = bf16[8,4,128,512]{3,0,2,1:T(8,128)(2,1)S(1)} fusion(f32[2,128,8,512]{3,2,1,0:T(8,128)} %bitcast.151, s32[8,4]{0,1:T(4,128)S(1)} %copy-done.11, s32[16]{0:T(128)S(1)} %bitcast.157), kind=kOutput, calls=%fused_computation.53 | convolution fusion | flops 404750848 | bytes 8388800 | tf_op jit(solution)/shard_map/dot_general | solution.py:136
  252.1 3.4 copy.61
  255.5 4.5 %all-to-all-start.1 = ((bf16[8,4,128,512]{3,2,1,0:T(8,128)(2,1)}), bf16[8,4,128,512]{3,2,1,0:T(8,128)(2,1)}, u32[]{:S(2)}, u32[]{:S(2)}) async-start(bf16[8,4,128,512]{3,2,1,0:T(8,128)(2,1)} %copy.61), calls=%async_computation.2 | async-start | bytes 8388608 | tf_op jit(solution)/shard_map/all_to_all | solution.py:139
  267.5 29.2 %reduce-scatter.2.cloned.1.call-done = bf16[256,1024]{1,0:T(8,128)(2,1)} async-done(((bf16[1024,1024]{1,0:T(8,128)(2,1)}), bf16[256,1024]{1,0:T(8,128)(2,1)}) %reduce-scatter.2.cloned.1.call-update) | async-done | bytes 524304 | tf_op jit(solution)/shard_map/reduce_scatter | solution.py:73
  298.7 53.9 %all-to-all-done.1 = bf16[8,4,128,512]{3,2,1,0:T(8,128)(2,1)} async-done(((bf16[8,4,128,512]{3,2,1,0:T(8,128)(2,1)}), bf16[8,4,128,512]{3,2,1,0:T(8,128)(2,1)}, u32[]{:S(2)}, u32[]{:S(2)}) %all-to-all-start.1) | async-done | bytes 4194336 | tf_op jit(solution)/shard_map/all_to_all | solution.py:139
  352.6 4.6 %copy.78 = bf16[4,8,128,512]{3,1,2,0:T(8,128)(2,1)S(1)} copy(bf16[4,8,128,512]{3,2,1,0:T(8,128)(2,1)} %bitcast.49) | data formatting | bytes 8388608
  (100 shorter events, 60.7 us)
Async XLA Ops:
  7.2 46.0 %copy-start = (bf16[1024,1024]{1,0:T(8,128)(2,1)S(1)}, bf16[1024,1024]{1,0:T(8,128)(2,1)}, u32[]{:S(2)}) copy-start(bf16[1024,1024]{1,0:T(8,128)(2,1)} %param.14) | copy-start | bytes 6291460
  8.0 2.2 copy-start.9
  9.1 21.7 %copy-start.5 = (s32[8,16]{1,0:T(8,128)}, s32[8,16]{1,0:T(8,128)S(1)}, u32[]{:S(2)}) copy-start(s32[8,16]{1,0:T(8,128)S(1)} %convert_reduce_fusion) | copy-start | bytes 1540
  10.0 0.6 copy-start.7
  19.3 100.6 %all-to-all-start = ((bf16[8,4,128,512]{3,2,1,0:T(8,128)(2,1)}), bf16[8,4,128,512]{3,2,1,0:T(8,128)(2,1)}, u32[]{:S(2)}, u32[]{:S(2)}) async-start(bf16[8,4,128,512]{3,2,1,0:T(8,128)(2,1)} %broadcast_select_fusion), calls=%async_computation | async-start | bytes 8388608 | tf_op jit(solution)/shard_map/all_to_all | solution.py:47
  26.6 26.6 %all-gather.2.cloned.1.call-start = ((), (), s32[]{:S(2)}) async-start(), calls=%async_computation.4 | async-start | bytes 2621440 | tf_op jit(solution)/shard_map/all_gather | solution.py:84
  31.5 0.6 copy-start.12
  163.5 10.8 %copy-start.4 = (bf16[2,512,4,64]{1,3,2,0:T(8,128)(2,1)S(1)}, bf16[2,512,4,64]{1,3,2,0:T(8,128)(2,1)}, u32[]{:S(2)}) copy-start(bf16[2,512,4,64]{1,3,2,0:T(8,128)(2,1)} %get-tuple-element.453) | copy-start | bytes 1572868 | tf_op jit(solution)/shard_map/while
  168.6 5.7 %copy-start.1 = (f32[4,512,2048]{2,1,0:T(8,128)}, f32[4,512,2048]{2,1,0:T(8,128)S(1)}, u32[]{:S(2)}) copy-start(f32[4,512,2048]{2,1,0:T(8,128)S(1)} %exponential_divide_fusion.2) | copy-start | bytes 50331652 | tf_op jit(solution)/shard_map/while
  184.7 4.8 %copy-start.2 = (f32[2048,4,64]{0,2,1:T(8,128)S(1)}, f32[2048,4,64]{0,2,1:T(8,128)}, u32[]{:S(2)}) copy-start(f32[2048,4,64]{0,2,1:T(8,128)} %get-tuple-element.433) | copy-start | bytes 6291460 | tf_op jit(solution)/shard_map/while
  192.3 1.3 copy-start.3
  199.2 10.8 %copy-start.4 = (bf16[2,512,4,64]{1,3,2,0:T(8,128)(2,1)S(1)}, bf16[2,512,4,64]{1,3,2,0:T(8,128)(2,1)}, u32[]{:S(2)}) copy-start(bf16[2,512,4,64]{1,3,2,0:T(8,128)(2,1)} %get-tuple-element.453) | copy-start | bytes 1572868 | tf_op jit(solution)/shard_map/while
  204.2 5.7 %copy-start.1 = (f32[4,512,2048]{2,1,0:T(8,128)}, f32[4,512,2048]{2,1,0:T(8,128)S(1)}, u32[]{:S(2)}) copy-start(f32[4,512,2048]{2,1,0:T(8,128)S(1)} %exponential_divide_fusion.2) | copy-start | bytes 50331652 | tf_op jit(solution)/shard_map/while
  222.0 4.8 %copy-start.2 = (f32[2048,4,64]{0,2,1:T(8,128)S(1)}, f32[2048,4,64]{0,2,1:T(8,128)}, u32[]{:S(2)}) copy-start(f32[2048,4,64]{0,2,1:T(8,128)} %get-tuple-element.433) | copy-start | bytes 6291460 | tf_op jit(solution)/shard_map/while
  229.6 1.3 copy-start.3
  241.5 4.0 %copy-start.11 = (s32[8,4]{0,1:T(4,128)S(1)}, s32[8,4]{0,1:T(4,128)}, u32[]{:S(2)}) copy-start(s32[8,4]{0,1:T(4,128)} %multiply_add_fusion) | copy-start | bytes 388
  241.5 4.0 %copy-start.13 = (s32[1,16]{1,0:T(1,128)S(1)}, s32[1,16]{1,0:T(1,128)}, u32[]{:S(2)}) copy-start(s32[1,16]{1,0:T(1,128)} %copy-done.12) | copy-start | bytes 196
  255.5 97.1 %all-to-all-start.1 = ((bf16[8,4,128,512]{3,2,1,0:T(8,128)(2,1)}), bf16[8,4,128,512]{3,2,1,0:T(8,128)(2,1)}, u32[]{:S(2)}, u32[]{:S(2)}) async-start(bf16[8,4,128,512]{3,2,1,0:T(8,128)(2,1)} %copy.61), calls=%async_computation.2 | async-start | bytes 8388608 | tf_op jit(solution)/shard_map/all_to_all | solution.py:139
  260.1 3.9 %copy-start.8 = (s32[8,4]{1,0:T(8,128)S(1)}, s32[8,4]{1,0:T(8,128)}, u32[]{:S(2)}) copy-start(s32[8,4]{1,0:T(8,128)} %copy-done.7) | copy-start | bytes 388
  260.1 4.0 %copy-start.6 = (s32[8,16]{1,0:T(8,128)S(1)}, s32[8,16]{1,0:T(8,128)}, u32[]{:S(2)}) copy-start(s32[8,16]{1,0:T(8,128)} %copy-done.5) | copy-start | bytes 1540
  260.1 4.0 %copy-start.10 = (pred[8,16]{1,0:T(8,128)(4,1)S(1)}, pred[8,16]{1,0:T(8,128)(4,1)}, u32[]{:S(2)}) copy-start(pred[8,16]{1,0:T(8,128)(4,1)} %copy-done.9) | copy-start | bytes 388
  260.1 36.6 %reduce-scatter.2.cloned.1.call-start = ((), (), s32[]{:S(2)}) async-start(), calls=%async_computation.3 | async-start | bytes 2621440 | tf_op jit(solution)/shard_map/reduce_scatter | solution.py:73
Sparse Core Ops, SparseCore 0:
  29.0 24.1 all-gather.1
  264.1 32.5 reduce-scatter.1
where the time goes:
time: 370 us; the launch traced here: 368 us
  waiting for transfers between devices  168 us (45%)
  matrix products  79.5 us (21%)
  local copies, waits for them, and re-layouts  66.8 us (18%)
  other arithmetic  27.8 us (8%)
  between operations  14.3 us (4%)
  starting transfers between devices  11.9 us (3%)
    all_to_all x1, waiting for transfers between devices, body(): lax.all_to_all(outgoing, 'view', split_axis=0, concat_axis=0, tiled=True)  63.1 us
    all_to_all x1, waiting for transfers between devices, body(): lax.all_to_all(outgoing_grads.astype(jnp.bfloat16), 'view', split_axis=0,...  53.9 us
    reduce_scatter x1, waiting for transfers between devices, body(): lax.psum_scatter(lax.dot_general(part_weight, attended_rows, (((0,), (1,)...  29.2 us
    all_gather x1, waiting for transfers between devices, body(): lax.all_gather(out_grad, 'head', axis=1, tiled=True)  21.1 us
    dot_general x4, matrix products, score_rows(): jnp.einsum('qhd,khd->hqk', query_part, key_heads, preferred_element_type=...  17.7 us
    while x18, local copies, waits for them, and re-layouts  16.4 us
    dot_general x2, matrix products, backward_step(): jnp.einsum('qhd,khd->hqk', grad_part, value_heads, preferred_element_type...  14.8 us
    dot_general x2, matrix products, forward_step(): jnp.einsum('hqk,khd->qhd', weights, value_heads, preferred_element_type=j...  11.5 us
  transfers between devices with their start and end apart: 4, of which 4 were waited for; matrix products, arithmetic and copies ran while one was open for 5% of the time, Pallas kernels for 0%

commit v1 on v0

--- a/solution.py
+++ b/solution.py
@@ -1,10 +1,417 @@
+import functools
+
 import jax
 import jax.numpy as jnp
 from jax import lax
+from jax.experimental import pallas as pl
+from jax.experimental.pallas import tpu as pltpu
 from jax.sharding import PartitionSpec as P
 
 HEAD_DIM = 64
 BLOCK_TOKENS = 128
+LOG2E = 1.4426950408889634
+F32 = jnp.float32
+BF16 = jnp.bfloat16
+
+
+def join(a, b):
+    return jnp.concatenate([a[:, :HEAD_DIM], b[:, :HEAD_DIM]], axis=1)
+
+
+def join_high(a, b):
+    return jnp.concatenate([a[:, HEAD_DIM:], b[:, HEAD_DIM:]], axis=1)
+
+
+def dot(a, b):
+    return jnp.dot(a, b, preferred_element_type=F32)
+
+
+def pack_kernel(q_ref, k_ref, v_ref, kv_ref, qp_ref):
+    rows = q_ref.shape[0]
+    for pair in range(q_ref.shape[1] // 128):
+        lanes = slice(128 * pair, 128 * (pair + 1))
+        k, v = k_ref[:, lanes], v_ref[:, lanes]
+        kv_ref[0, 2 * pair] = join(k, v)
+        kv_ref[0, 2 * pair + 1] = join_high(k, v)
+        top, low = q_ref[: rows // 2, lanes], q_ref[rows // 2 :, lanes]
+        qp_ref[0, 2 * pair] = join(top, low)
+        qp_ref[0, 2 * pair + 1] = join_high(top, low)
+
+
+def pack(q, k, v):
+    tokens, columns = q.shape
+    half = tokens // 2
+    heads = columns // HEAD_DIM
+    rows = pl.BlockSpec((half, columns), lambda i: (i, 0))
+    return pl.pallas_call(
+        pack_kernel,
+        grid=(2,),
+        in_specs=[rows] * 3,
+        out_specs=[
+            pl.BlockSpec((1, heads, half, 128), lambda i: (i, 0, 0, 0)),
+            pl.BlockSpec((1, heads, half // 2, 128), lambda i: (i, 0, 0, 0)),
+        ],
+        out_shape=[
+            jax.ShapeDtypeStruct((2, heads, half, 128), BF16),
+            jax.ShapeDtypeStruct((2, heads, half // 2, 128), BF16),
+        ],
+        name="pack",
+    )(q, k, v)
+
+
+def unpack_kernel(kv_ref, qp_ref, q_ref, k_ref, v_ref):
+    rows = q_ref.shape[0]
+    for pair in range(q_ref.shape[1] // 128):
+        lanes = slice(128 * pair, 128 * (pair + 1))
+        a, b = kv_ref[0, 2 * pair], kv_ref[0, 2 * pair + 1]
+        k_ref[:, lanes] = join(a, b)
+        v_ref[:, lanes] = join_high(a, b)
+        a, b = qp_ref[0, 2 * pair], qp_ref[0, 2 * pair + 1]
+        q_ref[: rows // 2, lanes] = join(a, b)
+        q_ref[rows // 2 :, lanes] = join_high(a, b)
+
+
+def unpack(kv, qp):
+    _, heads, half, _ = kv.shape
+    columns = heads * HEAD_DIM
+    rows = pl.BlockSpec((half, columns), lambda i: (i, 0))
+    return pl.pallas_call(
+        unpack_kernel,
+        grid=(2,),
+        in_specs=[
+            pl.BlockSpec((1, heads, half, 128), lambda i: (i, 0, 0, 0)),
+            pl.BlockSpec((1, heads, half // 2, 128), lambda i: (i, 0, 0, 0)),
+        ],
+        out_specs=[rows] * 3,
+        out_shape=[jax.ShapeDtypeStruct((2 * half, columns), BF16)] * 3,
+        name="unpack",
+    )(kv, qp)
+
+
+def grad_kernel(x_ref, og_ref, w_ref, out_ref):
+    parts, rows, columns = og_ref.shape
+    total = None
+    for part in range(parts):
+        piece = lax.dot_general(
+            og_ref[part],
+            w_ref[:, columns * part : columns * (part + 1)],
+            (((1,), (1,)), ((), ())),
+            preferred_element_type=F32,
+        )
+        total = piece if total is None else total + piece
+    total = total.astype(BF16)
+    for pair in range(total.shape[1] // 128):
+        lanes = slice(128 * pair, 128 * (pair + 1))
+        top, low = total[: rows // 2, lanes], total[rows // 2 :, lanes]
+        out_ref[2 * pair] = join(top, low)
+        out_ref[2 * pair + 1] = join_high(top, low)
+
+
+def attended_grads(plane, og, weight, plane_columns):
+    parts, rows, columns = og.shape
+    depth = parts * columns
+    return pl.pallas_call(
+        grad_kernel,
+        grid_spec=pltpu.PrefetchScalarGridSpec(
+            num_scalar_prefetch=1,
+            grid=(1,),
+            in_specs=[
+                pl.BlockSpec((parts, rows, columns), lambda i, x: (0, 0, 0)),
+                pl.BlockSpec((plane_columns, depth), lambda i, x: (x[0], 0)),
+            ],
+            out_specs=pl.BlockSpec(
+                (plane_columns // HEAD_DIM, rows // 2, 128), lambda i, x: (0, 0, 0)
+            ),
+        ),
+        out_shape=jax.ShapeDtypeStruct((plane_columns // HEAD_DIM, rows // 2, 128), BF16),
+        name="attended_grads",
+    )(plane, og, weight)
+
+
+def mix_kernel(x_ref, own_ref, other_ref, w_ref, out_ref):
+    heads, rows, _ = own_ref.shape
+    depth = heads * HEAD_DIM
+    x = x_ref[0]
+
+    def rows_of(ref):
+        top, low = [], []
+        for pair in range(heads // 2):
+            a, b = ref[2 * pair], ref[2 * pair + 1]
+            top.append(join(a, b))
+            low.append(join_high(a, b))
+        return jnp.concatenate(
+            [jnp.concatenate(top, axis=1), jnp.concatenate(low, axis=1)], axis=0
+        )
+
+    own = dot(rows_of(own_ref), w_ref[pl.ds(pl.multiple_of(x * depth, depth), depth), :])
+    other = dot(
+        rows_of(other_ref), w_ref[pl.ds(pl.multiple_of((1 - x) * depth, depth), depth), :]
+    )
+    mixed = (own + other).astype(BF16)
+    width = mixed.shape[1] // 2
+    out_ref[0] = mixed[:, :width]
+    out_ref[1] = mixed[:, width:]
+
+
+def mix(plane, own, other, weight):
+    heads, rows, _ = own.shape
+    width = heads * HEAD_DIM
+    whole = pl.BlockSpec((heads, rows, 128), lambda i, x: (0, 0, 0))
+    return pl.pallas_call(
+        mix_kernel,
+        grid_spec=pltpu.PrefetchScalarGridSpec(
+            num_scalar_prefetch=1,
+            grid=(1,),
+            in_specs=[
+                whole,
+                whole,
+                pl.BlockSpec((weight.shape[0], width), lambda i, x: (0, x[0])),
+            ],
+            out_specs=pl.BlockSpec((2, 2 * rows, width // 2), lambda i, x: (0, 0, 0)),
+        ),
+        out_shape=jax.ShapeDtypeStruct((2, 2 * rows, width // 2), BF16),
+        name="mix",
+    )(plane, own, other, weight)
+
+
+def bring_sources(c_ref, own_ref, other_ref, kv_scr, sem):
+    c = c_ref[0]
+    first = pltpu.make_async_copy(own_ref, kv_scr.at[c], sem.at[0])
+    second = pltpu.make_async_copy(other_ref, kv_scr.at[1 - c], sem.at[1])
+    first.start()
+    second.start()
+    first.wait()
+    second.wait()
+
+
+def place(sv_ref, sb_ref, view, slot, per_half):
+    block = sb_ref[view, slot]
+    start = pl.multiple_of(lax.rem(block, per_half) * BLOCK_TOKENS, BLOCK_TOKENS)
+    return lax.div(block, per_half), sv_ref[view, slot], pl.ds(start, BLOCK_TOKENS)
+
+
+def gather_slots(sv_ref, sb_ref, view, kv_scr, kvg, kvt):
+    per_half = kv_scr.shape[2] // BLOCK_TOKENS
+    for slot in range(sv_ref.shape[1]):
+        half, source, rows = place(sv_ref, sb_ref, view, slot, per_half)
+        block = kv_scr[half, source, rows, :]
+        kvg[slot * BLOCK_TOKENS : (slot + 1) * BLOCK_TOKENS, :] = block
+        kvt[:, slot * BLOCK_TOKENS : (slot + 1) * BLOCK_TOKENS] = block.T
+
+
+def turned(block):
+    t = block.T
+    return jnp.concatenate([t[:HEAD_DIM], t[HEAD_DIM:]], axis=1)
+
+
+def turned_back(t):
+    width = t.shape[1] // 2
+    return jnp.concatenate([t[:, :width], t[:, width:]], axis=0).T
+
+
+def forward_kernel(
+    sv_ref, sb_ref, c_ref, own_ref, other_ref, q_ref, e_ref, o_ref, l_ref, kv_scr, kvg, kvt, s_scr, sem
+):
+    view = pl.program_id(0)
+
+    @pl.when(view == 0)
+    def _():
+        bring_sources(c_ref, own_ref, other_ref, kv_scr, sem)
+
+    gather_slots(sv_ref, sb_ref, view, kv_scr, kvg, kvt)
+    keys, queries = s_scr.shape
+    step = 256
+    q = turned(q_ref[0]) * jnp.asarray(HEAD_DIM**-0.5, BF16)
+    q = jnp.concatenate([q, jnp.zeros_like(q)], axis=0)
+    top = None
+    for i in range(keys // step):
+        s = dot(kvg[i * step : (i + 1) * step, :], q)
+        s_scr[i * step : (i + 1) * step, :] = s
+        t = jnp.max(s.reshape(step // 8, 8, queries), axis=0)
+        top = t if top is None else jnp.maximum(top, t)
+    top = jnp.max(top, axis=0, keepdims=True)
+    total = None
+    for i in range(keys // step):
+        e = jnp.exp2((s_scr[i * step : (i + 1) * step, :] - top) * LOG2E)
+        t = jnp.sum(e.reshape(step // 8, 8, queries), axis=0)
+        total = t if total is None else total + t
+        e_ref[0, i * step : (i + 1) * step, :] = e.astype(BF16)
+    total = jnp.sum(total, axis=0, keepdims=True)
+    l_ref[0] = total
+    out = dot(kvt[...], e_ref[0])[HEAD_DIM:] / total
+    o_ref[0] = turned_back(out).astype(BF16)
+
+
+def backward_kernel(
+    sv_ref, sb_ref, c_ref, own_ref, other_ref, q_ref, e_ref, o_ref, l_ref, g_ref,
+    dq_ref, near_ref, far_ref, kv_scr, kvg, kvt, ds_scr, acc, sem,
+):
+    view = pl.program_id(0)
+
+    @pl.when(view == 0)
+    def _():
+        bring_sources(c_ref, own_ref, other_ref, kv_scr, sem)
+        acc[...] = jnp.zeros_like(acc)
+
+    gather_slots(sv_ref, sb_ref, view, kv_scr, kvg, kvt)
+    keys, queries = ds_scr.shape
+    per_half = kv_scr.shape[2] // BLOCK_TOKENS
+    step = 256
+    q = turned(q_ref[0]) * jnp.asarray(HEAD_DIM**-0.5, BF16)
+    q_rows = jnp.concatenate([q, jnp.zeros_like(q)], axis=0).T
+    g = (turned(g_ref[0]).astype(F32) / l_ref[0]).astype(BF16)
+    delta = jnp.sum(turned(o_ref[0]).astype(F32) * g.astype(F32), axis=0, keepdims=True)
+    g = jnp.concatenate([jnp.zeros_like(g), g], axis=0)
+    g_rows = g.T
+    for i in range(keys // step):
+        rows = slice(i * step, (i + 1) * step)
+        e = e_ref[0, rows, :]
+        dp = dot(kvg[rows, :], g)
+        ds = (e.astype(F32) * (dp - delta)).astype(BF16)
+        ds_scr[rows, :] = ds
+        dkv = dot(ds, q_rows) + dot(e, g_rows)
+        for part in range(step // BLOCK_TOKENS):
+            slot = i * (step // BLOCK_TOKENS) + part
+            half, source, where = place(sv_ref, sb_ref, view, slot, per_half)
+            acc[half, source, where, :] += dkv[part * BLOCK_TOKENS : (part + 1) * BLOCK_TOKENS]
+    dq = dot(kvt[...], ds_scr[...])[:HEAD_DIM] * (HEAD_DIM**-0.5)
+    dq_ref[0] = turned_back(dq).astype(BF16)
+
+    @pl.when(view == pl.num_programs(0) - 1)
+    def _():
+        c = c_ref[0]
+        near_ref[...] = acc[c]
+        far_ref[...] = acc[1 - c].astype(BF16)
+
+
+def attention_specs(views, half):
+    hbm = pl.BlockSpec(memory_space=pl.ANY)
+    packed = pl.BlockSpec((1, half // 2, 128), lambda i, *_: (i, 0, 0))
+    return hbm, packed
+
+
+def forward(routes, own, other, q, keys):
+    views, half, _ = own.shape
+    hbm, packed = attention_specs(views, half)
+    return pl.pallas_call(
+        forward_kernel,
+        grid_spec=pltpu.PrefetchScalarGridSpec(
+            num_scalar_prefetch=3,
+            grid=(views,),
+            in_specs=[hbm, hbm, packed],
+            out_specs=[
+                pl.BlockSpec((1, keys, half), lambda i, *_: (i, 0, 0)),
+                packed,
+                pl.BlockSpec((1, 1, half), lambda i, *_: (i, 0, 0)),
+            ],
+            scratch_shapes=[
+                pltpu.VMEM((2, views, half, 128), BF16),
+                pltpu.VMEM((keys, 128), BF16),
+                pltpu.VMEM((128, keys), BF16),
+                pltpu.VMEM((keys, half), F32),
+                pltpu.SemaphoreType.DMA((2,)),
+            ],
+        ),
+        out_shape=[
+            jax.ShapeDtypeStruct((views, keys, half), BF16),
+            jax.ShapeDtypeStruct((views, half // 2, 128), BF16),
+            jax.ShapeDtypeStruct((views, 1, half), F32),
+        ],
+        compiler_params=pltpu.CompilerParams(dimension_semantics=("arbitrary",)),
+        cost_estimate=pl.CostEstimate(
+            flops=views * keys * half * 256 * 2,
+            transcendentals=views * keys * half,
+            bytes_accessed=views * keys * half * 2,
+        ),
+        name="forward",
+    )(*routes, own, other, q)
+
+
+def backward(routes, own, other, q, e, o, l, g):
+    views, half, _ = own.shape
+    keys = e.shape[1]
+    hbm, packed = attention_specs(views, half)
+    whole = pl.BlockSpec((views, half, 128), lambda i, *_: (0, 0, 0))
+    return pl.pallas_call(
+        backward_kernel,
+        grid_spec=pltpu.PrefetchScalarGridSpec(
+            num_scalar_prefetch=3,
+            grid=(views,),
+            in_specs=[
+                hbm,
+                hbm,
+                packed,
+                pl.BlockSpec((1, keys, half), lambda i, *_: (i, 0, 0)),
+                packed,
+                pl.BlockSpec((1, 1, half), lambda i, *_: (i, 0, 0)),
+                packed,
+            ],
+            out_specs=[packed, whole, whole],
+            scratch_shapes=[
+                pltpu.VMEM((2, views, half, 128), BF16),
+                pltpu.VMEM((keys, 128), BF16),
+                pltpu.VMEM((128, keys), BF16),
+                pltpu.VMEM((keys, half), BF16),
+                pltpu.VMEM((2, views, half, 128), F32),
+                pltpu.SemaphoreType.DMA((2,)),
+            ],
+        ),
+        out_shape=[
+            jax.ShapeDtypeStruct((views, half // 2, 128), BF16),
+            jax.ShapeDtypeStruct((views, half, 128), F32),
+            jax.ShapeDtypeStruct((views, half, 128), BF16),
+        ],
+        compiler_params=pltpu.CompilerParams(dimension_semantics=("arbitrary",)),
+        cost_estimate=pl.CostEstimate(
+            flops=views * keys * half * 512 * 2,
+            transcendentals=0,
+            bytes_accessed=views * keys * half * 2,
+        ),
+        name="backward",
+    )(*routes, own, other, q, e, o, l, g)
+
+
+def plane_body(query_rows, key_rows, value_rows, out_weight, out_grad, source_view, source_block):
+    tokens, columns = query_rows.shape
+    half = tokens // 2
+    heads = columns // HEAD_DIM
+    keys = source_view.shape[1] * BLOCK_TOKENS
+    group = lax.axis_size("head")
+    head_index = lax.axis_index("head")
+    core = lax.rem(head_index, 2).astype(jnp.int32).reshape(1)
+    plane = lax.div(head_index, 2).astype(jnp.int32).reshape(1)
+    partner = [(i, i ^ 1) for i in range(group)]
+    across = [(i, i ^ 2) for i in range(group)]
+    pairs = [[2 * i, 2 * i + 1] for i in range(group // 2)]
+
+    def core_swap(x):
+        return lax.all_to_all(
+            x, "head", split_axis=0, concat_axis=0, axis_index_groups=pairs, tiled=True
+        )
+
+    def view_swap(x):
+        return lax.all_to_all(x, "view", split_axis=0, concat_axis=0, tiled=True)
+
+    kv, qp = pack(query_rows, key_rows, value_rows)
+    kv = view_swap(core_swap(kv.reshape(2 * heads, half, 128)))
+    qp = view_swap(core_swap(qp.reshape(2 * heads, half // 2, 128)))
+    og = out_grad.reshape(1, 2, half, columns)
+    og = jnp.broadcast_to(og, (group // 2, 2, half, columns)).reshape(group, half, columns)
+    og = lax.all_to_all(og, "head", split_axis=0, concat_axis=0, tiled=True)
+    g = view_swap(attended_grads(plane, og, out_weight, 2 * columns))
+    kv_other = lax.ppermute(kv, "head", partner)
+    routes = (source_view, source_block, core)
+    e, o, l = forward(routes, kv, kv_other, qp, keys)
+    dq, near, far = backward(routes, kv, kv_other, qp, e, o, l, g)
+    o = view_swap(o)
+    mixed = mix(plane, o, lax.ppermute(o, "head", across), out_weight)
+    mixed_out = core_swap(mixed).reshape(tokens, columns)
+    far = lax.ppermute(far, "head", partner)
+    dkv = (near + far.astype(F32)).astype(BF16)
+    dkv = core_swap(view_swap(dkv))
+    dq = core_swap(view_swap(dq))
+    grads = unpack(dkv.reshape(2, heads, half, 128), dq.reshape(2, heads, half // 2, 128))
+    return (mixed_out, *grads)
 
 
 def score_rows(query_part, key_heads, score_scale):
@@ -163,8 +570,20 @@
         P(),
         P(),
     )
+    views, group = mesh.shape["view"], mesh.shape["head"]
+
+    def chosen(*args):
+        columns = args[0].shape[1]
+        fits = (
+            group == 4
+            and 2 * columns == views * HEAD_DIM
+            and columns % 128 == 0
+            and args[0].shape[0] % (4 * BLOCK_TOKENS) == 0
+        )
+        return plane_body(*args) if fits else body(*args)
+
     return jax.shard_map(
-        body,
+        chosen,
         mesh=mesh,
         in_specs=placed,
         out_specs=(P("view", "head"), P("view", "head"), P("view", "head"), P("view", "head")),

time: 370 us -> 215 us (0.58)
  waiting for transfers between devices: 168 us -> 51.3 us
  matrix products: 79.5 us -> 0 us
  blocking collectives: 0 us -> 72.4 us
  local copies, waits for them, and re-layouts: 66.8 us -> 1.88 us
  Pallas kernels: 0 us -> 57.3 us
  other arithmetic: 27.8 us -> 2.45 us
  starting transfers between devices: 11.9 us -> 27.4 us
  between operations: 14.3 us -> 0.78 us
    dot_general x18 -> x0, matrix products: 79.5 us -> none  [the longest x4 17.7 us: score_rows(): jnp.einsum('qhd,khd->hqk', query_part, key_heads, preferred_element_type=...]
    all_to_all x0 -> x6, blocking collectives: none -> 72.4 us  [the longest x1 31.5 us: view_swap(): return lax.all_to_all(x, 'view', split_axis=0, concat_axis=0, tiled=True)]
    all_to_all x2 -> x6, waiting for transfers between devices: 117 us -> 51.3 us  [the longest x5 51.3 us: view_swap(): return lax.all_to_all(x, 'view', split_axis=0, concat_axis=0, tiled=True)]
    pallas_call x0 -> x6, Pallas kernels: none -> 57.3 us  [the longest x1 24.2 us: backward(): pl.pallas_call(backward_kernel, grid_spec=pltpu.PrefetchScalarGridSpec(nu...]
    reduce_scatter x1 -> x0, waiting for transfers between devices: 29.2 us -> none  [body(): lax.psum_scatter(lax.dot_general(part_weight, attended_rows, (((0,), (1,)...]
    all_gather x1 -> x0, waiting for transfers between devices: 21.1 us -> none  [body(): lax.all_gather(out_grad, 'head', axis=1, tiled=True)]
    while x20 -> x0, local copies, waits for them, and re-layouts: 19.3 us -> none
    all_to_all x2 -> x6, starting transfers between devices: 11.9 us -> 26.4 us  [the longest x5 23 us: view_swap(): return lax.all_to_all(x, 'view', split_axis=0, concat_axis=0, tiled=True)]
  transfers between devices with their start and end apart: 4 -> 9, of which waited for: 4 -> 3; matrix products, arithmetic and copies ran while one was open for 5% -> 1% of each run, Pallas kernels for 0% -> 24%
where the time goes in v1:
time: 215 us; the launch traced here: 214 us
  blocking collectives  72.4 us (34%)
  Pallas kernels  57.3 us (27%)
  waiting for transfers between devices  51.3 us (24%)
  starting transfers between devices  27.4 us (13%)
  other arithmetic  2.45 us (1%)
    all_to_all x5, waiting for transfers between devices, view_swap(): return lax.all_to_all(x, 'view', split_axis=0, concat_axis=0, tiled=True)  51.3 us
    all_to_all x1, blocking collectives, view_swap(): return lax.all_to_all(x, 'view', split_axis=0, concat_axis=0, tiled=True)  31.5 us
    pallas_call x1, Pallas kernels, backward(): pl.pallas_call(backward_kernel, grid_spec=pltpu.PrefetchScalarGridSpec(nu...  24.2 us
    all_to_all x5, starting transfers between devices, view_swap(): return lax.all_to_all(x, 'view', split_axis=0, concat_axis=0, tiled=True)  23 us
    all_to_all x4, blocking collectives, core_swap(): lax.all_to_all(x, 'head', split_axis=0, concat_axis=0, axis_index_groups=...  22.3 us
    pallas_call x1, Pallas kernels, forward(): pl.pallas_call(forward_kernel, grid_spec=pltpu.PrefetchScalarGridSpec(num...  21.8 us
    all_to_all x1, blocking collectives, plane_body(): og = lax.all_to_all(og, 'head', split_axis=0, concat_axis=0, tiled=True)  18.6 us
  transfers between devices with their start and end apart: 9, of which 3 were waited for; matrix products, arithmetic and copies ran while one was open for 1% of the time, Pallas kernels for 24%

profile of v1, /device:TPU:0, one launch (start us, length us, event | category | flops | bytes accessed | tf_op | source)
XLA Modules:
  0.0 213.6 jit_solution(3664563399978163358)
XLA Ops:
  0.6 2.6 %pack.1 = (bf16[2,4,512,128]{3,2,1,0:T(8,128)(2,1)}, bf16[2,4,256,128]{3,2,1,0:T(8,128)(2,1)}) custom-call(bf16[1024,256]{1,0:T(8,128)(2,1)} %q_ref.1, bf16[1024,256]{1,0:T(8,128)(2,1)} %k_ref.1, bf16[1024,256]{1,0:T(8,128)(2,1)} %v_ref.1), custom_call_target="tpu_custom_call" | custom-call | tf_op jit(solution)/shard_map/pack/pallas_call | solution.py:46
  3.2 6.1 %all_to_all.60 = bf16[8,256,128]{2,1,0:T(8,128)(2,1)} all-to-all(bf16[8,256,128]{2,1,0:T(8,128)(2,1)} %bitcast.15), channel_id=1, replica_groups={{0,1},{2,3},{4,5},{6,7},{8,9},{10,11},{12,13},{14,15},{16,17},{18,19},{..., dimensions={0} | all-to-all | bytes 1048576 | tf_op jit(solution)/shard_map/all_to_all | solution.py:388
  9.3 5.7 %all_to_all.61 = bf16[8,512,128]{2,1,0:T(8,128)(2,1)S(1)} all-to-all(bf16[8,512,128]{2,1,0:T(8,128)(2,1)} %bitcast.13), channel_id=1, replica_groups={{0,1},{2,3},{4,5},{6,7},{8,9},{10,11},{12,13},{14,15},{16,17},{18,19},{..., dimensions={0} | all-to-all | bytes 2097152 | tf_op jit(solution)/shard_map/all_to_all | solution.py:388
  15.0 0.1 broadcast_in_dim.8
  15.1 18.6 %all_to_all.62.og_ref = bf16[4,512,256]{2,1,0:T(8,128)(2,1)} all-to-all(bf16[4,512,256]{2,1,0:T(8,128)(2,1)S(1)} %bitcast.10), channel_id=1, replica_groups=mesh['view'=8,'head'=4] {'head'}, dimensions={0} | all-to-all | bytes 2097152 | tf_op jit(solution)/shard_map/all_to_all | solution.py:400
  33.6 31.5 %all_to_all.63.own_ref = bf16[8,512,128]{2,1,0:T(8,128)(2,1)S(1)} all-to-all(bf16[8,512,128]{2,1,0:T(8,128)(2,1)S(1)} %all_to_all.61), channel_id=1, replica_groups=mesh['view'=8,'head'=4] {'view'}, dimensions={0} | all-to-all | bytes 2097152 | tf_op jit(solution)/shard_map/all_to_all | solution.py:393
  65.2 3.5 %all-to-all-start.3 = ((bf16[8,256,128]{2,1,0:T(8,128)(2,1)}), bf16[8,256,128]{2,1,0:T(8,128)(2,1)S(1)}, u32[]{:S(2)}, u32[]{:S(2)}) async-start(bf16[8,256,128]{2,1,0:T(8,128)(2,1)} %all_to_all.60), calls=%async_computation.3 | async-start | bytes 1048576 | tf_op jit(solution)/shard_map/all_to_all | solution.py:393
  68.7 0.0 collective-permute-start
  68.8 3.2 %attended_grads.1 = bf16[8,256,128]{2,1,0:T(8,128)(2,1)} custom-call(s32[1]{0:T(128)} %bitcast.x_ref, bf16[4,512,256]{2,1,0:T(8,128)(2,1)} %all_to_all.62.og_ref, bf16[1024,1024]{1,0:T(8,128)(2,1)} %w_ref.3), custom_call_target="tpu_custom_call" | custom-call | tf_op jit(solution)/shard_map/attended_grads/pallas_call | solution.py:113
  71.9 10.9 %all-to-all-done.3.q_ref = bf16[8,256,128]{2,1,0:T(8,128)(2,1)S(1)} async-done(((bf16[8,256,128]{2,1,0:T(8,128)(2,1)}), bf16[8,256,128]{2,1,0:T(8,128)(2,1)S(1)}, u32[]{:S(2)}, u32[]{:S(2)}) %all-to-all-start.3) | async-done | bytes 524320 | tf_op jit(solution)/shard_map/all_to_all | solution.py:393
  82.8 3.6 %all-to-all-start.7 = ((bf16[8,256,128]{2,1,0:T(8,128)(2,1)}), bf16[8,256,128]{2,1,0:T(8,128)(2,1)S(1)}, u32[]{:S(2)}, u32[]{:S(2)}) async-start(bf16[8,256,128]{2,1,0:T(8,128)(2,1)} %attended_grads.1), calls=%async_computation.7 | async-start | bytes 1048576 | tf_op jit(solution)/shard_map/all_to_all | solution.py:393
  86.5 1.0 copy-done.7
  87.5 21.8 %forward.1 = (bf16[8,2048,512]{2,1,0:T(8,128)(2,1)}, bf16[8,256,128]{2,1,0:T(8,128)(2,1)}, f32[8,1,512]{2,1,0:T(1,128)}) custom-call(s32[8,16]{1,0:T(8,128)} %sv_ref.3, s32[8,16]{1,0:T(8,128)} %sb_ref.3, s32[1]{0:T(128)} %bitcast.1.c_ref, bf16[8,512,128]{2,1,0:T(8,128)(2,1)} %copy-done.3, bf16[8,512,128]{2,1,0:T(8,128)(2,1)} %copy-done.7, ...), custom_call_target="tpu_custom_call" | custom-call | flops 4294967296 | bytes 16777216 | tf_op jit(solution)/shard_map/forward/pallas_call | solution.py:296
  109.3 0.0 copy-start.6
  109.3 6.0 %all-to-all-start.4 = ((bf16[8,256,128]{2,1,0:T(8,128)(2,1)}), bf16[8,256,128]{2,1,0:T(8,128)(2,1)S(1)}, u32[]{:S(2)}, u32[]{:S(2)}) async-start(bf16[8,256,128]{2,1,0:T(8,128)(2,1)} %get-tuple-element.17.o_ref), calls=%async_computation.4 | async-start | bytes 1048576 | tf_op jit(solution)/shard_map/all_to_all | solution.py:393
  115.3 24.2 %backward.1 = (bf16[8,256,128]{2,1,0:T(8,128)(2,1)}, f32[8,512,128]{2,1,0:T(8,128)}, bf16[8,512,128]{2,1,0:T(8,128)(2,1)}) custom-call(s32[8,16]{1,0:T(8,128)} %sv_ref.3, s32[8,16]{1,0:T(8,128)} %sb_ref.3, s32[1]{0:T(128)} %bitcast.1.c_ref, bf16[8,512,128]{2,1,0:T(8,128)(2,1)} %copy-done.3, bf16[8,512,128]{2,1,0:T(8,128)(2,1)} %copy-done.7, ...), custom_call_target="tpu_custom_call" | custom-call | flops 8589934592 | bytes 16777216 | tf_op jit(solution)/shard_map/backward/pallas_call | solution.py:335
  139.5 0.1 collective-permute-start.2
  139.6 0.0 all-to-all-done.4.own_ref
  139.6 0.0 copy-start.2
  139.6 6.1 %all-to-all-start.10 = ((bf16[8,256,128]{2,1,0:T(8,128)(2,1)}), bf16[8,256,128]{2,1,0:T(8,128)(2,1)}, u32[]{:S(2)}, u32[]{:S(2)}) async-start(bf16[8,256,128]{2,1,0:T(8,128)(2,1)} %get-tuple-element.22), calls=%async_computation.10 | async-start | bytes 1048576 | tf_op jit(solution)/shard_map/all_to_all | solution.py:393
  145.7 0.9 collective-permute-start.1
  146.6 14.2 %all-to-all-done.10 = bf16[8,256,128]{2,1,0:T(8,128)(2,1)} async-done(((bf16[8,256,128]{2,1,0:T(8,128)(2,1)}), bf16[8,256,128]{2,1,0:T(8,128)(2,1)}, u32[]{:S(2)}, u32[]{:S(2)}) %all-to-all-start.10) | async-done | bytes 524320 | tf_op jit(solution)/shard_map/all_to_all | solution.py:393
  160.8 3.5 %all-to-all-start.11 = ((bf16[8,256,128]{2,1,0:T(8,128)(2,1)}), bf16[8,256,128]{2,1,0:T(8,128)(2,1)S(1)}, u32[]{:S(2)}, u32[]{:S(2)}) async-start(bf16[8,256,128]{2,1,0:T(8,128)(2,1)} %all-to-all-done.10), calls=%async_computation.11 | async-start | bytes 1048576 | tf_op jit(solution)/shard_map/all_to_all | solution.py:388
  164.3 0.0 collective-permute-done.2
  164.3 2.4 %add_convert_fusion = bf16[8,512,128]{2,1,0:T(8,128)(2,1)} fusion(f32[8,512,128]{2,1,0:T(8,128)S(1)} %copy-done.1, bf16[8,512,128]{2,1,0:T(8,128)(2,1)} %collective-permute-done.2), kind=kLoop, calls=%fused_computation | loop fusion | flops 1572864 | bytes 4194304 | tf_op jit(solution)/shard_map/convert_element_type | solution.py:410
  166.8 3.1 %mix.1 = bf16[2,512,256]{2,1,0:T(8,128)(2,1)} custom-call(s32[1]{0:T(128)} %bitcast.x_ref, bf16[8,256,128]{2,1,0:T(8,128)(2,1)} %copy-done.2, bf16[8,256,128]{2,1,0:T(8,128)(2,1)} %collective-permute-done.1.other_ref, bf16[1024,1024]{1,0:T(8,128)(2,1)} %w_ref.3), custom_call_target="tpu_custom_call" | custom-call | tf_op jit(solution)/shard_map/mix/pallas_call | solution.py:160
  169.9 5.2 %all_to_all.64 = bf16[2,512,256]{2,1,0:T(8,128)(2,1)S(1)} all-to-all(bf16[2,512,256]{2,1,0:T(8,128)(2,1)} %mix.1), channel_id=1, replica_groups={{0,1},{2,3},{4,5},{6,7},{8,9},{10,11},{12,13},{14,15},{16,17},{18,19},{..., dimensions={0} | all-to-all | bytes 1048576 | tf_op jit(solution)/shard_map/all_to_all | solution.py:388
  175.1 3.6 %all-to-all-start.8 = ((bf16[8,512,128]{2,1,0:T(8,128)(2,1)}), bf16[8,512,128]{2,1,0:T(8,128)(2,1)S(1)}, u32[]{:S(2)}, u32[]{:S(2)}) async-start(bf16[8,512,128]{2,1,0:T(8,128)(2,1)} %add_convert_fusion), calls=%async_computation.8 | async-start | bytes 2097152 | tf_op jit(solution)/shard_map/all_to_all | solution.py:393
  178.8 26.2 %all-to-all-done.8 = bf16[8,512,128]{2,1,0:T(8,128)(2,1)S(1)} async-done(((bf16[8,512,128]{2,1,0:T(8,128)(2,1)}), bf16[8,512,128]{2,1,0:T(8,128)(2,1)S(1)}, u32[]{:S(2)}, u32[]{:S(2)}) %all-to-all-start.8) | async-done | bytes 1048608 | tf_op jit(solution)/shard_map/all_to_all | solution.py:393
  204.9 5.4 %all_to_all.65 = bf16[8,512,128]{2,1,0:T(8,128)(2,1)} all-to-all(bf16[8,512,128]{2,1,0:T(8,128)(2,1)S(1)} %all-to-all-done.8), channel_id=1, replica_groups={{0,1},{2,3},{4,5},{6,7},{8,9},{10,11},{12,13},{14,15},{16,17},{18,19},{..., dimensions={0} | all-to-all | bytes 2097152 | tf_op jit(solution)/shard_map/all_to_all | solution.py:388
  210.3 2.5 %unpack.1 = (bf16[1024,256]{1,0:T(8,128)(2,1)}, bf16[1024,256]{1,0:T(8,128)(2,1)}, bf16[1024,256]{1,0:T(8,128)(2,1)}) custom-call(bf16[2,4,512,128]{3,2,1,0:T(8,128)(2,1)} %bitcast.9, bf16[2,4,256,128]{3,2,1,0:T(8,128)(2,1)} %bitcast.11), custom_call_target="tpu_custom_call" | custom-call | tf_op jit(solution)/shard_map/unpack/pallas_call | solution.py:78
  212.8 0.8 copy.12
  (17 shorter events, 0.0 us)
Async XLA Ops:
  0.6 14.4 %copy-start.4 = (bf16[1024,256]{1,0:T(8,128)(2,1)S(1)}, bf16[1024,256]{1,0:T(8,128)(2,1)}, u32[]{:S(2)}) copy-start(bf16[1024,256]{1,0:T(8,128)(2,1)} %param.11) | copy-start | bytes 1572868
  65.2 6.8 %copy-start.3 = (bf16[8,512,128]{2,1,0:T(8,128)(2,1)}, bf16[8,512,128]{2,1,0:T(8,128)(2,1)S(1)}, u32[]{:S(2)}) copy-start(bf16[8,512,128]{2,1,0:T(8,128)(2,1)S(1)} %all_to_all.63.own_ref) | copy-start | bytes 3145732
  65.2 17.7 %all-to-all-start.3 = ((bf16[8,256,128]{2,1,0:T(8,128)(2,1)}), bf16[8,256,128]{2,1,0:T(8,128)(2,1)S(1)}, u32[]{:S(2)}, u32[]{:S(2)}) async-start(bf16[8,256,128]{2,1,0:T(8,128)(2,1)} %all_to_all.60), calls=%async_computation.3 | async-start | bytes 1048576 | tf_op jit(solution)/shard_map/all_to_all | solution.py:393
  68.7 17.8 %collective-permute-start = (bf16[8,512,128]{2,1,0:T(8,128)(2,1)S(1)}, bf16[8,512,128]{2,1,0:T(8,128)(2,1)S(1)}, u32[]{:S(2)}, u32[]{:S(2)}) collective-permute-start(bf16[8,512,128]{2,1,0:T(8,128)(2,1)S(1)} %all_to_all.63.own_ref), channel_id=1, source_target_pairs={{0,1},{1,0},{2,3},{3,2},{4,5},{5,4},{6,7},{7,6},{8,9},{9,8},{10,11... | collective-permute-start | bytes 3145736 | tf_op jit(solution)/shard_map/ppermute | solution.py:402
  82.8 3.7 %copy-start.5 = (bf16[8,256,128]{2,1,0:T(8,128)(2,1)}, bf16[8,256,128]{2,1,0:T(8,128)(2,1)S(1)}, u32[]{:S(2)}) copy-start(bf16[8,256,128]{2,1,0:T(8,128)(2,1)S(1)} %all-to-all-done.3.q_ref) | copy-start | bytes 1572868
  82.8 26.5 %all-to-all-start.7 = ((bf16[8,256,128]{2,1,0:T(8,128)(2,1)}), bf16[8,256,128]{2,1,0:T(8,128)(2,1)S(1)}, u32[]{:S(2)}, u32[]{:S(2)}) async-start(bf16[8,256,128]{2,1,0:T(8,128)(2,1)} %attended_grads.1), calls=%async_computation.7 | async-start | bytes 1048576 | tf_op jit(solution)/shard_map/all_to_all | solution.py:393
  86.5 1.0 copy-start.7
  109.3 6.0 %copy-start.6 = (bf16[8,256,128]{2,1,0:T(8,128)(2,1)}, bf16[8,256,128]{2,1,0:T(8,128)(2,1)S(1)}, u32[]{:S(2)}) copy-start(bf16[8,256,128]{2,1,0:T(8,128)(2,1)S(1)} %all-to-all-done.7.g_ref) | copy-start | bytes 1572868
  109.3 30.3 %all-to-all-start.4 = ((bf16[8,256,128]{2,1,0:T(8,128)(2,1)}), bf16[8,256,128]{2,1,0:T(8,128)(2,1)S(1)}, u32[]{:S(2)}, u32[]{:S(2)}) async-start(bf16[8,256,128]{2,1,0:T(8,128)(2,1)} %get-tuple-element.17.o_ref), calls=%async_computation.4 | async-start | bytes 1048576 | tf_op jit(solution)/shard_map/all_to_all | solution.py:393
  139.5 24.8 %copy-start.1 = (f32[8,512,128]{2,1,0:T(8,128)S(1)}, f32[8,512,128]{2,1,0:T(8,128)}, u32[]{:S(2)}) copy-start(f32[8,512,128]{2,1,0:T(8,128)} %get-tuple-element.20) | copy-start | bytes 6291460
  139.5 24.8 %collective-permute-start.2 = (bf16[8,512,128]{2,1,0:T(8,128)(2,1)}, bf16[8,512,128]{2,1,0:T(8,128)(2,1)}, u32[]{:S(2)}, u32[]{:S(2)}) collective-permute-start(bf16[8,512,128]{2,1,0:T(8,128)(2,1)} %get-tuple-element.21), channel_id=1, source_target_pairs={{0,1},{1,0},{2,3},{3,2},{4,5},{5,4},{6,7},{7,6},{8,9},{9,8},{10,11... | collective-permute-start | bytes 3145736 | tf_op jit(solution)/shard_map/ppermute | solution.py:409
  139.6 27.2 %copy-start.2 = (bf16[8,256,128]{2,1,0:T(8,128)(2,1)}, bf16[8,256,128]{2,1,0:T(8,128)(2,1)S(1)}, u32[]{:S(2)}) copy-start(bf16[8,256,128]{2,1,0:T(8,128)(2,1)S(1)} %all-to-all-done.4.own_ref) | copy-start | bytes 1572868
  139.6 21.2 %all-to-all-start.10 = ((bf16[8,256,128]{2,1,0:T(8,128)(2,1)}), bf16[8,256,128]{2,1,0:T(8,128)(2,1)}, u32[]{:S(2)}, u32[]{:S(2)}) async-start(bf16[8,256,128]{2,1,0:T(8,128)(2,1)} %get-tuple-element.22), calls=%async_computation.10 | async-start | bytes 1048576 | tf_op jit(solution)/shard_map/all_to_all | solution.py:393
  145.7 21.1 %collective-permute-start.1 = (bf16[8,256,128]{2,1,0:T(8,128)(2,1)S(1)}, bf16[8,256,128]{2,1,0:T(8,128)(2,1)}, u32[]{:S(2)}, u32[]{:S(2)}) collective-permute-start(bf16[8,256,128]{2,1,0:T(8,128)(2,1)S(1)} %all-to-all-done.4.own_ref), channel_id=1, source_target_pairs={{0,2},{1,3},{2,0},{3,1},{4,6},{5,7},{6,4},{7,5},{8,10},{9,11},{10,... | collective-permute-start | bytes 1572872 | tf_op jit(solution)/shard_map/ppermute | solution.py:407
  160.8 9.1 %all-to-all-start.11 = ((bf16[8,256,128]{2,1,0:T(8,128)(2,1)}), bf16[8,256,128]{2,1,0:T(8,128)(2,1)S(1)}, u32[]{:S(2)}, u32[]{:S(2)}) async-start(bf16[8,256,128]{2,1,0:T(8,128)(2,1)} %all-to-all-done.10), calls=%async_computation.11 | async-start | bytes 1048576 | tf_op jit(solution)/shard_map/all_to_all | solution.py:388
  169.9 40.4 %copy-start = (bf16[8,256,128]{2,1,0:T(8,128)(2,1)}, bf16[8,256,128]{2,1,0:T(8,128)(2,1)S(1)}, u32[]{:S(2)}) copy-start(bf16[8,256,128]{2,1,0:T(8,128)(2,1)S(1)} %all-to-all-done.11) | copy-start | bytes 1572868
  175.1 29.8 %all-to-all-start.8 = ((bf16[8,512,128]{2,1,0:T(8,128)(2,1)}), bf16[8,512,128]{2,1,0:T(8,128)(2,1)S(1)}, u32[]{:S(2)}, u32[]{:S(2)}) async-start(bf16[8,512,128]{2,1,0:T(8,128)(2,1)} %add_convert_fusion), calls=%async_computation.8 | async-start | bytes 2097152 | tf_op jit(solution)/shard_map/all_to_all | solution.py:393

commit v2 on v0

--- a/solution.py
+++ b/solution.py
@@ -1,10 +1,555 @@
 import jax
 import jax.numpy as jnp
 from jax import lax
+from jax.experimental import pallas as pl
+from jax.experimental.pallas import tpu as pltpu
 from jax.sharding import PartitionSpec as P
+
 
 HEAD_DIM = 64
 BLOCK_TOKENS = 128
+LOG2E = 1.4426950408889634
+F32 = jnp.float32
+BF16 = jnp.bfloat16
+HBM = pl.BlockSpec(memory_space=pl.ANY)
+
+
+def join(a, b):
+    return jnp.concatenate([a[:, :HEAD_DIM], b[:, :HEAD_DIM]], axis=1)
+
+
+def join_high(a, b):
+    return jnp.concatenate([a[:, HEAD_DIM:], b[:, HEAD_DIM:]], axis=1)
+
+
+def dot(a, b):
+    return jnp.dot(a, b, preferred_element_type=F32)
+
+
+def aligned(index, size):
+    return pl.ds(pl.multiple_of(index * size, size), size)
+
+
+def call(kernel, scalars, args, in_specs, out_specs, out_shape, grid=(1,), scratch=(), flops=0):
+    return pl.pallas_call(
+        kernel,
+        grid_spec=pltpu.PrefetchScalarGridSpec(
+            num_scalar_prefetch=len(scalars),
+            grid=grid,
+            in_specs=in_specs,
+            out_specs=out_specs,
+            scratch_shapes=list(scratch),
+        ),
+        out_shape=out_shape,
+        compiler_params=pltpu.CompilerParams(dimension_semantics=("arbitrary",) * len(grid)),
+        cost_estimate=pl.CostEstimate(flops=flops, transcendentals=0, bytes_accessed=0)
+        if flops
+        else None,
+    )(*scalars, *args)
+
+
+def whole(*shape):
+    return pl.BlockSpec(shape, lambda *_: (0,) * len(shape))
+
+
+def shape_of(*shape, dtype=BF16):
+    return jax.ShapeDtypeStruct(shape, dtype)
+
+
+def messages(count):
+    return [(j, i) for j in range(count) for i in range(2)]
+
+
+def source_of(meta_ref, core, j, i, count):
+    return (core ^ i) * count + (meta_ref[1] ^ j)
+
+
+def pick(meta_ref, ref, j, i, rows):
+    head, half = meta_ref[1] ^ j, meta_ref[2] ^ i
+    return ref[aligned(half, rows), aligned(head // 2, 128)], head % 2 == 1
+
+
+def pack_kq(meta_ref, q_ref, k_ref, *outs):
+    rows = q_ref.shape[0] // 2
+    for out, (j, i) in zip(outs, messages(len(outs) // 2)):
+        k, odd = pick(meta_ref, k_ref, j, i, rows)
+        q, _ = pick(meta_ref, q_ref, j, i, rows)
+        out[...] = jnp.where(odd, join_high(k, q), join(k, q))
+
+
+def pack_v(meta_ref, v_ref, keep_ref, give_ref):
+    rows = v_ref.shape[0] // 2
+    for out_ref, half in ((keep_ref, meta_ref[0]), (give_ref, 1 - meta_ref[0])):
+        for pair in range(out_ref.shape[0] // 2):
+            v = v_ref[aligned(half, rows), 128 * pair : 128 * (pair + 1)]
+            top, low = v[: rows // 2], v[rows // 2 :]
+            out_ref[2 * pair] = join(top, low)
+            out_ref[2 * pair + 1] = join_high(top, low)
+
+
+def unpack_kq(meta_ref, *refs):
+    count = (len(refs) - 4) // 2
+    parts, (q_ref, k_ref, scr, sem) = refs[: 2 * count], refs[2 * count :]
+    copies = [
+        pltpu.make_async_copy(part, scr.at[meta_ref[2] ^ i, meta_ref[1] ^ j], sem.at[n])
+        for n, (part, (j, i)) in enumerate(zip(parts, messages(count)))
+    ]
+    for copy in copies:
+        copy.start()
+    for copy in copies:
+        copy.wait()
+    rows = scr.shape[2]
+    for half in range(2):
+        for pair in range(count // 2):
+            lanes = slice(128 * pair, 128 * (pair + 1))
+            a, b = scr[half, 2 * pair], scr[half, 2 * pair + 1]
+            k_ref[half * rows : (half + 1) * rows, lanes] = join(a, b)
+            q_ref[half * rows : (half + 1) * rows, lanes] = join_high(a, b)
+
+
+def unpack_v(meta_ref, all_ref, got_ref, v_ref, scr, sem):
+    c = meta_ref[0]
+    count = scr.shape[1]
+    copies = [
+        pltpu.make_async_copy(
+            all_ref.at[pl.ds(c * count, count), pl.ds(0, scr.shape[2])], scr.at[c], sem.at[0]
+        ),
+        pltpu.make_async_copy(got_ref, scr.at[1 - c], sem.at[1]),
+    ]
+    for copy in copies:
+        copy.start()
+    for copy in copies:
+        copy.wait()
+    rows = 2 * scr.shape[2]
+    for half in range(2):
+        for pair in range(count // 2):
+            lanes = slice(128 * pair, 128 * (pair + 1))
+            a, b = scr[half, 2 * pair], scr[half, 2 * pair + 1]
+            v_ref[half * rows : half * rows + rows // 2, lanes] = join(a, b)
+            v_ref[half * rows + rows // 2 : (half + 1) * rows, lanes] = join_high(a, b)
+
+
+def attended_grads(place_ref, *refs):
+    parts, (keep_ref, got_ref, w_ref, out_ref) = refs[:-4], refs[-4:]
+    rows, columns = parts[0].shape
+    total = None
+    for n, part in enumerate(parts):
+        piece = lax.dot_general(
+            part[...],
+            w_ref[:, aligned(place_ref[1] ^ n, columns)],
+            (((1,), (1,)), ((), ())),
+            preferred_element_type=F32,
+        )
+        total = piece if total is None else total + piece
+    total = total.astype(BF16)
+    for pair in range(total.shape[1] // 128):
+        lanes = slice(128 * pair, 128 * (pair + 1))
+        top, low = total[: rows // 2, lanes], total[rows // 2 :, lanes]
+        out_ref[2 * pair, rows // 2 :, :] = join(top, low)
+        out_ref[2 * pair + 1, rows // 2 :, :] = join_high(top, low)
+    count = keep_ref.shape[0]
+    core = place_ref[1] % 2
+    out_ref[pl.ds(core * count, count), : rows // 2, :] = keep_ref[...]
+    out_ref[pl.ds((1 - core) * count, count), : rows // 2, :] = got_ref[...]
+
+
+def combine_v(near_ref, far_ref, o_ref, out_ref):
+    rows = near_ref.shape[1]
+    out_ref[:, :rows, :] = (near_ref[...] + far_ref[...].astype(F32)).astype(BF16)
+    out_ref[:, rows:, :] = o_ref[...]
+
+
+def mix(place_ref, own_ref, other_ref, w_ref, keep_ref, send_ref):
+    heads = own_ref.shape[0]
+    depth = heads * HEAD_DIM
+    x = place_ref[0]
+
+    def rows_of(ref):
+        top, low = [], []
+        for pair in range(heads // 2):
+            a, b = ref[2 * pair], ref[2 * pair + 1]
+            top.append(join(a, b))
+            low.append(join_high(a, b))
+        return jnp.concatenate(
+            [jnp.concatenate(top, axis=1), jnp.concatenate(low, axis=1)], axis=0
+        )
+
+    own = dot(rows_of(own_ref), w_ref[aligned(x, depth), :])
+    other = dot(rows_of(other_ref), w_ref[aligned(1 - x, depth), :])
+    mixed = (own + other).astype(BF16)
+    width = mixed.shape[1] // 2
+    first = place_ref[1] % 2 == 0
+    keep_ref[...] = jnp.where(first, mixed[:, :width], mixed[:, width:])
+    send_ref[...] = jnp.where(first, mixed[:, width:], mixed[:, :width])
+
+
+def place(sv_ref, sb_ref, view, slot, per_part):
+    block = sb_ref[view, slot]
+    return lax.div(block, per_part), sv_ref[view, slot], aligned(lax.rem(block, per_part), BLOCK_TOKENS)
+
+
+def gather(sv_ref, sb_ref, view, src, rows_scr, turned_scr):
+    per_half = src.shape[2] // BLOCK_TOKENS
+    for slot in range(sv_ref.shape[1]):
+        half, source, rows = place(sv_ref, sb_ref, view, slot, per_half)
+        block = src[half, source, rows, :]
+        span = slice(slot * BLOCK_TOKENS, (slot + 1) * BLOCK_TOKENS)
+        if rows_scr is not None:
+            rows_scr[span, :] = block
+        if turned_scr is not None:
+            turned_scr[:, span] = block.T
+
+
+def scatter_folded(sv_ref, sb_ref, view, acc, lhs_ref, rhs_scr):
+    per_quarter = acc.shape[2] // BLOCK_TOKENS
+    for slot in range(sv_ref.shape[1]):
+        quarter, source, rows = place(sv_ref, sb_ref, view, slot, per_quarter)
+        span = slice(slot * BLOCK_TOKENS, (slot + 1) * BLOCK_TOKENS)
+        acc[lax.div(quarter, 2), source, rows, :] += dot(
+            lhs_ref[span, :], rhs_scr[lax.rem(quarter, 2)]
+        )
+
+
+def hand_back(meta_ref, acc, near_ref, far_ref):
+    c = meta_ref[0]
+    count = acc.shape[1] // 2
+    for n, (j, i) in enumerate(messages(count)):
+        near_ref[n] = acc[c, source_of(meta_ref, c, j, i, count)]
+        far_ref[n] = acc[1 - c, source_of(meta_ref, 1 - c, j, i, count)].astype(BF16)
+
+
+def hand_back_views(meta_ref, acc, near_ref, far_ref):
+    near_ref[...] = acc[meta_ref[0]]
+    far_ref[...] = acc[1 - meta_ref[0]].astype(BF16)
+
+
+def bring(meta_ref, own, other, scr, sem):
+    c = meta_ref[0]
+    count = len(own) // 2
+    copies = []
+    for n, (j, i) in enumerate(messages(count)):
+        for core, part, s in ((c, own[n], 2 * n), (1 - c, other[n], 2 * n + 1)):
+            where = scr.at[core, source_of(meta_ref, core, j, i, count)]
+            copies.append(pltpu.make_async_copy(part, where, sem.at[s]))
+    for copy in copies:
+        copy.start()
+    for copy in copies:
+        copy.wait()
+
+
+def unfold(block):
+    t = block.T
+    return jnp.concatenate([t[:HEAD_DIM], t[HEAD_DIM:]], axis=1)
+
+
+def fold(t):
+    width = t.shape[1] // 2
+    return jnp.concatenate([t[:, :width], t[:, width:]], axis=0).T
+
+
+SCALE = HEAD_DIM**-0.5
+
+
+def scores(sv_ref, sb_ref, meta_ref, *refs):
+    views = (len(refs) - 6) // 2
+    own, other = refs[:views], refs[views : 2 * views]
+    kq_ref, e_ref, l_ref, rows_scr, s_scr, sem = refs[2 * views :]
+    view = pl.program_id(0)
+
+    @pl.when(view == 0)
+    def _():
+        bring(meta_ref, own, other, kq_ref, sem)
+
+    gather(sv_ref, sb_ref, view, kq_ref, rows_scr, None)
+    keys, queries = s_scr.shape
+    step = 256
+    q = kq_ref[meta_ref[0], view].T[HEAD_DIM:] * jnp.asarray(SCALE, BF16)
+    q = jnp.concatenate([q, jnp.zeros_like(q)], axis=0)
+    top = None
+    for i in range(keys // step):
+        s = dot(rows_scr[i * step : (i + 1) * step, :], q)
+        s_scr[i * step : (i + 1) * step, :] = s
+        t = jnp.max(s.reshape(step // 8, 8, queries), axis=0)
+        top = t if top is None else jnp.maximum(top, t)
+    top = jnp.max(top, axis=0, keepdims=True)
+    total = None
+    for i in range(keys // step):
+        e = jnp.exp2((s_scr[i * step : (i + 1) * step, :] - top) * LOG2E)
+        t = jnp.sum(e.reshape(step // 8, 8, queries), axis=0)
+        total = t if total is None else total + t
+        e_ref[0, i * step : (i + 1) * step, :] = e.astype(BF16)
+    l_ref[0] = jnp.sum(total, axis=0, keepdims=True)
+
+
+def attend(sv_ref, sb_ref, meta_ref, *refs):
+    (
+        own, other, kq_ref, e_ref, l_ref, g_ref, kv_ref, o_ref, near_ref, far_ref,
+        kq_scr, v_scr, turned_scr, g_scr, acc, sem,
+    ) = refs
+    views = kq_scr.shape[1]
+    view = pl.program_id(0)
+
+    @pl.when(view == 0)
+    def _():
+        c = meta_ref[0]
+        copies = [
+            pltpu.make_async_copy(kq_ref, kq_scr, sem.at[0]),
+            pltpu.make_async_copy(own.at[:, pl.ds(0, v_scr.shape[2])], v_scr.at[c], sem.at[1]),
+            pltpu.make_async_copy(
+                other.at[:, pl.ds(0, v_scr.shape[2])], v_scr.at[1 - c], sem.at[2]
+            ),
+        ]
+        for copy in copies:
+            copy.start()
+        for copy in copies:
+            copy.wait()
+        acc[...] = jnp.zeros_like(acc)
+        rows = v_scr.shape[2]
+        for half in range(2):
+            for source in range(views):
+                v = v_scr[half, source]
+                k = kq_scr[half, source]
+                kv_ref[half, source, :rows, :] = join(k[:rows], v)
+                kv_ref[half, source, rows:, :] = jnp.concatenate(
+                    [k[rows:, :HEAD_DIM], v[:, HEAD_DIM:]], axis=1
+                )
+
+    gather(sv_ref, sb_ref, view, kv_ref, None, turned_scr)
+    out = dot(turned_scr[...], e_ref[0])[HEAD_DIM:] / l_ref[0]
+    o_ref[0] = fold(out).astype(BF16)
+    g = (unfold(g_ref[0]).astype(F32) / l_ref[0]).astype(BF16)
+    zero = jnp.zeros_like(g)
+    g_scr[0] = jnp.concatenate([g, zero], axis=0).T
+    g_scr[1] = jnp.concatenate([zero, g], axis=0).T
+    scatter_folded(sv_ref, sb_ref, view, acc, e_ref.at[0], g_scr)
+
+    @pl.when(view == pl.num_programs(0) - 1)
+    def _():
+        hand_back_views(meta_ref, acc, near_ref, far_ref)
+
+
+def backward(
+    sv_ref, sb_ref, meta_ref, kv_ref, kq_ref, e_ref, o_ref, l_ref, g_ref,
+    dq_ref, near_ref, far_ref, kv_scr, q_scr, rows_scr, turned_scr, ds_scr, qz_scr, acc, sem,
+):
+    view = pl.program_id(0)
+
+    @pl.when(view == 0)
+    def _():
+        first = pltpu.make_async_copy(kv_ref, kv_scr, sem.at[0])
+        second = pltpu.make_async_copy(kq_ref.at[meta_ref[0]], q_scr, sem.at[1])
+        first.start()
+        second.start()
+        acc[...] = jnp.zeros_like(acc)
+        first.wait()
+        second.wait()
+
+    gather(sv_ref, sb_ref, view, kv_scr, rows_scr, turned_scr)
+    keys, _ = ds_scr.shape
+    step = 256
+    q = q_scr[view].T[HEAD_DIM:] * jnp.asarray(SCALE, BF16)
+    zero = jnp.zeros_like(q)
+    qz_scr[0] = jnp.concatenate([q, zero], axis=0).T
+    qz_scr[1] = jnp.concatenate([zero, q], axis=0).T
+    g = (unfold(g_ref[0]).astype(F32) / l_ref[0]).astype(BF16)
+    delta = jnp.sum(unfold(o_ref[0]).astype(F32) * g.astype(F32), axis=0, keepdims=True)
+    g = jnp.concatenate([zero, g], axis=0)
+    for i in range(keys // step):
+        rows = slice(i * step, (i + 1) * step)
+        dp = dot(rows_scr[rows, :], g)
+        ds_scr[rows, :] = (e_ref[0, rows, :].astype(F32) * (dp - delta)).astype(BF16)
+    scatter_folded(sv_ref, sb_ref, view, acc, ds_scr, qz_scr)
+    dq = dot(turned_scr[...], ds_scr[...])[:HEAD_DIM] * SCALE
+    dq_ref[0] = jnp.concatenate([jnp.zeros_like(dq), dq], axis=0).T.astype(BF16)
+
+    @pl.when(view == pl.num_programs(0) - 1)
+    def _():
+        hand_back(meta_ref, acc, near_ref, far_ref)
+
+
+def combine_kq(meta_ref, near_ref, far_ref, dq_ref, *outs):
+    count = len(outs) // 2
+    rows = near_ref.shape[1]
+    for n, (out, (j, i)) in enumerate(zip(outs, messages(count))):
+        dk = (near_ref[n] + far_ref[n].astype(F32)).astype(BF16)
+        dq = dq_ref[source_of(meta_ref, meta_ref[0], j, i, count)]
+        out[:rows, :] = jnp.concatenate([dk[:, :HEAD_DIM], dq[:rows, HEAD_DIM:]], axis=1)
+        out[rows:, :] = join_high(dk, dq[rows:])
+
+
+def plane_body(query_rows, key_rows, value_rows, out_weight, out_grad, source_view, source_block):
+    tokens, columns = query_rows.shape
+    half = tokens // 2
+    count = columns // HEAD_DIM
+    views = 2 * count
+    keys = source_view.shape[1] * BLOCK_TOKENS
+    group = lax.axis_size("head")
+    head_index = lax.axis_index("head").astype(jnp.int32)
+    view_index = lax.axis_index("view").astype(jnp.int32)
+    core = lax.rem(head_index, 2)
+    meta = jnp.stack([core, lax.rem(view_index, count), lax.div(view_index, count)])
+    spot = jnp.stack([lax.div(head_index, 2), head_index])
+    routes = (source_view, source_block, meta)
+
+    def flip(x, bits):
+        return lax.ppermute(x, "head", [(n, n ^ bits) for n in range(group)])
+
+    def view_swap(x):
+        return lax.all_to_all(x, "view", split_axis=0, concat_axis=0, tiled=True)
+
+    def pairs_of(j, i):
+        for v in range(views):
+            for h in range(group):
+                to = (h % 2) * count + ((v % count) ^ j)
+                yield v * group + h, to * group + (h - h % 2) + ((v // count) ^ i)
+
+    def send(parts, back=False):
+        out = []
+        for part, (j, i) in zip(parts, messages(count)):
+            pairs = [(b, a) if back else (a, b) for a, b in pairs_of(j, i)]
+            out.append(lax.ppermute(part, ("view", "head"), pairs))
+        return out
+
+    full = whole(tokens, columns)
+    wide, wide_shape = whole(half, 128), shape_of(half, 128)
+    thin, thin_shape = whole(count, half // 2, 128), shape_of(count, half // 2, 128)
+    kq = call(
+        pack_kq, (meta,), (query_rows, key_rows), [full] * 2, [wide] * views, [wide_shape] * views
+    )
+    kq = send(kq)
+    v, v_give = call(pack_v, (meta,), (value_rows,), [full], [thin] * 2, [thin_shape] * 2)
+    v_got = flip(v_give, 1)
+    first = core == 0
+    og_keep = lax.dynamic_slice_in_dim(out_grad, core * half, half, 0)
+    og_give = lax.dynamic_slice_in_dim(out_grad, (1 - core) * half, half, 0)
+    og = [og_keep, flip(og_give, 1), flip(og_keep, 2), flip(og_give, 3)]
+    g = call(
+        attended_grads,
+        (spot,),
+        (*og, v, v_got, out_weight),
+        [whole(half, columns)] * group
+        + [thin] * 2
+        + [pl.BlockSpec((views * HEAD_DIM, group * columns), lambda i, s: (s[0], 0))],
+        whole(views, half, 128),
+        shape_of(views, half, 128),
+    )
+    vg = view_swap(g)
+    kq_other = [flip(x, 1) for x in kq]
+    vg_other = flip(vg, 1)
+    per_view_e = pl.BlockSpec((1, keys, half), lambda i, *_: (i, 0, 0))
+    per_view_l = pl.BlockSpec((1, 1, half), lambda i, *_: (i, 0, 0))
+    per_view = pl.BlockSpec((1, half // 2, 128), lambda i, *_: (i, 0, 0))
+    per_view_g = pl.BlockSpec((1, half // 2, 128), lambda i, *_: (i, 1, 0))
+    all_rows = whole(2, views, half, 128)
+    unit = 2 * views * keys * half * 64
+    kq_all, e, l = call(
+        scores,
+        routes,
+        (*kq, *kq_other),
+        [HBM] * (2 * views),
+        [all_rows, per_view_e, per_view_l],
+        [
+            shape_of(2, views, half, 128),
+            shape_of(views, keys, half),
+            shape_of(views, 1, half, dtype=F32),
+        ],
+        grid=(views,),
+        scratch=[
+            pltpu.VMEM((keys, 128), BF16),
+            pltpu.VMEM((keys, half), F32),
+            pltpu.SemaphoreType.DMA((2 * views,)),
+        ],
+        flops=unit * 4,
+    )
+    folded = whole(views, half // 2, 128)
+    near_far = [shape_of(views, half // 2, 128, dtype=F32), shape_of(views, half // 2, 128)]
+    kv_all, o, near_v, far_v = call(
+        attend,
+        routes,
+        (vg, vg_other, kq_all, e, l, vg),
+        [HBM] * 3 + [per_view_e, per_view_l, per_view_g],
+        [all_rows, per_view, folded, folded],
+        [shape_of(2, views, half, 128), shape_of(views, half // 2, 128), *near_far],
+        grid=(views,),
+        scratch=[
+            pltpu.VMEM((2, views, half, 128), BF16),
+            pltpu.VMEM((2, views, half // 2, 128), BF16),
+            pltpu.VMEM((128, keys), BF16),
+            pltpu.VMEM((2, half, 128), BF16),
+            pltpu.VMEM((2, views, half // 2, 128), F32),
+            pltpu.SemaphoreType.DMA((3,)),
+        ],
+        flops=unit * 3,
+    )
+    far_v = flip(far_v, 1)
+    dvo = call(
+        combine_v, (), (near_v, far_v, o), [folded] * 3, whole(views, half, 128),
+        shape_of(views, half, 128),
+    )
+    dvo = view_swap(dvo)
+    dq, near_k, far_k = call(
+        backward,
+        routes,
+        (kv_all, kq_all, e, o, l, vg),
+        [HBM, HBM, per_view_e, per_view, per_view_l, per_view_g],
+        [pl.BlockSpec((1, half, 128), lambda i, *_: (i, 0, 0)), folded, folded],
+        [shape_of(views, half, 128), *near_far],
+        grid=(views,),
+        scratch=[
+            pltpu.VMEM((2, views, half, 128), BF16),
+            pltpu.VMEM((views, half, 128), BF16),
+            pltpu.VMEM((keys, 128), BF16),
+            pltpu.VMEM((128, keys), BF16),
+            pltpu.VMEM((keys, half), BF16),
+            pltpu.VMEM((2, half, 128), BF16),
+            pltpu.VMEM((2, views, half // 2, 128), F32),
+            pltpu.SemaphoreType.DMA((2,)),
+        ],
+        flops=unit * 8,
+    )
+    far_k = flip(far_k, 1)
+    dkq = call(
+        combine_kq,
+        (meta,),
+        (near_k, far_k, dq),
+        [folded, folded, whole(views, half, 128)],
+        [wide] * views,
+        [wide_shape] * views,
+    )
+    dkq = send(dkq, back=True)
+    o_other = flip(lax.slice_in_dim(dvo, half // 2, half, axis=1), 2)
+    mixed, mixed_give = call(
+        mix,
+        (spot,),
+        (dvo, o_other, out_weight),
+        [
+            pl.BlockSpec((views, half // 2, 128), lambda i, s: (0, 1, 0)),
+            folded,
+            pl.BlockSpec((group * columns, 2 * columns), lambda i, s: (0, s[0])),
+        ],
+        [whole(half, columns)] * 2,
+        [shape_of(half, columns)] * 2,
+    )
+    mixed_got = flip(mixed_give, 1)
+    mixed_out = jnp.concatenate(
+        [jnp.where(first, mixed, mixed_got), jnp.where(first, mixed_got, mixed)], axis=0
+    )
+    give = lax.slice_in_dim(dvo, 0, half // 2, axis=1)
+    dv_got = flip(lax.dynamic_slice_in_dim(give, (1 - core) * count, count, 0), 1)
+    value_grad = call(
+        unpack_v, (meta,), (dvo, dv_got), [HBM] * 2, full, shape_of(tokens, columns),
+        scratch=[
+            pltpu.VMEM((2, count, half // 2, 128), BF16), pltpu.SemaphoreType.DMA((2,))
+        ],
+    )
+    query_grad, key_grad = call(
+        unpack_kq, (meta,), tuple(dkq), [HBM] * views, [full] * 2,
+        [shape_of(tokens, columns)] * 2,
+        scratch=[
+            pltpu.VMEM((2, count, half, 128), BF16), pltpu.SemaphoreType.DMA((views,))
+        ],
+    )
+    return mixed_out, query_grad, key_grad, value_grad
 
 
 def score_rows(query_part, key_heads, score_scale):
@@ -153,20 +698,30 @@
     return (mixed_out, query_grad, key_grad, value_grad)
 
 
+def planes(*args):
+    return plane_body(*args)
+
+
 def solution(mesh):
-    placed = (
-        P("view", "head"),
-        P("view", "head"),
-        P("view", "head"),
-        P(),
-        P("view", "head"),
-        P(),
-        P(),
-    )
-    return jax.shard_map(
-        body,
-        mesh=mesh,
-        in_specs=placed,
-        out_specs=(P("view", "head"), P("view", "head"), P("view", "head"), P("view", "head")),
-        check_vma=False,
-    )
+    placed = P("view", "head")
+    views, group = mesh.shape["view"], mesh.shape["head"]
+
+    def step(*args):
+        tokens, columns = args[0].shape
+        count = columns // group // HEAD_DIM
+        fits = (
+            group == 4
+            and views == 2 * count
+            and count & (count - 1) == 0
+            and tokens // views % (4 * BLOCK_TOKENS) == 0
+        )
+        inner = jax.shard_map(
+            planes if fits else body,
+            mesh=mesh,
+            in_specs=(placed, placed, placed, P(), placed, P(), P()),
+            out_specs=(placed,) * 4,
+            check_vma=False,
+        )
+        return inner(*args)
+
+    return step

time: 370 us -> 207 us (0.56)
  waiting for transfers between devices: 168 us -> 41.2 us
  Pallas kernels: 0 us -> 80.9 us
  matrix products: 79.5 us -> 0 us
  local copies, waits for them, and re-layouts: 66.8 us -> 7.62 us
  blocking collectives: 0 us -> 32.6 us
  starting transfers between devices: 11.9 us -> 40.4 us
  other arithmetic: 27.8 us -> 2.06 us
  between operations: 14.3 us -> 1.03 us
    all_to_all x2 -> x1, waiting for transfers between devices: 117 us -> 6.73 us  [view_swap(): return lax.all_to_all(x, 'view', split_axis=0, concat_axis=0, tiled=True)]
    pallas_call x0 -> x11, Pallas kernels: none -> 80.9 us  [call(): pl.pallas_call(kernel, grid_spec=pltpu.PrefetchScalarGridSpec(num_scalar_...]
    dot_general x18 -> x0, matrix products: 79.5 us -> none  [the longest x4 17.7 us: score_rows(): jnp.einsum('qhd,khd->hqk', query_part, key_heads, preferred_element_type=...]
    ppermute x0 -> x34, starting transfers between devices: none -> 35.9 us  [the longest x16 23.3 us: send(): out.append(lax.ppermute(part, ('view', 'head'), pairs))]
    ppermute x0 -> x34, waiting for transfers between devices: none -> 34.5 us  [the longest x16 22.4 us: send(): out.append(lax.ppermute(part, ('view', 'head'), pairs))]
    all_to_all x0 -> x1, blocking collectives: none -> 32.6 us  [view_swap(): return lax.all_to_all(x, 'view', split_axis=0, concat_axis=0, tiled=True)]
    reduce_scatter x1 -> x0, waiting for transfers between devices: 29.2 us -> none  [body(): lax.psum_scatter(lax.dot_general(part_weight, attended_rows, (((0,), (1,)...]
    all_gather x1 -> x0, waiting for transfers between devices: 21.1 us -> none  [body(): lax.all_gather(out_grad, 'head', axis=1, tiled=True)]
  transfers between devices with their start and end apart: 4 -> 35, of which waited for: 4 -> 15; matrix products, arithmetic and copies ran while one was open for 5% -> 1% of each run, Pallas kernels for 0% -> 27%
where the time goes in v2:
time: 207 us; the launch traced here: 206 us
  Pallas kernels  80.9 us (39%)
  waiting for transfers between devices  41.2 us (20%)
  starting transfers between devices  40.4 us (20%)
  blocking collectives  32.6 us (16%)
  local copies, waits for them, and re-layouts  7.62 us (4%)
    pallas_call x11, Pallas kernels, call(): pl.pallas_call(kernel, grid_spec=pltpu.PrefetchScalarGridSpec(num_scalar_...  80.9 us
    all_to_all x1, blocking collectives, view_swap(): return lax.all_to_all(x, 'view', split_axis=0, concat_axis=0, tiled=True)  32.6 us
    ppermute x16, starting transfers between devices, send(): out.append(lax.ppermute(part, ('view', 'head'), pairs))  23.3 us
    ppermute x16, waiting for transfers between devices, send(): out.append(lax.ppermute(part, ('view', 'head'), pairs))  22.4 us
    ppermute x18, starting transfers between devices, flip(): return lax.ppermute(x, 'head', [(n, n ^ bits) for n in range(group)])  12.6 us
    ppermute x18, waiting for transfers between devices, flip(): return lax.ppermute(x, 'head', [(n, n ^ bits) for n in range(group)])  12.1 us
    all_to_all x1, waiting for transfers between devices, view_swap(): return lax.all_to_all(x, 'view', split_axis=0, concat_axis=0, tiled=True)  6.73 us
    unnamed x78, local copies, waits for them, and re-layouts  6.44 us
  transfers between devices with their start and end apart: 35, of which 15 were waited for; matrix products, arithmetic and copies ran while one was open for 1% of the time, Pallas kernels for 27%

profile of v2, /device:TPU:0, one launch (start us, length us, event | category | flops | bytes accessed | tf_op | source)
XLA Modules:
  0.0 205.7 jit_solution(12212919804345787134)
XLA Ops:
  1.7 2.5 %collective-permute-start.2 = (bf16[512,256]{1,0:T(8,128)(2,1)S(1)}, bf16[512,256]{1,0:T(8,128)(2,1)S(1)}, u32[]{:S(2)}, u32[]{:S(2)}) collective-permute-start(bf16[512,256]{1,0:T(8,128)(2,1)S(1)} %get-tuple-element.72), channel_id=1, source_target_pairs={{0,3},{1,2},{2,1},{3,0},{4,7},{5,6},{6,5},{7,4},{8,11},{9,10},{10,... | collective-permute-start | bytes 786440 | tf_op jit(solution)/shard_map/ppermute | solution.py:395
  5.5 2.6 %shard_map.102 = (bf16[4,256,128]{2,1,0:T(8,128)(2,1)}, bf16[4,256,128]{2,1,0:T(8,128)(2,1)}) custom-call(s32[3]{0:T(128)} %pad_add_fusion.1.meta_ref, bf16[1024,256]{1,0:T(8,128)(2,1)} %v_ref.1), custom_call_target="tpu_custom_call" | custom-call | tf_op jit(solution)/shard_map/pallas_call | solution.py:34
  8.9 2.0 collective-permute-done.2.refs_3_
  10.9 5.8 %collective-permute-done.1.refs_2_ = bf16[512,256]{1,0:T(8,128)(2,1)S(1)} collective-permute-done((bf16[512,256]{1,0:T(8,128)(2,1)S(1)}, bf16[512,256]{1,0:T(8,128)(2,1)S(1)}, u32[]{:S(2)}, u32[]{:S(2)}) %collective-permute-start.1) | collective-permute-done | bytes 262176 | tf_op jit(solution)/shard_map/ppermute | solution.py:395
  17.5 4.2 %shard_map.103 = bf16[8,512,128]{2,1,0:T(8,128)(2,1)} custom-call(s32[2]{0:T(128)} %pad_add_fusion.place_ref, bf16[512,256]{1,0:T(8,128)(2,1)} %copy-done.3, bf16[512,256]{1,0:T(8,128)(2,1)} %copy-done.8, bf16[512,256]{1,0:T(8,128)(2,1)} %copy-done.9, bf16[512,256]{1,0:T(8,128)(2,1)} %copy-done.7, bf16[4,256,128]{2,1,0:T(8,128)(2,1)} %get-tuple-element.36.refs_4_, ...), custom_call_target="tpu_custom_call" | custom-call | tf_op jit(solution)/shard_map/pallas_call | solution.py:34
  21.7 32.6 %all_to_all.10.refs_0_.refs_5_.g_ref = bf16[8,512,128]{2,1,0:T(8,128)(2,1)S(1)} all-to-all(bf16[8,512,128]{2,1,0:T(8,128)(2,1)} %shard_map.103), channel_id=1, replica_groups=mesh['view'=8,'head'=4] {'view'}, dimensions={0} | all-to-all | bytes 2097152 | tf_op jit(solution)/shard_map/all_to_all | solution.py:398
  54.3 3.3 %shard_map.104 = (bf16[512,128]{1,0:T(8,128)(2,1)}, bf16[512,128]{1,0:T(8,128)(2,1)}, bf16[512,128]{1,0:T(8,128)(2,1)}, bf16[512,128]{1,0:T(8,128)(2,1)}, bf16[5...) custom-call(s32[3]{0:T(128)} %pad_add_fusion.1.meta_ref, ...), custom_call_target="tpu_custom_call" | custom-call | tf_op jit(solution)/shard_map/pallas_call | solution.py:34
  59.1 1.6 collective-permute-start.6
  61.5 2.3 %collective-permute-start.8 = (bf16[512,128]{1,0:T(8,128)(2,1)}, bf16[512,128]{1,0:T(8,128)(2,1)S(1)}, u32[]{:S(2)}, u32[]{:S(2)}) collective-permute-start(bf16[512,128]{1,0:T(8,128)(2,1)} %get-tuple-element.41), channel_id=1, source_target_pairs={{0,5},{1,21},{2,7},{3,23},{4,1},{5,17},{6,3},{7,19},{8,13},{9,29},... | collective-permute-start | bytes 393224 | tf_op jit(solution)/shard_map/ppermute | solution.py:410
  64.9 7.7 %collective-permute-done.6.refs_1_ = bf16[512,128]{1,0:T(8,128)(2,1)S(1)} collective-permute-done((bf16[512,128]{1,0:T(8,128)(2,1)}, bf16[512,128]{1,0:T(8,128)(2,1)S(1)}, u32[]{:S(2)}, u32[]{:S(2)}) %collective-permute-start.6) | collective-permute-done | bytes 131104 | tf_op jit(solution)/shard_map/ppermute | solution.py:410
  72.7 1.8 collective-permute-start.11
  74.5 2.0 collective-permute-done.8.refs_3_
  76.9 3.8 %collective-permute-done.10.refs_5_ = bf16[512,128]{1,0:T(8,128)(2,1)S(1)} collective-permute-done((bf16[512,128]{1,0:T(8,128)(2,1)}, bf16[512,128]{1,0:T(8,128)(2,1)S(1)}, u32[]{:S(2)}, u32[]{:S(2)}) %collective-permute-start.10) | collective-permute-done | bytes 131104 | tf_op jit(solution)/shard_map/ppermute | solution.py:410
  81.3 2.1 %collective-permute-start.15 = (bf16[512,128]{1,0:T(8,128)(2,1)S(1)}, bf16[512,128]{1,0:T(8,128)(2,1)S(1)}, u32[]{:S(2)}, u32[]{:S(2)}) collective-permute-start(bf16[512,128]{1,0:T(8,128)(2,1)S(1)} %collective-permute-done.7.refs_2_), channel_id=1, source_target_pairs={{0,1},{1,0},{2,3},{3,2},{4,5},{5,4},{6,7},{7,6},{8,9},{9,8},{10,11... | collective-permute-start | bytes 393224 | tf_op jit(solution)/shard_map/ppermute | solution.py:395
  88.3 17.8 %shard_map.105 = (bf16[2,8,512,128]{3,2,1,0:T(8,128)(2,1)}, bf16[8,2048,512]{2,1,0:T(8,128)(2,1)}, f32[8,1,512]{2,1,0:T(1,128)}) custom-call(s32[8,16]{1,0:T(8,128)} %sv_ref.5, s32[8,16]{1,0:T(8,128)} %sb_ref.5, s32[3]{0:T(128)} %pad_add_fusion.1.meta_ref, bf16[512,128]{1,0:T(8,128)(2,1)} %copy-done.21, bf16[512,128]{1,0:T(8,128)(2,1)} %copy-done.22, ...), custom_call_target="tpu_custom_call" | custom-call | flops 4294967296 | tf_op jit(solution)/shard_map/pallas_call | solution.py:34
  107.2 17.8 %shard_map.106 = (bf16[2,8,512,128]{3,2,1,0:T(8,128)(2,1)}, bf16[8,256,128]{2,1,0:T(8,128)(2,1)}, f32[8,256,128]{2,1,0:T(8,128)}, bf16[8,256,128]{2,1,0:T(8,128)(2,1)}) custom-call(s32[8,16]{1,0:T(8,128)} %sv_ref.5, s32[8,16]{1,0:T(8,128)} %sb_ref.5, s32[3]{0:T(128)} %pad_add_fusion.1.meta_ref, bf16[8,512,128]{2,1,0:T(8,128)(2,1)} %copy-done.1, ...), custom_call_target="tpu_custom_call" | custom-call | flops 3221225472 | tf_op jit(solution)/shard_map/pallas_call | solution.py:34
  125.3 1.8 collective-permute-done.21.far_ref
  127.9 2.7 %shard_map.107 = bf16[8,512,128]{2,1,0:T(8,128)(2,1)} custom-call(f32[8,256,128]{2,1,0:T(8,128)} %get-tuple-element.49.near_ref, bf16[8,256,128]{2,1,0:T(8,128)(2,1)} %copy-done.6, bf16[8,256,128]{2,1,0:T(8,128)(2,1)} %get-tuple-element.51.o_ref), custom_call_target="tpu_custom_call" | custom-call | tf_op jit(solution)/shard_map/pallas_call | solution.py:34
  130.6 4.4 %all-to-all-start.1 = ((bf16[8,512,128]{2,1,0:T(8,128)(2,1)}), bf16[8,512,128]{2,1,0:T(8,128)(2,1)S(1)}, u32[]{:S(2)}, u32[]{:S(2)}) async-start(bf16[8,512,128]{2,1,0:T(8,128)(2,1)} %shard_map.107), calls=%async_computation.1 | async-start | bytes 2097152 | tf_op jit(solution)/shard_map/all_to_all | solution.py:398
  135.1 19.3 %shard_map.109 = (bf16[8,512,128]{2,1,0:T(8,128)(2,1)}, f32[8,256,128]{2,1,0:T(8,128)}, bf16[8,256,128]{2,1,0:T(8,128)(2,1)}) custom-call(s32[8,16]{1,0:T(8,128)} %sv_ref.5, s32[8,16]{1,0:T(8,128)} %sb_ref.5, s32[3]{0:T(128)} %pad_add_fusion.1.meta_ref, bf16[2,8,512,128]{3,2,1,0:T(8,128)(2,1)} %get-tuple-element.54.kv_ref, ...), custom_call_target="tpu_custom_call" | custom-call | flops 8589934592 | tf_op jit(solution)/shard_map/pallas_call | solution.py:34
  154.5 6.7 %all-to-all-done.1.own_ref.all_ref = bf16[8,512,128]{2,1,0:T(8,128)(2,1)S(1)} async-done(((bf16[8,512,128]{2,1,0:T(8,128)(2,1)}), bf16[8,512,128]{2,1,0:T(8,128)(2,1)S(1)}, u32[]{:S(2)}, u32[]{:S(2)}) %all-to-all-start.1) | async-done | bytes 1048608 | tf_op jit(solution)/shard_map/all_to_all | solution.py:398
  161.3 1.6 collective-permute-start.22
  163.7 3.4 %shard_map.110 = (bf16[512,128]{1,0:T(8,128)(2,1)}, bf16[512,128]{1,0:T(8,128)(2,1)}, bf16[512,128]{1,0:T(8,128)(2,1)}, bf16[512,128]{1,0:T(8,128)(2,1)}, bf16[5...) custom-call(s32[3]{0:T(128)} %pad_add_fusion.1.meta_ref, ...), custom_call_target="tpu_custom_call" | custom-call | tf_op jit(solution)/shard_map/pallas_call | solution.py:34
  168.7 1.8 collective-permute-start.26
  172.6 1.6 collective-permute-done.22.other_ref
  175.1 3.8 %shard_map.108 = (bf16[512,256]{1,0:T(8,128)(2,1)}, bf16[512,256]{1,0:T(8,128)(2,1)}) custom-call(s32[2]{0:T(128)} %pad_add_fusion.place_ref, bf16[8,512,128]{2,1,0:T(8,128)(2,1)} %copy-done, bf16[8,256,128]{2,1,0:T(8,128)(2,1)} %copy-done.4, bf16[1024,1024]{1,0:T(8,128)(2,1)} %w_ref.1), custom_call_target="tpu_custom_call" | custom-call | tf_op jit(solution)/shard_map/pallas_call | solution.py:34
  178.9 2.4 %collective-permute-start.33 = (bf16[4,256,128]{2,1,0:T(8,128)(2,1)S(1)}, bf16[4,256,128]{2,1,0:T(8,128)(2,1)S(1)}, u32[]{:S(2)}, u32[]{:S(2)}) collective-permute-start(bf16[4,256,128]{2,1,0:T(8,128)(2,1)S(1)} %constant_dynamic-slice_fusion), channel_id=1, source_target_pairs={{0,1},{1,0},{2,3},{3,2},{4,5},{5,4},{6,7},{7,6},{8,9},{9,8},{10,11... | collective-permute-start | bytes 786440 | tf_op jit(solution)/shard_map/ppermute | solution.py:395
  182.3 4.6 %collective-permute-start.30 = (bf16[512,128]{1,0:T(8,128)(2,1)S(1)}, bf16[512,128]{1,0:T(8,128)(2,1)S(1)}, u32[]{:S(2)}, u32[]{:S(2)}) collective-permute-start(bf16[512,128]{1,0:T(8,128)(2,1)S(1)} %copy-done.29), channel_id=1, source_target_pairs={{9,0},{25,1},{11,2},{27,3},{13,4},{29,5},{15,6},{31,7},{1,8},{17,9... | collective-permute-start | bytes 393224 | tf_op jit(solution)/shard_map/ppermute | solution.py:410
  187.0 3.1 %collective-permute-start.32 = (bf16[512,128]{1,0:T(8,128)(2,1)S(1)}, bf16[512,128]{1,0:T(8,128)(2,1)S(1)}, u32[]{:S(2)}, u32[]{:S(2)}) collective-permute-start(bf16[512,128]{1,0:T(8,128)(2,1)S(1)} %copy-done.27), channel_id=1, source_target_pairs={{13,0},{29,1},{15,2},{31,3},{9,4},{25,5},{11,6},{27,7},{5,8},{21,9... | collective-permute-start | bytes 393224 | tf_op jit(solution)/shard_map/ppermute | solution.py:410
  190.7 6.1 %collective-permute-done.31.refs_6_ = bf16[512,128]{1,0:T(8,128)(2,1)S(1)} collective-permute-done((bf16[512,128]{1,0:T(8,128)(2,1)S(1)}, bf16[512,128]{1,0:T(8,128)(2,1)S(1)}, u32[]{:S(2)}, u32[]{:S(2)}) %collective-permute-start.31) | collective-permute-done | bytes 131104 | tf_op jit(solution)/shard_map/ppermute | solution.py:410
  198.1 3.3 %shard_map.111 = (bf16[1024,256]{1,0:T(8,128)(2,1)}, bf16[1024,256]{1,0:T(8,128)(2,1)}) custom-call(s32[3]{0:T(128)} %pad_add_fusion.1.meta_ref, bf16[512,128]{1,0:T(8,128)(2,1)} %copy-done.13, bf16[512,128]{1,0:T(8,128)(2,1)} %copy-done.14, bf16[512,128]{1,0:T(8,128)(2,1)} %copy-done.15, bf16[512,128]{1,0:T(8,128)(2,1)} %copy-done.16, ...), custom_call_target="tpu_custom_call" | custom-call | tf_op jit(solution)/shard_map/pallas_call | solution.py:34
  202.1 2.7 %shard_map.112 = bf16[1024,256]{1,0:T(8,128)(2,1)} custom-call(s32[3]{0:T(128)} %pad_add_fusion.1.meta_ref, bf16[8,512,128]{2,1,0:T(8,128)(2,1)} %copy-done, bf16[4,256,128]{2,1,0:T(8,128)(2,1)} %copy-done.12), custom_call_target="tpu_custom_call" | custom-call | tf_op jit(solution)/shard_map/pallas_call | solution.py:34
  (135 shorter events, 25.4 us)
Async XLA Ops:
  1.7 9.2 %collective-permute-start.2 = (bf16[512,256]{1,0:T(8,128)(2,1)S(1)}, bf16[512,256]{1,0:T(8,128)(2,1)S(1)}, u32[]{:S(2)}, u32[]{:S(2)}) collective-permute-start(bf16[512,256]{1,0:T(8,128)(2,1)S(1)} %get-tuple-element.72), channel_id=1, source_target_pairs={{0,3},{1,2},{2,1},{3,0},{4,7},{5,6},{6,5},{7,4},{8,11},{9,10},{10,... | collective-permute-start | bytes 786440 | tf_op jit(solution)/shard_map/ppermute | solution.py:395
  4.2 6.7 %collective-permute-start = (bf16[512,256]{1,0:T(8,128)(2,1)S(1)}, bf16[512,256]{1,0:T(8,128)(2,1)S(1)}, u32[]{:S(2)}, u32[]{:S(2)}) collective-permute-start(bf16[512,256]{1,0:T(8,128)(2,1)S(1)} %get-tuple-element.72), channel_id=1, source_target_pairs={{0,1},{1,0},{2,3},{3,2},{4,5},{5,4},{6,7},{7,6},{8,9},{9,8},{10,11... | collective-permute-start | bytes 786440 | tf_op jit(solution)/shard_map/ppermute | solution.py:395
  4.9 11.8 %collective-permute-start.1 = (bf16[512,256]{1,0:T(8,128)(2,1)S(1)}, bf16[512,256]{1,0:T(8,128)(2,1)S(1)}, u32[]{:S(2)}, u32[]{:S(2)}) collective-permute-start(bf16[512,256]{1,0:T(8,128)(2,1)S(1)} %get-tuple-element.73.refs_0_), channel_id=1, source_target_pairs={{0,2},{1,3},{2,0},{3,1},{4,6},{5,7},{6,4},{7,5},{8,10},{9,11},{10,... | collective-permute-start | bytes 786440 | tf_op jit(solution)/shard_map/ppermute | solution.py:395
  8.2 8.5 %collective-permute-start.3 = (bf16[4,256,128]{2,1,0:T(8,128)(2,1)}, bf16[4,256,128]{2,1,0:T(8,128)(2,1)S(1)}, u32[]{:S(2)}, u32[]{:S(2)}) collective-permute-start(bf16[4,256,128]{2,1,0:T(8,128)(2,1)} %get-tuple-element.37), channel_id=1, source_target_pairs={{0,1},{1,0},{2,3},{3,2},{4,5},{5,4},{6,7},{7,6},{8,9},{9,8},{10,11... | collective-permute-start | bytes 786440 | tf_op jit(solution)/shard_map/ppermute | solution.py:395
  54.3 51.9 %collective-permute-start.4 = (bf16[8,512,128]{2,1,0:T(8,128)(2,1)S(1)}, bf16[8,512,128]{2,1,0:T(8,128)(2,1)S(1)}, u32[]{:S(2)}, u32[]{:S(2)}) collective-permute-start(bf16[8,512,128]{2,1,0:T(8,128)(2,1)S(1)} %all_to_all.10.refs_0_.refs_5_.g_ref), channel_id=1, source_target_pairs={{0,1},{1,0},{2,3},{3,2},{4,5},{5,4},{6,7},{7,6},{8,9},{9,8},{10,11... | collective-permute-start | bytes 3145736 | tf_op jit(solution)/shard_map/ppermute | solution.py:395
  57.5 6.3 %collective-permute-start.5 = (bf16[512,128]{1,0:T(8,128)(2,1)}, bf16[512,128]{1,0:T(8,128)(2,1)S(1)}, u32[]{:S(2)}, u32[]{:S(2)}) collective-permute-start(bf16[512,128]{1,0:T(8,128)(2,1)} %get-tuple-element.38), channel_id=1, source_target_pairs={{0,0},{1,16},{2,2},{3,18},{4,4},{5,20},{6,6},{7,22},{8,8},{9,24},{... | collective-permute-start | bytes 393224 | tf_op jit(solution)/shard_map/ppermute | solution.py:410
  59.1 13.5 %collective-permute-start.6 = (bf16[512,128]{1,0:T(8,128)(2,1)}, bf16[512,128]{1,0:T(8,128)(2,1)S(1)}, u32[]{:S(2)}, u32[]{:S(2)}) collective-permute-start(bf16[512,128]{1,0:T(8,128)(2,1)} %get-tuple-element.39), channel_id=1, source_target_pairs={{0,1},{1,17},{2,3},{3,19},{4,5},{5,21},{6,7},{7,23},{8,9},{9,25},{... | collective-permute-start | bytes 393224 | tf_op jit(solution)/shard_map/ppermute | solution.py:410
  60.7 11.9 %collective-permute-start.7 = (bf16[512,128]{1,0:T(8,128)(2,1)}, bf16[512,128]{1,0:T(8,128)(2,1)S(1)}, u32[]{:S(2)}, u32[]{:S(2)}) collective-permute-start(bf16[512,128]{1,0:T(8,128)(2,1)} %get-tuple-element.40), channel_id=1, source_target_pairs={{0,4},{1,20},{2,6},{3,22},{4,0},{5,16},{6,2},{7,18},{8,12},{9,28},... | collective-permute-start | bytes 393224 | tf_op jit(solution)/shard_map/ppermute | solution.py:410
  61.5 15.0 %collective-permute-start.8 = (bf16[512,128]{1,0:T(8,128)(2,1)}, bf16[512,128]{1,0:T(8,128)(2,1)S(1)}, u32[]{:S(2)}, u32[]{:S(2)}) collective-permute-start(bf16[512,128]{1,0:T(8,128)(2,1)} %get-tuple-element.41), channel_id=1, source_target_pairs={{0,5},{1,21},{2,7},{3,23},{4,1},{5,17},{6,3},{7,19},{8,13},{9,29},... | collective-permute-start | bytes 393224 | tf_op jit(solution)/shard_map/ppermute | solution.py:410
  63.8 12.7 %collective-permute-start.9 = (bf16[512,128]{1,0:T(8,128)(2,1)}, bf16[512,128]{1,0:T(8,128)(2,1)S(1)}, u32[]{:S(2)}, u32[]{:S(2)}) collective-permute-start(bf16[512,128]{1,0:T(8,128)(2,1)} %get-tuple-element.42), channel_id=1, source_target_pairs={{0,8},{1,24},{2,10},{3,26},{4,12},{5,28},{6,14},{7,30},{8,0},{9,16... | collective-permute-start | bytes 393224 | tf_op jit(solution)/shard_map/ppermute | solution.py:410
  72.6 8.0 %collective-permute-start.10 = (bf16[512,128]{1,0:T(8,128)(2,1)}, bf16[512,128]{1,0:T(8,128)(2,1)S(1)}, u32[]{:S(2)}, u32[]{:S(2)}) collective-permute-start(bf16[512,128]{1,0:T(8,128)(2,1)} %get-tuple-element.43), channel_id=1, source_target_pairs={{0,9},{1,25},{2,11},{3,27},{4,13},{5,29},{6,15},{7,31},{8,1},{9,17... | collective-permute-start | bytes 393224 | tf_op jit(solution)/shard_map/ppermute | solution.py:410
  72.7 8.6 %collective-permute-start.11 = (bf16[512,128]{1,0:T(8,128)(2,1)}, bf16[512,128]{1,0:T(8,128)(2,1)S(1)}, u32[]{:S(2)}, u32[]{:S(2)}) collective-permute-start(bf16[512,128]{1,0:T(8,128)(2,1)} %get-tuple-element.44), channel_id=1, source_target_pairs={{0,12},{1,28},{2,14},{3,30},{4,8},{5,24},{6,10},{7,26},{8,4},{9,20... | collective-permute-start | bytes 393224 | tf_op jit(solution)/shard_map/ppermute | solution.py:410
  76.5 8.5 %collective-permute-start.12 = (bf16[512,128]{1,0:T(8,128)(2,1)}, bf16[512,128]{1,0:T(8,128)(2,1)S(1)}, u32[]{:S(2)}, u32[]{:S(2)}) collective-permute-start(bf16[512,128]{1,0:T(8,128)(2,1)} %get-tuple-element.45), channel_id=1, source_target_pairs={{0,13},{1,29},{2,15},{3,31},{4,9},{5,25},{6,11},{7,27},{8,5},{9,21... | collective-permute-start | bytes 393224 | tf_op jit(solution)/shard_map/ppermute | solution.py:410
  76.5 8.8 %collective-permute-start.13 = (bf16[512,128]{1,0:T(8,128)(2,1)S(1)}, bf16[512,128]{1,0:T(8,128)(2,1)S(1)}, u32[]{:S(2)}, u32[]{:S(2)}) collective-permute-start(bf16[512,128]{1,0:T(8,128)(2,1)S(1)} %collective-permute-done.5.refs_0_), channel_id=1, source_target_pairs={{0,1},{1,0},{2,3},{3,2},{4,5},{5,4},{6,7},{7,6},{8,9},{9,8},{10,11... | collective-permute-start | bytes 393224 | tf_op jit(solution)/shard_map/ppermute | solution.py:395
  80.6 4.9 %collective-permute-start.14 = (bf16[512,128]{1,0:T(8,128)(2,1)S(1)}, bf16[512,128]{1,0:T(8,128)(2,1)S(1)}, u32[]{:S(2)}, u32[]{:S(2)}) collective-permute-start(bf16[512,128]{1,0:T(8,128)(2,1)S(1)} %collective-permute-done.6.refs_1_), channel_id=1, source_target_pairs={{0,1},{1,0},{2,3},{3,2},{4,5},{5,4},{6,7},{7,6},{8,9},{9,8},{10,11... | collective-permute-start | bytes 393224 | tf_op jit(solution)/shard_map/ppermute | solution.py:395
  81.3 4.5 %collective-permute-start.15 = (bf16[512,128]{1,0:T(8,128)(2,1)S(1)}, bf16[512,128]{1,0:T(8,128)(2,1)S(1)}, u32[]{:S(2)}, u32[]{:S(2)}) collective-permute-start(bf16[512,128]{1,0:T(8,128)(2,1)S(1)} %collective-permute-done.7.refs_2_), channel_id=1, source_target_pairs={{0,1},{1,0},{2,3},{3,2},{4,5},{5,4},{6,7},{7,6},{8,9},{9,8},{10,11... | collective-permute-start | bytes 393224 | tf_op jit(solution)/shard_map/ppermute | solution.py:395
  85.3 1.3 collective-permute-start.17
  86.4 1.8 collective-permute-start.20
  125.0 2.2 %collective-permute-start.21 = (bf16[8,256,128]{2,1,0:T(8,128)(2,1)}, bf16[8,256,128]{2,1,0:T(8,128)(2,1)S(1)}, u32[]{:S(2)}, u32[]{:S(2)}) collective-permute-start(bf16[8,256,128]{2,1,0:T(8,128)(2,1)} %get-tuple-element.50), channel_id=1, source_target_pairs={{0,1},{1,0},{2,3},{3,2},{4,5},{5,4},{6,7},{7,6},{8,9},{9,8},{10,11... | collective-permute-start | bytes 1572872 | tf_op jit(solution)/shard_map/ppermute | solution.py:395
  130.6 30.6 %all-to-all-start.1 = ((bf16[8,512,128]{2,1,0:T(8,128)(2,1)}), bf16[8,512,128]{2,1,0:T(8,128)(2,1)S(1)}, u32[]{:S(2)}, u32[]{:S(2)}) async-start(bf16[8,512,128]{2,1,0:T(8,128)(2,1)} %shard_map.107), calls=%async_computation.1 | async-start | bytes 2097152 | tf_op jit(solution)/shard_map/all_to_all | solution.py:398
  154.4 8.5 %collective-permute-start.24 = (bf16[8,256,128]{2,1,0:T(8,128)(2,1)}, bf16[8,256,128]{2,1,0:T(8,128)(2,1)S(1)}, u32[]{:S(2)}, u32[]{:S(2)}) collective-permute-start(bf16[8,256,128]{2,1,0:T(8,128)(2,1)} %get-tuple-element.56), channel_id=1, source_target_pairs={{0,1},{1,0},{2,3},{3,2},{4,5},{5,4},{6,7},{7,6},{8,9},{9,8},{10,11... | collective-permute-start | bytes 1572872 | tf_op jit(solution)/shard_map/ppermute | solution.py:395
  161.3 13.0 %collective-permute-start.22 = (bf16[8,256,128]{2,1,0:T(8,128)(2,1)S(1)}, bf16[8,256,128]{2,1,0:T(8,128)(2,1)S(1)}, u32[]{:S(2)}, u32[]{:S(2)}) collective-permute-start(bf16[8,256,128]{2,1,0:T(8,128)(2,1)S(1)} %get-tuple-element.69), channel_id=1, source_target_pairs={{0,2},{1,3},{2,0},{3,1},{4,6},{5,7},{6,4},{7,5},{8,10},{9,11},{10,... | collective-permute-start | bytes 1572872 | tf_op jit(solution)/shard_map/ppermute | solution.py:395
  167.1 11.7 %collective-permute-start.25 = (bf16[512,128]{1,0:T(8,128)(2,1)}, bf16[512,128]{1,0:T(8,128)(2,1)S(1)}, u32[]{:S(2)}, u32[]{:S(2)}) collective-permute-start(bf16[512,128]{1,0:T(8,128)(2,1)} %get-tuple-element.58), channel_id=1, source_target_pairs={{0,0},{16,1},{2,2},{18,3},{4,4},{20,5},{6,6},{22,7},{8,8},{24,9},{... | collective-permute-start | bytes 393224 | tf_op jit(solution)/shard_map/ppermute | solution.py:410
  168.7 12.6 %collective-permute-start.26 = (bf16[512,128]{1,0:T(8,128)(2,1)}, bf16[512,128]{1,0:T(8,128)(2,1)S(1)}, u32[]{:S(2)}, u32[]{:S(2)}) collective-permute-start(bf16[512,128]{1,0:T(8,128)(2,1)} %get-tuple-element.59), channel_id=1, source_target_pairs={{1,0},{17,1},{3,2},{19,3},{5,4},{21,5},{7,6},{23,7},{9,8},{25,9},{... | collective-permute-start | bytes 393224 | tf_op jit(solution)/shard_map/ppermute | solution.py:410
  170.4 11.9 %collective-permute-start.27 = (bf16[512,128]{1,0:T(8,128)(2,1)}, bf16[512,128]{1,0:T(8,128)(2,1)S(1)}, u32[]{:S(2)}, u32[]{:S(2)}) collective-permute-start(bf16[512,128]{1,0:T(8,128)(2,1)} %get-tuple-element.60), channel_id=1, source_target_pairs={{4,0},{20,1},{6,2},{22,3},{0,4},{16,5},{2,6},{18,7},{12,8},{28,9},... | collective-permute-start | bytes 393224 | tf_op jit(solution)/shard_map/ppermute | solution.py:410
  171.9 15.1 %collective-permute-start.28 = (bf16[512,128]{1,0:T(8,128)(2,1)}, bf16[512,128]{1,0:T(8,128)(2,1)S(1)}, u32[]{:S(2)}, u32[]{:S(2)}) collective-permute-start(bf16[512,128]{1,0:T(8,128)(2,1)} %get-tuple-element.61), channel_id=1, source_target_pairs={{5,0},{21,1},{7,2},{23,3},{1,4},{17,5},{3,6},{19,7},{13,8},{29,9},... | collective-permute-start | bytes 393224 | tf_op jit(solution)/shard_map/ppermute | solution.py:410
  174.3 12.7 %collective-permute-start.29 = (bf16[512,128]{1,0:T(8,128)(2,1)}, bf16[512,128]{1,0:T(8,128)(2,1)S(1)}, u32[]{:S(2)}, u32[]{:S(2)}) collective-permute-start(bf16[512,128]{1,0:T(8,128)(2,1)} %get-tuple-element.62), channel_id=1, source_target_pairs={{8,0},{24,1},{10,2},{26,3},{12,4},{28,5},{14,6},{30,7},{0,8},{16,9... | collective-permute-start | bytes 393224 | tf_op jit(solution)/shard_map/ppermute | solution.py:410
  178.9 22.5 %collective-permute-start.33 = (bf16[4,256,128]{2,1,0:T(8,128)(2,1)S(1)}, bf16[4,256,128]{2,1,0:T(8,128)(2,1)S(1)}, u32[]{:S(2)}, u32[]{:S(2)}) collective-permute-start(bf16[4,256,128]{2,1,0:T(8,128)(2,1)S(1)} %constant_dynamic-slice_fusion), channel_id=1, source_target_pairs={{0,1},{1,0},{2,3},{3,2},{4,5},{5,4},{6,7},{7,6},{8,9},{9,8},{10,11... | collective-permute-start | bytes 786440 | tf_op jit(solution)/shard_map/ppermute | solution.py:395
  181.3 23.5 %collective-permute-start.23 = (bf16[512,256]{1,0:T(8,128)(2,1)}, bf16[512,256]{1,0:T(8,128)(2,1)S(1)}, u32[]{:S(2)}, u32[]{:S(2)}) collective-permute-start(bf16[512,256]{1,0:T(8,128)(2,1)} %get-tuple-element.53), channel_id=1, source_target_pairs={{0,1},{1,0},{2,3},{3,2},{4,5},{5,4},{6,7},{7,6},{8,9},{9,8},{10,11... | collective-permute-start | bytes 786440 | tf_op jit(solution)/shard_map/ppermute | solution.py:395
  182.3 8.4 %collective-permute-start.30 = (bf16[512,128]{1,0:T(8,128)(2,1)S(1)}, bf16[512,128]{1,0:T(8,128)(2,1)S(1)}, u32[]{:S(2)}, u32[]{:S(2)}) collective-permute-start(bf16[512,128]{1,0:T(8,128)(2,1)S(1)} %copy-done.29), channel_id=1, source_target_pairs={{9,0},{25,1},{11,2},{27,3},{13,4},{29,5},{15,6},{31,7},{1,8},{17,9... | collective-permute-start | bytes 393224 | tf_op jit(solution)/shard_map/ppermute | solution.py:410
  186.9 9.9 %collective-permute-start.31 = (bf16[512,128]{1,0:T(8,128)(2,1)S(1)}, bf16[512,128]{1,0:T(8,128)(2,1)S(1)}, u32[]{:S(2)}, u32[]{:S(2)}) collective-permute-start(bf16[512,128]{1,0:T(8,128)(2,1)S(1)} %copy-done.28), channel_id=1, source_target_pairs={{12,0},{28,1},{14,2},{30,3},{8,4},{24,5},{10,6},{26,7},{4,8},{20,9... | collective-permute-start | bytes 393224 | tf_op jit(solution)/shard_map/ppermute | solution.py:410
  187.0 9.8 %collective-permute-start.32 = (bf16[512,128]{1,0:T(8,128)(2,1)S(1)}, bf16[512,128]{1,0:T(8,128)(2,1)S(1)}, u32[]{:S(2)}, u32[]{:S(2)}) collective-permute-start(bf16[512,128]{1,0:T(8,128)(2,1)S(1)} %copy-done.27), channel_id=1, source_target_pairs={{13,0},{29,1},{15,2},{31,3},{9,4},{25,5},{11,6},{27,7},{5,8},{21,9... | collective-permute-start | bytes 393224 | tf_op jit(solution)/shard_map/ppermute | solution.py:410
  (42 other events, 341.5 us)

commit v3 on v0

--- a/solution.py
+++ b/solution.py
@@ -1,10 +1,474 @@
 import jax
 import jax.numpy as jnp
 from jax import lax
+from jax.experimental import pallas as pl
+from jax.experimental.pallas import tpu as pltpu
 from jax.sharding import PartitionSpec as P
+
 
 HEAD_DIM = 64
 BLOCK_TOKENS = 128
+SCALE = HEAD_DIM**-0.5
+LOG2E = 1.4426950408889634
+F32 = jnp.float32
+BF16 = jnp.bfloat16
+HBM = pl.BlockSpec(memory_space=pl.ANY)
+STEP = 256
+
+
+def join(a, b):
+    return jnp.concatenate([a[:, :HEAD_DIM], b[:, :HEAD_DIM]], axis=1)
+
+
+def join_high(a, b):
+    return jnp.concatenate([a[:, HEAD_DIM:], b[:, HEAD_DIM:]], axis=1)
+
+
+def dot(a, b):
+    return jnp.dot(a, b, preferred_element_type=F32)
+
+
+def aligned(index, size):
+    return pl.ds(pl.multiple_of(index * size, size), size)
+
+
+def call(kernel, scalars, args, in_specs, out_specs, out_shape, grid=(1,), scratch=(), flops=0):
+    return pl.pallas_call(
+        kernel,
+        grid_spec=pltpu.PrefetchScalarGridSpec(
+            num_scalar_prefetch=len(scalars),
+            grid=grid,
+            in_specs=in_specs,
+            out_specs=out_specs,
+            scratch_shapes=list(scratch),
+        ),
+        out_shape=out_shape,
+        compiler_params=pltpu.CompilerParams(dimension_semantics=("arbitrary",) * len(grid)),
+        cost_estimate=pl.CostEstimate(flops=flops, transcendentals=0, bytes_accessed=0)
+        if flops
+        else None,
+    )(*scalars, *args)
+
+
+def whole(*shape):
+    return pl.BlockSpec(shape, lambda *_: (0,) * len(shape))
+
+
+def shape_of(*shape, dtype=BF16):
+    return jax.ShapeDtypeStruct(shape, dtype)
+
+
+def run_copies(*copies):
+    for copy in copies:
+        copy.start()
+    for copy in copies:
+        copy.wait()
+
+
+def fold_all(x_ref, out_ref):
+    rows, columns = x_ref.shape
+    count = columns // HEAD_DIM
+    for head in range(0, count, 2):
+        lanes = slice(HEAD_DIM * head, HEAD_DIM * (head + 2))
+        top, low = x_ref[: rows // 2, lanes], x_ref[rows // 2 :, lanes]
+        for n in range(head, out_ref.shape[0], count):
+            out_ref[n] = join(top, low)
+            out_ref[n + 1] = join_high(top, low)
+
+
+def fold_each(meta_ref, x_ref, outs):
+    rows = x_ref.shape[0]
+    for n, out in enumerate(outs):
+        head = meta_ref[0] ^ n
+        pair = aligned(head // 2, 128)
+        top, low = x_ref[: rows // 2, pair], x_ref[rows // 2 :, pair]
+        out[...] = jnp.where(head % 2 == 1, join_high(top, low), join(top, low))
+
+
+def pack_k(x_ref, out_ref):
+    fold_all(x_ref, out_ref)
+
+
+def pack_v(x_ref, out_ref):
+    fold_all(x_ref, out_ref)
+
+
+def pack_q(meta_ref, x_ref, *outs):
+    fold_each(meta_ref, x_ref, outs)
+
+
+def spread(parts, out_ref):
+    rows = out_ref.shape[0] // 2
+    for head in range(0, len(parts), 2):
+        lanes = slice(HEAD_DIM * head, HEAD_DIM * (head + 2))
+        out_ref[:rows, lanes] = join(parts[head], parts[head + 1])
+        out_ref[rows:, lanes] = join_high(parts[head], parts[head + 1])
+
+
+def collect(meta_ref, *refs):
+    parts, (out_ref, scr, sem) = refs[:-3], refs[-3:]
+    run_copies(
+        *(
+            pltpu.make_async_copy(part, scr.at[meta_ref[0] ^ n], sem.at[n])
+            for n, part in enumerate(parts)
+        )
+    )
+    spread([scr[n] for n in range(len(parts))], out_ref)
+
+
+def total_of(x_ref, out_ref):
+    count = out_ref.shape[1] // HEAD_DIM
+    parts = []
+    for head in range(count):
+        part = x_ref[head].astype(F32)
+        for n in range(head + count, x_ref.shape[0], count):
+            part = part + x_ref[n].astype(F32)
+        parts.append(part.astype(BF16))
+    spread(parts, out_ref)
+
+
+def total_k(meta_ref, *refs):
+    parts, (out_ref, scr, sem) = refs[:-3], refs[-3:]
+    count = out_ref.shape[1] // HEAD_DIM
+    run_copies(
+        *(
+            pltpu.make_async_copy(
+                part, scr.at[n // count * count + (meta_ref[0] ^ (n % count))], sem.at[n]
+            )
+            for n, part in enumerate(parts)
+        )
+    )
+    total_of(scr, out_ref)
+
+
+def total_v(x_ref, out_ref):
+    total_of(x_ref, out_ref)
+
+
+def attended_grads(meta_ref, own_ref, *refs):
+    count = own_ref.shape[1] // HEAD_DIM
+    outs, scr = refs[-1 - count : -1], refs[-1]
+    parts, w_ref = (own_ref, *refs[: -2 - count]), refs[-2 - count]
+    columns = own_ref.shape[1]
+    total = None
+    for n, part in enumerate(parts):
+        piece = lax.dot_general(
+            part[...],
+            w_ref[:, aligned(meta_ref[2] ^ n, columns)],
+            (((1,), (1,)), ((), ())),
+            preferred_element_type=F32,
+        )
+        total = piece if total is None else total + piece
+    scr[...] = total.astype(BF16)
+    fold_each(meta_ref, scr, outs)
+
+
+def mix(meta_ref, *refs):
+    parts, (w_ref, out_ref) = refs[:-2], refs[-2:]
+    columns = out_ref.shape[1]
+    total = None
+    for n, part in enumerate(parts):
+        piece = dot(part[...], w_ref[aligned(meta_ref[2] ^ n, columns), :])
+        total = piece if total is None else total + piece
+    out_ref[...] = total.astype(BF16)
+
+
+def place(sv_ref, sb_ref, view, slot, per_half):
+    block = sb_ref[view, slot]
+    return sv_ref[view, slot], lax.div(block, per_half), aligned(lax.rem(block, per_half), BLOCK_TOKENS)
+
+
+def gather(sv_ref, sb_ref, view, src, rows_scr=None, turned_scr=None):
+    per_half = src.shape[1] // BLOCK_TOKENS
+    for slot in range(sv_ref.shape[1]):
+        source, high, rows = place(sv_ref, sb_ref, view, slot, per_half)
+        block = src[source, rows, :]
+        block = jnp.where(high == 1, join_high(block, block), block)
+        span = slice(slot * BLOCK_TOKENS, (slot + 1) * BLOCK_TOKENS)
+        if rows_scr is not None:
+            rows_scr[span, :] = block
+        if turned_scr is not None:
+            turned_scr[:, span] = block.T[:HEAD_DIM]
+
+
+def scatter(sv_ref, sb_ref, view, acc, lhs, rhs):
+    per_view = acc.shape[1] // BLOCK_TOKENS
+    keys = sv_ref.shape[1] * BLOCK_TOKENS
+    for start in range(0, keys, STEP):
+        part = None
+        for a, b in zip(lhs, rhs):
+            piece = dot(a[start : start + STEP, :], b)
+            part = piece if part is None else part + piece
+        for inner in range(0, STEP, BLOCK_TOKENS):
+            source, _, rows = place(sv_ref, sb_ref, view, (start + inner) // BLOCK_TOKENS, per_view)
+            acc[source, rows, :] += part[inner : inner + BLOCK_TOKENS]
+
+
+def give_back(acc, out_ref):
+    rows = out_ref.shape[1]
+    for view in range(acc.shape[0]):
+        block = acc[view].astype(BF16)
+        out_ref[view] = join(block[:rows], block[rows:])
+
+
+def halves(block):
+    t = block.T
+    return [t[:HEAD_DIM], t[HEAD_DIM:]]
+
+
+def padded(t):
+    return jnp.concatenate([t, jnp.zeros_like(t)], axis=0)
+
+
+def scores(sv_ref, sb_ref, meta_ref, k_ref, *refs):
+    count = len(refs) - 8
+    parts = refs[:count]
+    e_ref, l_ref, k_scr, q_scr, rows_scr, s0, s1, sem = refs[count:]
+    step = pl.program_id(0)
+
+    @pl.when(step == 0)
+    def _():
+        run_copies(
+            pltpu.make_async_copy(k_ref, k_scr, sem.at[count]),
+            *(pltpu.make_async_copy(p, q_scr.at[n], sem.at[n]) for n, p in enumerate(parts)),
+        )
+
+    view = meta_ref[1] * count + (meta_ref[0] ^ step)
+    gather(sv_ref, sb_ref, view, k_scr, rows_scr=rows_scr)
+    keys, queries = s0.shape
+    tops = []
+    for t, s_scr in zip(halves(q_scr[step]), (s0, s1)):
+        q = padded(t * jnp.asarray(SCALE, BF16))
+        top = None
+        for i in range(0, keys, STEP):
+            s = dot(rows_scr[i : i + STEP, :], q)
+            s_scr[i : i + STEP, :] = s
+            m = jnp.max(s.reshape(STEP // 8, 8, queries), axis=0)
+            top = m if top is None else jnp.maximum(top, m)
+        tops.append(jnp.max(top, axis=0, keepdims=True))
+    for n, (top, s_scr) in enumerate(zip(tops, (s0, s1))):
+        total = None
+        for i in range(0, keys, STEP):
+            e = jnp.exp2((s_scr[i : i + STEP, :] - top) * LOG2E)
+            m = jnp.sum(e.reshape(STEP // 8, 8, queries), axis=0)
+            total = m if total is None else total + m
+            e_ref[0, n, i : i + STEP, :] = e.astype(BF16)
+        l_ref[0, n] = jnp.sum(total, axis=0, keepdims=True)
+
+
+def attend(sv_ref, sb_ref, meta_ref, v_ref, *refs):
+    count = (len(refs) - 9) // 2
+    parts, outs = refs[:count], refs[count + 2 : 2 * count + 2]
+    e_ref, l_ref = refs[count : count + 2]
+    delta_ref, dv_ref, v_scr, g_scr, turned_scr, acc, sem = refs[2 * count + 2 :]
+    step = pl.program_id(0)
+
+    @pl.when(step == 0)
+    def _():
+        run_copies(
+            pltpu.make_async_copy(v_ref, v_scr, sem.at[count]),
+            *(pltpu.make_async_copy(p, g_scr.at[n], sem.at[n]) for n, p in enumerate(parts)),
+        )
+        acc[...] = jnp.zeros_like(acc)
+
+    view = meta_ref[1] * count + (meta_ref[0] ^ step)
+    gather(sv_ref, sb_ref, view, v_scr, turned_scr=turned_scr)
+    out, grads = [], []
+    for n, g in enumerate(halves(g_scr[step])):
+        o = (dot(turned_scr[...], e_ref[0, n]) / l_ref[0, n]).astype(BF16)
+        g = (g.astype(F32) / l_ref[0, n]).astype(BF16)
+        delta_ref[0, n] = jnp.sum(o.astype(F32) * g.astype(F32), axis=0, keepdims=True)
+        out.append(o)
+        grads.append(padded(g).T)
+    out = jnp.concatenate(out, axis=0).T
+    for n, ref in enumerate(outs):
+
+        @pl.when(step == n)
+        def _():
+            ref[...] = out
+
+    scatter(sv_ref, sb_ref, view, acc, (e_ref.at[0, 0], e_ref.at[0, 1]), grads)
+
+    @pl.when(step == count - 1)
+    def _():
+        give_back(acc, dv_ref)
+
+
+def backward(sv_ref, sb_ref, meta_ref, k_ref, v_ref, *refs):
+    k_scr, v_scr, q_scr, g_scr, rows_scr, turned_scr, ds0, ds1, acc, sem = refs[-10:]
+    count = q_scr.shape[0]
+    q_parts, g_parts = refs[:count], refs[count : 2 * count]
+    e_ref, l_ref, delta_ref = refs[2 * count : 2 * count + 3]
+    outs = refs[2 * count + 3 : 3 * count + 3]
+    dk_refs = refs[3 * count + 3 : -10]
+    step = pl.program_id(0)
+
+    @pl.when(step == 0)
+    def _():
+        run_copies(
+            pltpu.make_async_copy(k_ref, k_scr, sem.at[2 * count]),
+            pltpu.make_async_copy(v_ref, v_scr, sem.at[2 * count + 1]),
+            *(pltpu.make_async_copy(p, q_scr.at[n], sem.at[n]) for n, p in enumerate(q_parts)),
+            *(
+                pltpu.make_async_copy(p, g_scr.at[n], sem.at[count + n])
+                for n, p in enumerate(g_parts)
+            ),
+        )
+        acc[...] = jnp.zeros_like(acc)
+
+    view = meta_ref[1] * count + (meta_ref[0] ^ step)
+    gather(sv_ref, sb_ref, view, v_scr, rows_scr=rows_scr)
+    gather(sv_ref, sb_ref, view, k_scr, turned_scr=turned_scr)
+    keys = rows_scr.shape[0]
+    queries = [padded(t * jnp.asarray(SCALE, BF16)).T for t in halves(q_scr[step])]
+    for n, (g, ds_scr) in enumerate(zip(halves(g_scr[step]), (ds0, ds1))):
+        g = padded((g.astype(F32) / l_ref[0, n]).astype(BF16))
+        for i in range(0, keys, STEP):
+            dp = dot(rows_scr[i : i + STEP, :], g)
+            e = e_ref[0, n, i : i + STEP, :].astype(F32)
+            ds_scr[i : i + STEP, :] = (e * (dp - delta_ref[0, n])).astype(BF16)
+    scatter(sv_ref, sb_ref, view, acc, (ds0, ds1), queries)
+    dq = [(dot(turned_scr[...], ds[...]) * SCALE).astype(BF16) for ds in (ds0, ds1)]
+    dq = jnp.concatenate(dq, axis=0).T
+    for n, ref in enumerate(outs):
+
+        @pl.when(step == n)
+        def _():
+            ref[...] = dq
+
+    @pl.when(step == count - 1)
+    def _():
+        for n, ref in enumerate(dk_refs):
+            rows = ref.shape[0]
+            block = acc[(meta_ref[1] * count + meta_ref[0]) ^ n].astype(BF16)
+            ref[...] = join(block[:rows], block[rows:])
+
+
+def plane_body(query_rows, key_rows, value_rows, out_weight, out_grad, source_view, source_block):
+    tokens, columns = query_rows.shape
+    half = tokens // 2
+    count = columns // HEAD_DIM
+    views = lax.axis_size("view")
+    group = lax.axis_size("head")
+    keys = source_view.shape[1] * BLOCK_TOKENS
+    head_index = lax.axis_index("head").astype(jnp.int32)
+    view_index = lax.axis_index("view").astype(jnp.int32)
+    meta = jnp.stack([lax.rem(view_index, count), lax.div(view_index, count), head_index])
+    routes = (source_view, source_block, meta)
+
+    def gathered(x):
+        return [x] + [
+            lax.ppermute(x, "head", [(n, n ^ bits) for n in range(group)])
+            for bits in range(1, group)
+        ]
+
+    def view_swap(x):
+        return lax.all_to_all(x, "view", split_axis=0, concat_axis=0, tiled=True)
+
+    def send(parts):
+        return [parts[0]] + [
+            lax.ppermute(part, "view", [(n, n ^ bits) for n in range(views)])
+            for bits, part in enumerate(parts)
+            if bits
+        ]
+
+    full, rows_shape = whole(tokens, columns), shape_of(tokens, columns)
+    one, one_shape = whole(half, 128), shape_of(half, 128)
+    every, every_shape = whole(views, half, 128), shape_of(views, half, 128)
+    k = call(pack_k, (), (key_rows,), [full], every, every_shape)
+    k = view_swap(k)
+    q = call(pack_q, (meta,), (query_rows,), [full], [one] * count, [one_shape] * count)
+    q = send(q)
+    og = gathered(out_grad)
+    v = call(pack_v, (), (value_rows,), [full], every, every_shape)
+    v = view_swap(v)
+    g = call(
+        attended_grads,
+        (meta,),
+        (*og, out_weight),
+        [full] * group + [pl.BlockSpec((columns, group * columns), lambda i, m: (m[2], 0))],
+        [one] * count,
+        [one_shape] * count,
+        scratch=[pltpu.VMEM((tokens, columns), BF16)],
+    )
+    g = send(g)
+    e_spec = pl.BlockSpec((1, 2, keys, half), lambda i, *_: (i, 0, 0, 0))
+    row_spec = pl.BlockSpec((1, 2, 1, half), lambda i, *_: (i, 0, 0, 0))
+    row_shape = shape_of(count, 2, 1, half, dtype=F32)
+    unit = 2 * count * keys * tokens * HEAD_DIM
+    held = pltpu.VMEM((views, half, 128), BF16)
+    mine = pltpu.VMEM((count, half, 128), BF16)
+    totals = pltpu.VMEM((views, tokens, 128), F32)
+    rows_scr = pltpu.VMEM((keys, 128), BF16)
+    turned_scr = pltpu.VMEM((HEAD_DIM, keys), BF16)
+    e, l = call(
+        scores,
+        routes,
+        (k, *q),
+        [HBM] * (1 + count),
+        [e_spec, row_spec],
+        [shape_of(count, 2, keys, half), row_shape],
+        grid=(count,),
+        scratch=[
+            held, mine, rows_scr, pltpu.VMEM((keys, half), F32), pltpu.VMEM((keys, half), F32),
+            pltpu.SemaphoreType.DMA((count + 1,)),
+        ],
+        flops=unit * 4,
+    )
+    *o, delta, dv = call(
+        attend,
+        routes,
+        (v, *g, e, l),
+        [HBM] * (1 + count) + [e_spec, row_spec],
+        [one] * count + [row_spec, every],
+        [one_shape] * count + [row_shape, every_shape],
+        grid=(count,),
+        scratch=[held, mine, turned_scr, totals, pltpu.SemaphoreType.DMA((count + 1,))],
+        flops=unit * 3,
+    )
+    dv = view_swap(dv)
+    o = send(o)
+    back = call(
+        backward,
+        routes,
+        (k, v, *q, *g, e, l, delta),
+        [HBM] * (2 + 2 * count) + [e_spec, row_spec, row_spec],
+        [one] * (count + views),
+        [one_shape] * (count + views),
+        grid=(count,),
+        scratch=[
+            held, held, mine, mine, rows_scr, turned_scr,
+            pltpu.VMEM((keys, half), BF16), pltpu.VMEM((keys, half), BF16),
+            totals, pltpu.SemaphoreType.DMA((2 * count + 2,)),
+        ],
+        flops=unit * 8,
+    )
+    dk = send(back[count:])
+    dq = send(back[:count])
+
+    def collected(parts):
+        return call(
+            collect, (meta,), tuple(parts), [HBM] * count, full, rows_shape,
+            scratch=[mine, pltpu.SemaphoreType.DMA((count,))],
+        )
+
+    attended = collected(o)
+    attended = gathered(attended)
+    mixed_out = call(
+        mix,
+        (meta,),
+        (*attended, out_weight),
+        [full] * group + [pl.BlockSpec((group * columns, columns), lambda i, m: (0, m[2]))],
+        full,
+        rows_shape,
+    )
+    value_grad = call(total_v, (), (dv,), [every], full, rows_shape)
+    query_grad = collected(dq)
+    key_grad = call(
+        total_k, (meta,), tuple(dk), [HBM] * views, full, rows_shape,
+        scratch=[held, pltpu.SemaphoreType.DMA((views,))],
+    )
+    return mixed_out, query_grad, key_grad, value_grad
 
 
 def score_rows(query_part, key_heads, score_scale):
@@ -153,20 +617,31 @@
     return (mixed_out, query_grad, key_grad, value_grad)
 
 
+def planes(*args):
+    return plane_body(*args)
+
+
 def solution(mesh):
-    placed = (
-        P("view", "head"),
-        P("view", "head"),
-        P("view", "head"),
-        P(),
-        P("view", "head"),
-        P(),
-        P(),
-    )
-    return jax.shard_map(
-        body,
-        mesh=mesh,
-        in_specs=placed,
-        out_specs=(P("view", "head"), P("view", "head"), P("view", "head"), P("view", "head")),
-        check_vma=False,
-    )
+    placed = P("view", "head")
+    views, group = mesh.shape["view"], mesh.shape["head"]
+
+    def step(*args):
+        tokens, columns = args[0].shape
+        count = columns // group // HEAD_DIM
+        fits = (
+            views == 2 * count
+            and count > 1
+            and count & (count - 1) == 0
+            and group & (group - 1) == 0
+            and tokens // views % (4 * BLOCK_TOKENS) == 0
+        )
+        inner = jax.shard_map(
+            planes if fits else body,
+            mesh=mesh,
+            in_specs=(placed, placed, placed, P(), placed, P(), P()),
+            out_specs=(placed,) * 4,
+            check_vma=False,
+        )
+        return inner(*args)
+
+    return step

time: 370 us -> 192 us (0.52)
  waiting for transfers between devices: 168 us -> 48.7 us
  Pallas kernels: 0 us -> 79.6 us
  matrix products: 79.5 us -> 0 us
  local copies, waits for them, and re-layouts: 66.8 us -> 6.46 us
  starting transfers between devices: 11.9 us -> 54.8 us
  other arithmetic: 27.8 us -> 0.64 us
  between operations: 14.3 us -> 0.91 us
    all_to_all x2 -> x3, waiting for transfers between devices: 117 us -> 23.5 us  [view_swap(): return lax.all_to_all(x, 'view', split_axis=0, concat_axis=0, tiled=True)]
    pallas_call x0 -> x12, Pallas kernels: none -> 79.6 us  [call(): pl.pallas_call(kernel, grid_spec=pltpu.PrefetchScalarGridSpec(num_scalar_...]
    dot_general x18 -> x0, matrix products: 79.5 us -> none  [the longest x4 17.7 us: score_rows(): jnp.einsum('qhd,khd->hqk', query_part, key_heads, preferred_element_type=...]
    ppermute x0 -> x25, starting transfers between devices: none -> 38.1 us  [the longest x19 34 us: send(): lax.ppermute(part, 'view', [(n, n ^ bits) for n in range(views)])]
    reduce_scatter x1 -> x0, waiting for transfers between devices: 29.2 us -> none  [body(): lax.psum_scatter(lax.dot_general(part_weight, attended_rows, (((0,), (1,)...]
    ppermute x0 -> x25, waiting for transfers between devices: none -> 25.2 us  [the longest x19 12.9 us: send(): lax.ppermute(part, 'view', [(n, n ^ bits) for n in range(views)])]
    all_gather x1 -> x0, waiting for transfers between devices: 21.1 us -> none  [body(): lax.all_gather(out_grad, 'head', axis=1, tiled=True)]
    while x20 -> x0, local copies, waits for them, and re-layouts: 19.3 us -> none
  transfers between devices with their start and end apart: 4 -> 28, of which waited for: 4 -> 6; matrix products, arithmetic and copies ran while one was open for 5% -> 0% of each run, Pallas kernels for 0% -> 31%
where the time goes in v3:
time: 192 us; the launch traced here: 191 us
  Pallas kernels  79.6 us (41%)
  starting transfers between devices  54.8 us (29%)
  waiting for transfers between devices  48.7 us (25%)
  local copies, waits for them, and re-layouts  6.46 us (3%)
    pallas_call x12, Pallas kernels, call(): pl.pallas_call(kernel, grid_spec=pltpu.PrefetchScalarGridSpec(num_scalar_...  79.6 us
    ppermute x19, starting transfers between devices, send(): lax.ppermute(part, 'view', [(n, n ^ bits) for n in range(views)])  34 us
    all_to_all x3, waiting for transfers between devices, view_swap(): return lax.all_to_all(x, 'view', split_axis=0, concat_axis=0, tiled=True)  23.5 us
    all_to_all x3, starting transfers between devices, view_swap(): return lax.all_to_all(x, 'view', split_axis=0, concat_axis=0, tiled=True)  16.6 us
    ppermute x19, waiting for transfers between devices, send(): lax.ppermute(part, 'view', [(n, n ^ bits) for n in range(views)])  12.9 us
    ppermute x6, waiting for transfers between devices, gathered(): lax.ppermute(x, 'head', [(n, n ^ bits) for n in range(group)])  12.3 us
    unnamed x50, local copies, waits for them, and re-layouts  6.46 us
    ppermute x6, starting transfers between devices, gathered(): lax.ppermute(x, 'head', [(n, n ^ bits) for n in range(group)])  4.1 us
  transfers between devices with their start and end apart: 28, of which 6 were waited for; matrix products, arithmetic and copies ran while one was open for 0% of the time, Pallas kernels for 31%

profile of v3, /device:TPU:0, one launch (start us, length us, event | category | flops | bytes accessed | tf_op | source)
XLA Modules:
  0.0 191.1 jit_solution(1089378807075836609)
XLA Ops:
  0.6 2.3 %shard_map.104 = bf16[8,512,128]{2,1,0:T(8,128)(2,1)} custom-call(bf16[1024,256]{1,0:T(8,128)(2,1)} %x_ref.4), custom_call_target="tpu_custom_call" | custom-call | tf_op jit(solution)/shard_map/pallas_call | solution.py:36
  2.9 7.3 %all-to-all-start.1 = ((bf16[8,512,128]{2,1,0:T(8,128)(2,1)}), bf16[8,512,128]{2,1,0:T(8,128)(2,1)S(1)}, u32[]{:S(2)}, u32[]{:S(2)}) async-start(bf16[8,512,128]{2,1,0:T(8,128)(2,1)} %shard_map.104), calls=%async_computation.1 | async-start | bytes 2097152 | tf_op jit(solution)/shard_map/all_to_all | solution.py:366
  10.2 2.3 %shard_map.102 = bf16[8,512,128]{2,1,0:T(8,128)(2,1)} custom-call(bf16[1024,256]{1,0:T(8,128)(2,1)} %x_ref.3), custom_call_target="tpu_custom_call" | custom-call | tf_op jit(solution)/shard_map/pallas_call | solution.py:36
  12.5 23.5 %all-to-all-done.1.k_ref = bf16[8,512,128]{2,1,0:T(8,128)(2,1)S(1)} async-done(((bf16[8,512,128]{2,1,0:T(8,128)(2,1)}), bf16[8,512,128]{2,1,0:T(8,128)(2,1)S(1)}, u32[]{:S(2)}, u32[]{:S(2)}) %all-to-all-start.1) | async-done | bytes 1048608 | tf_op jit(solution)/shard_map/all_to_all | solution.py:366
  36.0 3.6 %all-to-all-start = ((bf16[8,512,128]{2,1,0:T(8,128)(2,1)}), bf16[8,512,128]{2,1,0:T(8,128)(2,1)S(1)}, u32[]{:S(2)}, u32[]{:S(2)}) async-start(bf16[8,512,128]{2,1,0:T(8,128)(2,1)} %shard_map.102), calls=%async_computation | async-start | bytes 2097152 | tf_op jit(solution)/shard_map/all_to_all | solution.py:366
  39.6 1.5 collective-permute-start.1
  42.4 2.7 %shard_map.105 = (bf16[512,128]{1,0:T(8,128)(2,1)}, bf16[512,128]{1,0:T(8,128)(2,1)}, bf16[512,128]{1,0:T(8,128)(2,1)}, bf16[512,128]{1,0:T(8,128)(2,1)}) custom-call(s32[3]{0:T(128)} %pad_add_fusion.meta_ref, bf16[1024,256]{1,0:T(8,128)(2,1)} %x_ref.5), custom_call_target="tpu_custom_call" | custom-call | tf_op jit(solution)/shard_map/pallas_call | solution.py:36
  45.1 2.0 %collective-permute-start.6 = (bf16[512,128]{1,0:T(8,128)(2,1)}, bf16[512,128]{1,0:T(8,128)(2,1)S(1)}, u32[]{:S(2)}, u32[]{:S(2)}) collective-permute-start(bf16[512,128]{1,0:T(8,128)(2,1)} %get-tuple-element.37), channel_id=1, source_target_pairs={{0,4},{4,0},{8,12},{12,8},{16,20},{20,16},{24,28},{28,24},{1,5},{5... | collective-permute-start | bytes 393224 | tf_op jit(solution)/shard_map/ppermute | solution.py:370
  48.5 6.1 %collective-permute-done.1.refs_1_ = bf16[1024,256]{1,0:T(8,128)(2,1)S(1)} collective-permute-done((bf16[1024,256]{1,0:T(8,128)(2,1)}, bf16[1024,256]{1,0:T(8,128)(2,1)S(1)}, u32[]{:S(2)}, u32[]{:S(2)}) %collective-permute-start.1) | collective-permute-done | bytes 524320 | tf_op jit(solution)/shard_map/ppermute | solution.py:361
  54.6 2.9 %collective-permute-start.8 = (bf16[512,128]{1,0:T(8,128)(2,1)}, bf16[512,128]{1,0:T(8,128)(2,1)S(1)}, u32[]{:S(2)}, u32[]{:S(2)}) collective-permute-start(bf16[512,128]{1,0:T(8,128)(2,1)} %get-tuple-element.39), channel_id=1, source_target_pairs={{0,12},{4,8},{8,4},{12,0},{16,28},{20,24},{24,20},{28,16},{1,13},{... | collective-permute-start | bytes 393224 | tf_op jit(solution)/shard_map/ppermute | solution.py:370
  57.5 6.2 %collective-permute-done.2.refs_2_ = bf16[1024,256]{1,0:T(8,128)(2,1)} collective-permute-done((bf16[1024,256]{1,0:T(8,128)(2,1)}, bf16[1024,256]{1,0:T(8,128)(2,1)}, u32[]{:S(2)}, u32[]{:S(2)}) %collective-permute-start.2) | collective-permute-done | bytes 524320 | tf_op jit(solution)/shard_map/ppermute | solution.py:361
  63.7 4.1 %shard_map.103 = (bf16[512,128]{1,0:T(8,128)(2,1)}, bf16[512,128]{1,0:T(8,128)(2,1)}, bf16[512,128]{1,0:T(8,128)(2,1)}, bf16[512,128]{1,0:T(8,128)(2,1)}) custom-call(s32[3]{0:T(128)} %pad_add_fusion.meta_ref, bf16[1024,256]{1,0:T(8,128)(2,1)} %own_ref.1, bf16[1024,256]{1,0:T(8,128)(2,1)} %copy-done.7, bf16[1024,256]{1,0:T(8,128)(2,1)} %copy-done.6, ...), custom_call_target="tpu_custom_call" | custom-call | tf_op jit(solution)/shard_map/pallas_call | solution.py:36
  67.8 1.7 collective-permute-start.3
  69.5 1.5 collective-permute-start.4
  72.0 16.6 %shard_map.106 = (bf16[4,2,2048,512]{3,2,1,0:T(8,128)(2,1)}, f32[4,2,1,512]{3,2,1,0:T(1,128)}) custom-call(s32[8,16]{1,0:T(8,128)} %sv_ref.5, s32[8,16]{1,0:T(8,128)} %sb_ref.5, s32[3]{0:T(128)} %pad_add_fusion.meta_ref, bf16[8,512,128]{2,1,0:T(8,128)(2,1)} %copy-done.2, bf16[512,128]{1,0:T(8,128)(2,1)} %get-tuple-element.36.refs_0_, ...), custom_call_target="tpu_custom_call" | custom-call | flops 4294967296 | tf_op jit(solution)/shard_map/pallas_call | solution.py:36
  89.7 16.5 %shard_map.107 = (bf16[512,128]{1,0:T(8,128)(2,1)}, bf16[512,128]{1,0:T(8,128)(2,1)}, bf16[512,128]{1,0:T(8,128)(2,1)}, bf16[512,128]{1,0:T(8,128)(2,1)}, f32[4,...) custom-call(s32[8,16]{1,0:T(8,128)} %sv_ref.5, s32[8,16]{1,0:T(8,128)} %sb_ref.5, s32[3]{0:T(128)} %pad_add_fusion.meta_ref, ...), custom_call_target="tpu_custom_call" | custom-call | flops 3221225472 | tf_op jit(solution)/shard_map/pallas_call | solution.py:36
  106.2 5.7 %all-to-all-start.2 = ((bf16[8,512,128]{2,1,0:T(8,128)(2,1)}), bf16[8,512,128]{2,1,0:T(8,128)(2,1)S(1)}, u32[]{:S(2)}, u32[]{:S(2)}) async-start(bf16[8,512,128]{2,1,0:T(8,128)(2,1)} %get-tuple-element.59), calls=%async_computation.2 | async-start | bytes 2097152 | tf_op jit(solution)/shard_map/all_to_all | solution.py:366
  111.9 2.0 %collective-permute-start.9 = (bf16[512,128]{1,0:T(8,128)(2,1)}, bf16[512,128]{1,0:T(8,128)(2,1)S(1)}, u32[]{:S(2)}, u32[]{:S(2)}) collective-permute-start(bf16[512,128]{1,0:T(8,128)(2,1)} %get-tuple-element.43), channel_id=1, source_target_pairs={{0,4},{4,0},{8,12},{12,8},{16,20},{20,16},{24,28},{28,24},{1,5},{5... | collective-permute-start | bytes 393224 | tf_op jit(solution)/shard_map/ppermute | solution.py:370
  115.4 20.7 %shard_map.110 = (bf16[512,128]{1,0:T(8,128)(2,1)}, bf16[512,128]{1,0:T(8,128)(2,1)}, bf16[512,128]{1,0:T(8,128)(2,1)}, bf16[512,128]{1,0:T(8,128)(2,1)}, bf16[5...) custom-call(s32[8,16]{1,0:T(8,128)} %sv_ref.5, ...), custom_call_target="tpu_custom_call" | custom-call | flops 8589934592 | tf_op jit(solution)/shard_map/pallas_call | solution.py:36
  136.1 2.1 %collective-permute-start.15 = (bf16[512,128]{1,0:T(8,128)(2,1)}, bf16[512,128]{1,0:T(8,128)(2,1)}, u32[]{:S(2)}, u32[]{:S(2)}) collective-permute-start(bf16[512,128]{1,0:T(8,128)(2,1)} %get-tuple-element.48), channel_id=1, source_target_pairs={{0,4},{4,0},{8,12},{12,8},{16,20},{20,16},{24,28},{28,24},{1,5},{5... | collective-permute-start | bytes 393224 | tf_op jit(solution)/shard_map/ppermute | solution.py:370
  139.7 1.9 %collective-permute-start.18 = (bf16[512,128]{1,0:T(8,128)(2,1)}, bf16[512,128]{1,0:T(8,128)(2,1)S(1)}, u32[]{:S(2)}, u32[]{:S(2)}) collective-permute-start(bf16[512,128]{1,0:T(8,128)(2,1)} %get-tuple-element.52), channel_id=1, source_target_pairs={{0,4},{4,0},{8,12},{12,8},{16,20},{20,16},{24,28},{28,24},{1,5},{5... | collective-permute-start | bytes 393224 | tf_op jit(solution)/shard_map/ppermute | solution.py:370
  142.3 2.8 %shard_map.108.refs_0_ = bf16[1024,256]{1,0:T(8,128)(2,1)} custom-call(s32[3]{0:T(128)} %pad_add_fusion.meta_ref, bf16[512,128]{1,0:T(8,128)(2,1)} %get-tuple-element.42.refs_0_, bf16[512,128]{1,0:T(8,128)(2,1)} %copy-done.19, bf16[512,128]{1,0:T(8,128)(2,1)} %copy-done.20, bf16[512,128]{1,0:T(8,128)(2,1)} %copy-done.21), custom_call_target="tpu_custom_call" | custom-call | tf_op jit(solution)/shard_map/pallas_call | solution.py:36
  149.8 4.4 %collective-permute-done.19.refs_2_ = bf16[512,128]{1,0:T(8,128)(2,1)S(1)} collective-permute-done((bf16[512,128]{1,0:T(8,128)(2,1)}, bf16[512,128]{1,0:T(8,128)(2,1)S(1)}, u32[]{:S(2)}, u32[]{:S(2)}) %collective-permute-start.19) | collective-permute-done | bytes 131104 | tf_op jit(solution)/shard_map/ppermute | solution.py:370
  154.3 2.4 %collective-permute-start.21 = (bf16[512,128]{1,0:T(8,128)(2,1)}, bf16[512,128]{1,0:T(8,128)(2,1)S(1)}, u32[]{:S(2)}, u32[]{:S(2)}) collective-permute-start(bf16[512,128]{1,0:T(8,128)(2,1)} %get-tuple-element.55), channel_id=1, source_target_pairs={{0,16},{4,20},{8,24},{12,28},{16,0},{20,4},{24,8},{28,12},{1,17},{... | collective-permute-start | bytes 393224 | tf_op jit(solution)/shard_map/ppermute | solution.py:370
  156.6 3.6 %collective-permute-start.22 = (bf16[512,128]{1,0:T(8,128)(2,1)}, bf16[512,128]{1,0:T(8,128)(2,1)S(1)}, u32[]{:S(2)}, u32[]{:S(2)}) collective-permute-start(bf16[512,128]{1,0:T(8,128)(2,1)} %get-tuple-element.56), channel_id=1, source_target_pairs={{0,20},{4,16},{8,28},{12,24},{16,4},{20,0},{24,12},{28,8},{1,21},{... | collective-permute-start | bytes 393224 | tf_op jit(solution)/shard_map/ppermute | solution.py:370
  160.2 7.0 %collective-permute-done.21.refs_4_ = bf16[512,128]{1,0:T(8,128)(2,1)S(1)} collective-permute-done((bf16[512,128]{1,0:T(8,128)(2,1)}, bf16[512,128]{1,0:T(8,128)(2,1)S(1)}, u32[]{:S(2)}, u32[]{:S(2)}) %collective-permute-start.21) | collective-permute-done | bytes 131104 | tf_op jit(solution)/shard_map/ppermute | solution.py:370
  167.2 3.4 %collective-permute-start.23 = (bf16[512,128]{1,0:T(8,128)(2,1)}, bf16[512,128]{1,0:T(8,128)(2,1)S(1)}, u32[]{:S(2)}, u32[]{:S(2)}) collective-permute-start(bf16[512,128]{1,0:T(8,128)(2,1)} %get-tuple-element.57), channel_id=1, source_target_pairs={{0,24},{4,28},{8,16},{12,20},{16,8},{20,12},{24,0},{28,4},{1,25},{... | collective-permute-start | bytes 393224 | tf_op jit(solution)/shard_map/ppermute | solution.py:370
  170.6 3.7 %collective-permute-start.24 = (bf16[512,128]{1,0:T(8,128)(2,1)}, bf16[512,128]{1,0:T(8,128)(2,1)S(1)}, u32[]{:S(2)}, u32[]{:S(2)}) collective-permute-start(bf16[512,128]{1,0:T(8,128)(2,1)} %get-tuple-element.58), channel_id=1, source_target_pairs={{0,28},{4,24},{8,20},{12,16},{16,12},{20,8},{24,4},{28,0},{1,29},{... | collective-permute-start | bytes 393224 | tf_op jit(solution)/shard_map/ppermute | solution.py:370
  174.3 2.8 %shard_map.111 = bf16[1024,256]{1,0:T(8,128)(2,1)} custom-call(s32[3]{0:T(128)} %pad_add_fusion.meta_ref, bf16[512,128]{1,0:T(8,128)(2,1)} %get-tuple-element.47.refs_0_, bf16[512,128]{1,0:T(8,128)(2,1)} %collective-permute-done.15.refs_1_, bf16[512,128]{1,0:T(8,128)(2,1)} %collective-permute-done.16.refs_2_, bf16[512,128]{1,0:T(8,128)(2,1)} %copy-done.18), custom_call_target="tpu_custom_call" | custom-call | tf_op jit(solution)/shard_map/pallas_call | solution.py:36
  179.2 3.0 %shard_map.112 = bf16[1024,256]{1,0:T(8,128)(2,1)} custom-call(s32[3]{0:T(128)} %pad_add_fusion.meta_ref, bf16[512,128]{1,0:T(8,128)(2,1)} %get-tuple-element.51.refs_0_, bf16[512,128]{1,0:T(8,128)(2,1)} %copy-done.11, bf16[512,128]{1,0:T(8,128)(2,1)} %copy-done.12, bf16[512,128]{1,0:T(8,128)(2,1)} %copy-done.13, bf16[512,128]{1,0:T(8,128)(2,1)} %copy-done.14, ...), custom_call_target="tpu_custom_call" | custom-call | tf_op jit(solution)/shard_map/pallas_call | solution.py:36
  184.1 3.8 %shard_map.109 = bf16[1024,256]{1,0:T(8,128)(2,1)} custom-call(s32[3]{0:T(128)} %pad_add_fusion.meta_ref, bf16[1024,256]{1,0:T(8,128)(2,1)} %shard_map.108.refs_0_, bf16[1024,256]{1,0:T(8,128)(2,1)} %copy-done.5, bf16[1024,256]{1,0:T(8,128)(2,1)} %copy-done.4, bf16[1024,256]{1,0:T(8,128)(2,1)} %copy-done.3, bf16[1024,1024]{1,0:T(8,128)(2,1)} %refs_4_.1), custom_call_target="tpu_custom_call" | custom-call | tf_op jit(solution)/shard_map/pallas_call | solution.py:36
  188.9 2.2 %shard_map.113 = bf16[1024,256]{1,0:T(8,128)(2,1)} custom-call(bf16[8,512,128]{2,1,0:T(8,128)(2,1)} %copy-done.1), custom_call_target="tpu_custom_call" | custom-call | tf_op jit(solution)/shard_map/pallas_call | solution.py:36
  (87 shorter events, 18.1 us)
Async XLA Ops:
  2.9 33.1 %all-to-all-start.1 = ((bf16[8,512,128]{2,1,0:T(8,128)(2,1)}), bf16[8,512,128]{2,1,0:T(8,128)(2,1)S(1)}, u32[]{:S(2)}, u32[]{:S(2)}) async-start(bf16[8,512,128]{2,1,0:T(8,128)(2,1)} %shard_map.104), calls=%async_computation.1 | async-start | bytes 2097152 | tf_op jit(solution)/shard_map/all_to_all | solution.py:366
  36.0 35.3 %copy-start.2 = (bf16[8,512,128]{2,1,0:T(8,128)(2,1)}, bf16[8,512,128]{2,1,0:T(8,128)(2,1)S(1)}, u32[]{:S(2)}) copy-start(bf16[8,512,128]{2,1,0:T(8,128)(2,1)S(1)} %all-to-all-done.1.k_ref) | copy-start | bytes 3145732
  36.0 52.7 %all-to-all-start = ((bf16[8,512,128]{2,1,0:T(8,128)(2,1)}), bf16[8,512,128]{2,1,0:T(8,128)(2,1)S(1)}, u32[]{:S(2)}, u32[]{:S(2)}) async-start(bf16[8,512,128]{2,1,0:T(8,128)(2,1)} %shard_map.102), calls=%async_computation | async-start | bytes 2097152 | tf_op jit(solution)/shard_map/all_to_all | solution.py:366
  39.6 15.1 %collective-permute-start.1 = (bf16[1024,256]{1,0:T(8,128)(2,1)}, bf16[1024,256]{1,0:T(8,128)(2,1)S(1)}, u32[]{:S(2)}, u32[]{:S(2)}) collective-permute-start(bf16[1024,256]{1,0:T(8,128)(2,1)} %own_ref.1), channel_id=1, source_target_pairs={{0,2},{1,3},{2,0},{3,1},{4,6},{5,7},{6,4},{7,5},{8,10},{9,11},{10,... | collective-permute-start | bytes 1572872 | tf_op jit(solution)/shard_map/ppermute | solution.py:361
  41.1 16.4 %collective-permute-start = (bf16[1024,256]{1,0:T(8,128)(2,1)}, bf16[1024,256]{1,0:T(8,128)(2,1)S(1)}, u32[]{:S(2)}, u32[]{:S(2)}) collective-permute-start(bf16[1024,256]{1,0:T(8,128)(2,1)} %own_ref.1), channel_id=1, source_target_pairs={{0,1},{1,0},{2,3},{3,2},{4,5},{5,4},{6,7},{7,6},{8,9},{9,8},{10,11... | collective-permute-start | bytes 1572872 | tf_op jit(solution)/shard_map/ppermute | solution.py:361
  41.1 22.6 %collective-permute-start.2 = (bf16[1024,256]{1,0:T(8,128)(2,1)}, bf16[1024,256]{1,0:T(8,128)(2,1)}, u32[]{:S(2)}, u32[]{:S(2)}) collective-permute-start(bf16[1024,256]{1,0:T(8,128)(2,1)} %own_ref.1), channel_id=1, source_target_pairs={{0,3},{1,2},{2,1},{3,0},{4,7},{5,6},{6,5},{7,4},{8,11},{9,10},{10,... | collective-permute-start | bytes 1572872 | tf_op jit(solution)/shard_map/ppermute | solution.py:361
  45.1 25.9 %collective-permute-start.6 = (bf16[512,128]{1,0:T(8,128)(2,1)}, bf16[512,128]{1,0:T(8,128)(2,1)S(1)}, u32[]{:S(2)}, u32[]{:S(2)}) collective-permute-start(bf16[512,128]{1,0:T(8,128)(2,1)} %get-tuple-element.37), channel_id=1, source_target_pairs={{0,4},{4,0},{8,12},{12,8},{16,20},{20,16},{24,28},{28,24},{1,5},{5... | collective-permute-start | bytes 393224 | tf_op jit(solution)/shard_map/ppermute | solution.py:370
  47.0 24.2 %collective-permute-start.7 = (bf16[512,128]{1,0:T(8,128)(2,1)}, bf16[512,128]{1,0:T(8,128)(2,1)S(1)}, u32[]{:S(2)}, u32[]{:S(2)}) collective-permute-start(bf16[512,128]{1,0:T(8,128)(2,1)} %get-tuple-element.38), channel_id=1, source_target_pairs={{0,8},{4,12},{8,0},{12,4},{16,24},{20,28},{24,16},{28,20},{1,9},{5... | collective-permute-start | bytes 393224 | tf_op jit(solution)/shard_map/ppermute | solution.py:370
  54.6 16.7 %collective-permute-start.8 = (bf16[512,128]{1,0:T(8,128)(2,1)}, bf16[512,128]{1,0:T(8,128)(2,1)S(1)}, u32[]{:S(2)}, u32[]{:S(2)}) collective-permute-start(bf16[512,128]{1,0:T(8,128)(2,1)} %get-tuple-element.39), channel_id=1, source_target_pairs={{0,12},{4,8},{8,4},{12,0},{16,28},{20,24},{24,20},{28,16},{1,13},{... | collective-permute-start | bytes 393224 | tf_op jit(solution)/shard_map/ppermute | solution.py:370
  67.8 20.8 %collective-permute-start.3 = (bf16[512,128]{1,0:T(8,128)(2,1)}, bf16[512,128]{1,0:T(8,128)(2,1)S(1)}, u32[]{:S(2)}, u32[]{:S(2)}) collective-permute-start(bf16[512,128]{1,0:T(8,128)(2,1)} %get-tuple-element.33), channel_id=1, source_target_pairs={{0,4},{4,0},{8,12},{12,8},{16,20},{20,16},{24,28},{28,24},{1,5},{5... | collective-permute-start | bytes 393224 | tf_op jit(solution)/shard_map/ppermute | solution.py:370
  69.5 19.1 %collective-permute-start.4 = (bf16[512,128]{1,0:T(8,128)(2,1)}, bf16[512,128]{1,0:T(8,128)(2,1)S(1)}, u32[]{:S(2)}, u32[]{:S(2)}) collective-permute-start(bf16[512,128]{1,0:T(8,128)(2,1)} %get-tuple-element.34), channel_id=1, source_target_pairs={{0,8},{4,12},{8,0},{12,4},{16,24},{20,28},{24,16},{28,20},{1,9},{5... | collective-permute-start | bytes 393224 | tf_op jit(solution)/shard_map/ppermute | solution.py:370
  71.0 17.6 %collective-permute-start.5 = (bf16[512,128]{1,0:T(8,128)(2,1)}, bf16[512,128]{1,0:T(8,128)(2,1)S(1)}, u32[]{:S(2)}, u32[]{:S(2)}) collective-permute-start(bf16[512,128]{1,0:T(8,128)(2,1)} %get-tuple-element.35), channel_id=1, source_target_pairs={{0,12},{4,8},{8,4},{12,0},{16,28},{20,24},{24,20},{28,16},{1,13},{... | collective-permute-start | bytes 393224 | tf_op jit(solution)/shard_map/ppermute | solution.py:370
  106.2 81.7 %all-to-all-start.2 = ((bf16[8,512,128]{2,1,0:T(8,128)(2,1)}), bf16[8,512,128]{2,1,0:T(8,128)(2,1)S(1)}, u32[]{:S(2)}, u32[]{:S(2)}) async-start(bf16[8,512,128]{2,1,0:T(8,128)(2,1)} %get-tuple-element.59), calls=%async_computation.2 | async-start | bytes 2097152 | tf_op jit(solution)/shard_map/all_to_all | solution.py:366
  111.9 27.7 %collective-permute-start.9 = (bf16[512,128]{1,0:T(8,128)(2,1)}, bf16[512,128]{1,0:T(8,128)(2,1)S(1)}, u32[]{:S(2)}, u32[]{:S(2)}) collective-permute-start(bf16[512,128]{1,0:T(8,128)(2,1)} %get-tuple-element.43), channel_id=1, source_target_pairs={{0,4},{4,0},{8,12},{12,8},{16,20},{20,16},{24,28},{28,24},{1,5},{5... | collective-permute-start | bytes 393224 | tf_op jit(solution)/shard_map/ppermute | solution.py:370
  113.9 25.8 %collective-permute-start.10 = (bf16[512,128]{1,0:T(8,128)(2,1)}, bf16[512,128]{1,0:T(8,128)(2,1)S(1)}, u32[]{:S(2)}, u32[]{:S(2)}) collective-permute-start(bf16[512,128]{1,0:T(8,128)(2,1)} %get-tuple-element.44), channel_id=1, source_target_pairs={{0,8},{4,12},{8,0},{12,4},{16,24},{20,28},{24,16},{28,20},{1,9},{5... | collective-permute-start | bytes 393224 | tf_op jit(solution)/shard_map/ppermute | solution.py:370
  115.4 26.3 %collective-permute-start.11 = (bf16[512,128]{1,0:T(8,128)(2,1)}, bf16[512,128]{1,0:T(8,128)(2,1)S(1)}, u32[]{:S(2)}, u32[]{:S(2)}) collective-permute-start(bf16[512,128]{1,0:T(8,128)(2,1)} %get-tuple-element.45), channel_id=1, source_target_pairs={{0,12},{4,8},{8,4},{12,0},{16,28},{20,24},{24,20},{28,16},{1,13},{... | collective-permute-start | bytes 393224 | tf_op jit(solution)/shard_map/ppermute | solution.py:370
  136.1 9.1 %collective-permute-start.15 = (bf16[512,128]{1,0:T(8,128)(2,1)}, bf16[512,128]{1,0:T(8,128)(2,1)}, u32[]{:S(2)}, u32[]{:S(2)}) collective-permute-start(bf16[512,128]{1,0:T(8,128)(2,1)} %get-tuple-element.48), channel_id=1, source_target_pairs={{0,4},{4,0},{8,12},{12,8},{16,20},{20,16},{24,28},{28,24},{1,5},{5... | collective-permute-start | bytes 393224 | tf_op jit(solution)/shard_map/ppermute | solution.py:370
  138.1 8.1 %collective-permute-start.16 = (bf16[512,128]{1,0:T(8,128)(2,1)}, bf16[512,128]{1,0:T(8,128)(2,1)}, u32[]{:S(2)}, u32[]{:S(2)}) collective-permute-start(bf16[512,128]{1,0:T(8,128)(2,1)} %get-tuple-element.49), channel_id=1, source_target_pairs={{0,8},{4,12},{8,0},{12,4},{16,24},{20,28},{24,16},{28,20},{1,9},{5... | collective-permute-start | bytes 393224 | tf_op jit(solution)/shard_map/ppermute | solution.py:370
  139.6 7.4 %collective-permute-start.17 = (bf16[512,128]{1,0:T(8,128)(2,1)}, bf16[512,128]{1,0:T(8,128)(2,1)S(1)}, u32[]{:S(2)}, u32[]{:S(2)}) collective-permute-start(bf16[512,128]{1,0:T(8,128)(2,1)} %get-tuple-element.50), channel_id=1, source_target_pairs={{0,12},{4,8},{8,4},{12,0},{16,28},{20,24},{24,20},{28,16},{1,13},{... | collective-permute-start | bytes 393224 | tf_op jit(solution)/shard_map/ppermute | solution.py:370
  139.7 9.5 %collective-permute-start.18 = (bf16[512,128]{1,0:T(8,128)(2,1)}, bf16[512,128]{1,0:T(8,128)(2,1)S(1)}, u32[]{:S(2)}, u32[]{:S(2)}) collective-permute-start(bf16[512,128]{1,0:T(8,128)(2,1)} %get-tuple-element.52), channel_id=1, source_target_pairs={{0,4},{4,0},{8,12},{12,8},{16,20},{20,16},{24,28},{28,24},{1,5},{5... | collective-permute-start | bytes 393224 | tf_op jit(solution)/shard_map/ppermute | solution.py:370
  145.1 37.2 %collective-permute-start.14 = (bf16[1024,256]{1,0:T(8,128)(2,1)}, bf16[1024,256]{1,0:T(8,128)(2,1)S(1)}, u32[]{:S(2)}, u32[]{:S(2)}) collective-permute-start(bf16[1024,256]{1,0:T(8,128)(2,1)} %shard_map.108.refs_0_), channel_id=1, source_target_pairs={{0,3},{1,2},{2,1},{3,0},{4,7},{5,6},{6,5},{7,4},{8,11},{9,10},{10,... | collective-permute-start | bytes 1572872 | tf_op jit(solution)/shard_map/ppermute | solution.py:361
  145.2 37.1 %collective-permute-start.13 = (bf16[1024,256]{1,0:T(8,128)(2,1)}, bf16[1024,256]{1,0:T(8,128)(2,1)S(1)}, u32[]{:S(2)}, u32[]{:S(2)}) collective-permute-start(bf16[1024,256]{1,0:T(8,128)(2,1)} %shard_map.108.refs_0_), channel_id=1, source_target_pairs={{0,2},{1,3},{2,0},{3,1},{4,6},{5,7},{6,4},{7,5},{8,10},{9,11},{10,... | collective-permute-start | bytes 1572872 | tf_op jit(solution)/shard_map/ppermute | solution.py:361
  146.2 36.1 %collective-permute-start.12 = (bf16[1024,256]{1,0:T(8,128)(2,1)}, bf16[1024,256]{1,0:T(8,128)(2,1)S(1)}, u32[]{:S(2)}, u32[]{:S(2)}) collective-permute-start(bf16[1024,256]{1,0:T(8,128)(2,1)} %shard_map.108.refs_0_), channel_id=1, source_target_pairs={{0,1},{1,0},{2,3},{3,2},{4,5},{5,4},{6,7},{7,6},{8,9},{9,8},{10,11... | collective-permute-start | bytes 1572872 | tf_op jit(solution)/shard_map/ppermute | solution.py:361
  147.7 6.6 %collective-permute-start.19 = (bf16[512,128]{1,0:T(8,128)(2,1)}, bf16[512,128]{1,0:T(8,128)(2,1)S(1)}, u32[]{:S(2)}, u32[]{:S(2)}) collective-permute-start(bf16[512,128]{1,0:T(8,128)(2,1)} %get-tuple-element.53), channel_id=1, source_target_pairs={{0,8},{4,12},{8,0},{12,4},{16,24},{20,28},{24,16},{28,20},{1,9},{5... | collective-permute-start | bytes 393224 | tf_op jit(solution)/shard_map/ppermute | solution.py:370
  149.1 29.4 %copy-start.11 = (bf16[512,128]{1,0:T(8,128)(2,1)}, bf16[512,128]{1,0:T(8,128)(2,1)S(1)}, u32[]{:S(2)}) copy-start(bf16[512,128]{1,0:T(8,128)(2,1)S(1)} %collective-permute-done.18.refs_1_) | copy-start | bytes 393220
  149.1 7.5 %collective-permute-start.20 = (bf16[512,128]{1,0:T(8,128)(2,1)}, bf16[512,128]{1,0:T(8,128)(2,1)S(1)}, u32[]{:S(2)}, u32[]{:S(2)}) collective-permute-start(bf16[512,128]{1,0:T(8,128)(2,1)} %get-tuple-element.54), channel_id=1, source_target_pairs={{0,12},{4,8},{8,4},{12,0},{16,28},{20,24},{24,20},{28,16},{1,13},{... | collective-permute-start | bytes 393224 | tf_op jit(solution)/shard_map/ppermute | solution.py:370
  154.3 24.3 %copy-start.12 = (bf16[512,128]{1,0:T(8,128)(2,1)}, bf16[512,128]{1,0:T(8,128)(2,1)S(1)}, u32[]{:S(2)}) copy-start(bf16[512,128]{1,0:T(8,128)(2,1)S(1)} %collective-permute-done.19.refs_2_) | copy-start | bytes 393220
  154.3 12.9 %collective-permute-start.21 = (bf16[512,128]{1,0:T(8,128)(2,1)}, bf16[512,128]{1,0:T(8,128)(2,1)S(1)}, u32[]{:S(2)}, u32[]{:S(2)}) collective-permute-start(bf16[512,128]{1,0:T(8,128)(2,1)} %get-tuple-element.55), channel_id=1, source_target_pairs={{0,16},{4,20},{8,24},{12,28},{16,0},{20,4},{24,8},{28,12},{1,17},{... | collective-permute-start | bytes 393224 | tf_op jit(solution)/shard_map/ppermute | solution.py:370
  156.6 21.9 %copy-start.13 = (bf16[512,128]{1,0:T(8,128)(2,1)}, bf16[512,128]{1,0:T(8,128)(2,1)S(1)}, u32[]{:S(2)}) copy-start(bf16[512,128]{1,0:T(8,128)(2,1)S(1)} %collective-permute-done.20.refs_3_) | copy-start | bytes 393220
  156.6 13.9 %collective-permute-start.22 = (bf16[512,128]{1,0:T(8,128)(2,1)}, bf16[512,128]{1,0:T(8,128)(2,1)S(1)}, u32[]{:S(2)}, u32[]{:S(2)}) collective-permute-start(bf16[512,128]{1,0:T(8,128)(2,1)} %get-tuple-element.56), channel_id=1, source_target_pairs={{0,20},{4,16},{8,28},{12,24},{16,4},{20,0},{24,12},{28,8},{1,21},{... | collective-permute-start | bytes 393224 | tf_op jit(solution)/shard_map/ppermute | solution.py:370
  167.2 9.9 %collective-permute-start.23 = (bf16[512,128]{1,0:T(8,128)(2,1)}, bf16[512,128]{1,0:T(8,128)(2,1)S(1)}, u32[]{:S(2)}, u32[]{:S(2)}) collective-permute-start(bf16[512,128]{1,0:T(8,128)(2,1)} %get-tuple-element.57), channel_id=1, source_target_pairs={{0,24},{4,28},{8,16},{12,20},{16,8},{20,12},{24,0},{28,4},{1,25},{... | collective-permute-start | bytes 393224 | tf_op jit(solution)/shard_map/ppermute | solution.py:370
  170.6 8.0 %collective-permute-start.24 = (bf16[512,128]{1,0:T(8,128)(2,1)}, bf16[512,128]{1,0:T(8,128)(2,1)S(1)}, u32[]{:S(2)}, u32[]{:S(2)}) collective-permute-start(bf16[512,128]{1,0:T(8,128)(2,1)} %get-tuple-element.58), channel_id=1, source_target_pairs={{0,28},{4,24},{8,20},{12,16},{16,12},{20,8},{24,4},{28,0},{1,29},{... | collective-permute-start | bytes 393224 | tf_op jit(solution)/shard_map/ppermute | solution.py:370
  (21 other events, 50.8 us)

commit v4 on v3

--- a/solution.py
+++ b/solution.py
@@ -65,32 +65,30 @@
         copy.wait()
 
 
-def fold_all(x_ref, out_ref):
-    rows, columns = x_ref.shape
-    count = columns // HEAD_DIM
-    for head in range(0, count, 2):
-        lanes = slice(HEAD_DIM * head, HEAD_DIM * (head + 2))
-        top, low = x_ref[: rows // 2, lanes], x_ref[rows // 2 :, lanes]
-        for n in range(head, out_ref.shape[0], count):
-            out_ref[n] = join(top, low)
-            out_ref[n + 1] = join_high(top, low)
+def fold_pair(x_ref, out_ref):
+    rows = out_ref.shape[2]
+    top, low = x_ref[:rows, :], x_ref[rows:, :]
+    for n in range(out_ref.shape[0]):
+        out_ref[n, 0] = join(top, low)
+        out_ref[n, 1] = join_high(top, low)
 
 
 def fold_each(meta_ref, x_ref, outs):
     rows = x_ref.shape[0]
+    count = x_ref.shape[1] // HEAD_DIM
     for n, out in enumerate(outs):
-        head = meta_ref[0] ^ n
+        head = meta_ref[0] ^ (n % count)
         pair = aligned(head // 2, 128)
         top, low = x_ref[: rows // 2, pair], x_ref[rows // 2 :, pair]
         out[...] = jnp.where(head % 2 == 1, join_high(top, low), join(top, low))
 
 
 def pack_k(x_ref, out_ref):
-    fold_all(x_ref, out_ref)
-
-
-def pack_v(x_ref, out_ref):
-    fold_all(x_ref, out_ref)
+    fold_pair(x_ref, out_ref)
+
+
+def pack_v(meta_ref, x_ref, *outs):
+    fold_each(meta_ref, x_ref, outs)
 
 
 def pack_q(meta_ref, x_ref, *outs):
@@ -116,33 +114,22 @@
     spread([scr[n] for n in range(len(parts))], out_ref)
 
 
-def total_of(x_ref, out_ref):
-    count = out_ref.shape[1] // HEAD_DIM
+def total_pair(x_ref, out_ref):
     parts = []
-    for head in range(count):
-        part = x_ref[head].astype(F32)
-        for n in range(head + count, x_ref.shape[0], count):
-            part = part + x_ref[n].astype(F32)
+    for head in range(2):
+        part = x_ref[0, head].astype(F32)
+        for n in range(1, x_ref.shape[0]):
+            part = part + x_ref[n, head].astype(F32)
         parts.append(part.astype(BF16))
     spread(parts, out_ref)
 
 
-def total_k(meta_ref, *refs):
-    parts, (out_ref, scr, sem) = refs[:-3], refs[-3:]
-    count = out_ref.shape[1] // HEAD_DIM
-    run_copies(
-        *(
-            pltpu.make_async_copy(
-                part, scr.at[n // count * count + (meta_ref[0] ^ (n % count))], sem.at[n]
-            )
-            for n, part in enumerate(parts)
-        )
-    )
-    total_of(scr, out_ref)
+def total_k(x_ref, out_ref):
+    total_pair(x_ref, out_ref)
 
 
 def total_v(x_ref, out_ref):
-    total_of(x_ref, out_ref)
+    total_pair(x_ref, out_ref)
 
 
 def attended_grads(meta_ref, own_ref, *refs):
@@ -218,6 +205,14 @@
 
 def padded(t):
     return jnp.concatenate([t, jnp.zeros_like(t)], axis=0)
+
+
+def view_copies(meta_ref, count, parts, scr, sems):
+    here = meta_ref[1] * count + meta_ref[0]
+    return [
+        pltpu.make_async_copy(part, scr.at[here ^ n], sem)
+        for n, (part, sem) in enumerate(zip(parts, sems))
+    ]
 
 
 def scores(sv_ref, sb_ref, meta_ref, k_ref, *refs):
@@ -256,17 +251,19 @@
         l_ref[0, n] = jnp.sum(total, axis=0, keepdims=True)
 
 
-def attend(sv_ref, sb_ref, meta_ref, v_ref, *refs):
-    count = (len(refs) - 9) // 2
-    parts, outs = refs[:count], refs[count + 2 : 2 * count + 2]
-    e_ref, l_ref = refs[count : count + 2]
-    delta_ref, dv_ref, v_scr, g_scr, turned_scr, acc, sem = refs[2 * count + 2 :]
+def attend(sv_ref, sb_ref, meta_ref, *refs):
+    v_scr, g_scr, turned_scr, acc, sem = refs[-5:]
+    count, views = g_scr.shape[0], v_scr.shape[0]
+    v_parts, parts = refs[:views], refs[views : views + count]
+    e_ref, l_ref = refs[views + count : views + count + 2]
+    outs = refs[views + count + 2 : views + 2 * count + 2]
+    delta_ref, dv_ref = refs[views + 2 * count + 2 : -5]
     step = pl.program_id(0)
 
     @pl.when(step == 0)
     def _():
         run_copies(
-            pltpu.make_async_copy(v_ref, v_scr, sem.at[count]),
+            *view_copies(meta_ref, count, v_parts, v_scr, [sem.at[count + n] for n in range(views)]),
             *(pltpu.make_async_copy(p, g_scr.at[n], sem.at[n]) for n, p in enumerate(parts)),
         )
         acc[...] = jnp.zeros_like(acc)
@@ -294,20 +291,23 @@
         give_back(acc, dv_ref)
 
 
-def backward(sv_ref, sb_ref, meta_ref, k_ref, v_ref, *refs):
+def backward(sv_ref, sb_ref, meta_ref, k_ref, *refs):
     k_scr, v_scr, q_scr, g_scr, rows_scr, turned_scr, ds0, ds1, acc, sem = refs[-10:]
-    count = q_scr.shape[0]
+    count, views = q_scr.shape[0], v_scr.shape[0]
+    v_parts, refs = refs[:views], refs[views:]
     q_parts, g_parts = refs[:count], refs[count : 2 * count]
     e_ref, l_ref, delta_ref = refs[2 * count : 2 * count + 3]
     outs = refs[2 * count + 3 : 3 * count + 3]
-    dk_refs = refs[3 * count + 3 : -10]
+    dk_ref = refs[3 * count + 3]
     step = pl.program_id(0)
 
     @pl.when(step == 0)
     def _():
         run_copies(
             pltpu.make_async_copy(k_ref, k_scr, sem.at[2 * count]),
-            pltpu.make_async_copy(v_ref, v_scr, sem.at[2 * count + 1]),
+            *view_copies(
+                meta_ref, count, v_parts, v_scr, [sem.at[2 * count + 1 + n] for n in range(views)]
+            ),
             *(pltpu.make_async_copy(p, q_scr.at[n], sem.at[n]) for n, p in enumerate(q_parts)),
             *(
                 pltpu.make_async_copy(p, g_scr.at[n], sem.at[count + n])
@@ -338,10 +338,7 @@
 
     @pl.when(step == count - 1)
     def _():
-        for n, ref in enumerate(dk_refs):
-            rows = ref.shape[0]
-            block = acc[(meta_ref[1] * count + meta_ref[0]) ^ n].astype(BF16)
-            ref[...] = join(block[:rows], block[rows:])
+        give_back(acc, dk_ref)
 
 
 def plane_body(query_rows, key_rows, value_rows, out_weight, out_grad, source_view, source_block):
@@ -356,11 +353,17 @@
     meta = jnp.stack([lax.rem(view_index, count), lax.div(view_index, count), head_index])
     routes = (source_view, source_block, meta)
 
+    def flip(x, bits):
+        return lax.ppermute(x, "head", [(n, n ^ bits) for n in range(group)])
+
     def gathered(x):
-        return [x] + [
-            lax.ppermute(x, "head", [(n, n ^ bits) for n in range(group)])
-            for bits in range(1, group)
-        ]
+        parts = {0: x}
+        bits = group // 2
+        while bits:
+            for n, part in list(parts.items()):
+                parts[n + bits] = flip(part, bits)
+            bits //= 2
+        return [parts[n] for n in range(group)]
 
     def view_swap(x):
         return lax.all_to_all(x, "view", split_axis=0, concat_axis=0, tiled=True)
@@ -375,13 +378,26 @@
     full, rows_shape = whole(tokens, columns), shape_of(tokens, columns)
     one, one_shape = whole(half, 128), shape_of(half, 128)
     every, every_shape = whole(views, half, 128), shape_of(views, half, 128)
-    k = call(pack_k, (), (key_rows,), [full], every, every_shape)
+    groups = views // count
+    strip = pl.BlockSpec((tokens, 128), lambda i: (0, i))
+    duo = pl.BlockSpec((groups, 2, half, 128), lambda i: (0, i, 0, 0))
+    duo_shape = shape_of(groups, count, half, 128)
+
+    def packed(kernel, x):
+        out = call(kernel, (), (x,), [strip], duo, duo_shape, grid=(count // 2,))
+        return out.reshape(views, half, 128)
+
+    def totalled(kernel, x):
+        x = x.reshape(groups, count, half, 128)
+        return call(kernel, (), (x,), [duo], strip, rows_shape, grid=(count // 2,))
+
+    k = packed(pack_k, key_rows)
     k = view_swap(k)
     q = call(pack_q, (meta,), (query_rows,), [full], [one] * count, [one_shape] * count)
     q = send(q)
     og = gathered(out_grad)
-    v = call(pack_v, (), (value_rows,), [full], every, every_shape)
-    v = view_swap(v)
+    v = call(pack_v, (meta,), (value_rows,), [full], [one] * views, [one_shape] * views)
+    v = send(v)
     g = call(
         attended_grads,
         (meta,),
@@ -418,33 +434,33 @@
     *o, delta, dv = call(
         attend,
         routes,
-        (v, *g, e, l),
-        [HBM] * (1 + count) + [e_spec, row_spec],
+        (*v, *g, e, l),
+        [HBM] * (views + count) + [e_spec, row_spec],
         [one] * count + [row_spec, every],
         [one_shape] * count + [row_shape, every_shape],
         grid=(count,),
-        scratch=[held, mine, turned_scr, totals, pltpu.SemaphoreType.DMA((count + 1,))],
+        scratch=[held, mine, turned_scr, totals, pltpu.SemaphoreType.DMA((count + views,))],
         flops=unit * 3,
     )
     dv = view_swap(dv)
     o = send(o)
-    back = call(
+    *dq, dk = call(
         backward,
         routes,
-        (k, v, *q, *g, e, l, delta),
-        [HBM] * (2 + 2 * count) + [e_spec, row_spec, row_spec],
-        [one] * (count + views),
-        [one_shape] * (count + views),
+        (k, *v, *q, *g, e, l, delta),
+        [HBM] * (1 + views + 2 * count) + [e_spec, row_spec, row_spec],
+        [one] * count + [every],
+        [one_shape] * count + [every_shape],
         grid=(count,),
         scratch=[
             held, held, mine, mine, rows_scr, turned_scr,
             pltpu.VMEM((keys, half), BF16), pltpu.VMEM((keys, half), BF16),
-            totals, pltpu.SemaphoreType.DMA((2 * count + 2,)),
+            totals, pltpu.SemaphoreType.DMA((2 * count + 1 + views,)),
         ],
         flops=unit * 8,
     )
-    dk = send(back[count:])
-    dq = send(back[:count])
+    dk = view_swap(dk)
+    dq = send(dq)
 
     def collected(parts):
         return call(
@@ -462,12 +478,9 @@
         full,
         rows_shape,
     )
-    value_grad = call(total_v, (), (dv,), [every], full, rows_shape)
+    value_grad = totalled(total_v, dv)
     query_grad = collected(dq)
-    key_grad = call(
-        total_k, (meta,), tuple(dk), [HBM] * views, full, rows_shape,
-        scratch=[held, pltpu.SemaphoreType.DMA((views,))],
-    )
+    key_grad = totalled(total_k, dk)
     return mixed_out, query_grad, key_grad, value_grad
 
 

time: 192 us -> 218 us (1.14)
  blocking collectives: 0 us -> 28.7 us
  starting transfers between devices: 54.8 us -> 43.2 us
  waiting for transfers between devices: 48.7 us -> 57.7 us
    all_to_all x0 -> x1, blocking collectives: none -> 28.7 us  [view_swap(): return lax.all_to_all(x, 'view', split_axis=0, concat_axis=0, tiled=True)]
    all_to_all x3 -> x2, waiting for transfers between devices: 23.5 us -> 0.01 us  [view_swap(): return lax.all_to_all(x, 'view', split_axis=0, concat_axis=0, tiled=True)]
    ppermute x19, waiting for transfers between devices: 12.9 us -> 34.3 us  [send(): lax.ppermute(part, 'view', [(n, n ^ bits) for n in range(views)])]
    ppermute x6, waiting for transfers between devices: 12.3 us -> 23.4 us  [flip(): return lax.ppermute(x, 'head', [(n, n ^ bits) for n in range(group)])]
    all_to_all x3 -> x2, starting transfers between devices: 16.6 us -> 10.9 us  [view_swap(): return lax.all_to_all(x, 'view', split_axis=0, concat_axis=0, tiled=True)]
    ppermute x19, starting transfers between devices: 34 us -> 29.2 us  [send(): lax.ppermute(part, 'view', [(n, n ^ bits) for n in range(views)])]
    unnamed x50 -> x60, local copies, waits for them, and re-layouts: 6.46 us -> 6.36 us
  transfers between devices with their start and end apart: 28 -> 27, of which waited for: 6 -> 12; matrix products, arithmetic and copies ran while one was open for 0% -> 0% of each run, Pallas kernels for 31% -> 17%
where the time goes in v4:
time: 218 us; the launch traced here: 217 us
  Pallas kernels  79.8 us (37%)
  waiting for transfers between devices  57.7 us (26%)
  starting transfers between devices  43.2 us (20%)
  blocking collectives  28.7 us (13%)
  local copies, waits for them, and re-layouts  6.36 us (3%)
    pallas_call x12, Pallas kernels, call(): pl.pallas_call(kernel, grid_spec=pltpu.PrefetchScalarGridSpec(num_scalar_...  79.8 us
    ppermute x19, waiting for transfers between devices, send(): lax.ppermute(part, 'view', [(n, n ^ bits) for n in range(views)])  34.3 us
    ppermute x19, starting transfers between devices, send(): lax.ppermute(part, 'view', [(n, n ^ bits) for n in range(views)])  29.2 us
    all_to_all x1, blocking collectives, view_swap(): return lax.all_to_all(x, 'view', split_axis=0, concat_axis=0, tiled=True)  28.7 us
    ppermute x6, waiting for transfers between devices, flip(): return lax.ppermute(x, 'head', [(n, n ^ bits) for n in range(group)])  23.4 us
    all_to_all x2, starting transfers between devices, view_swap(): return lax.all_to_all(x, 'view', split_axis=0, concat_axis=0, tiled=True)  10.9 us
    unnamed x60, local copies, waits for them, and re-layouts  6.36 us
  transfers between devices with their start and end apart: 27, of which 12 were waited for; matrix products, arithmetic and copies ran while one was open for 0% of the time, Pallas kernels for 17%

profile of v4, /device:TPU:0, one launch (start us, length us, event | category | flops | bytes accessed | tf_op | source)
XLA Modules:
  0.0 217.4 jit_solution(2691200040987754342)
XLA Ops:
  0.6 2.1 shard_map.104
  2.8 7.3 %all-to-all-start = ((bf16[8,512,128]{2,1,0:T(8,128)(2,1)}), bf16[8,512,128]{2,1,0:T(8,128)(2,1)S(1)}, u32[]{:S(2)}, u32[]{:S(2)}) async-start(bf16[8,512,128]{2,1,0:T(8,128)(2,1)} %bitcast.6), calls=%async_computation | async-start | bytes 2097152 | tf_op jit(solution)/shard_map/all_to_all | solution.py:369
  11.6 12.1 %collective-permute-done.8.refs_1_ = bf16[1024,256]{1,0:T(8,128)(2,1)S(1)} collective-permute-done((bf16[1024,256]{1,0:T(8,128)(2,1)}, bf16[1024,256]{1,0:T(8,128)(2,1)S(1)}, u32[]{:S(2)}, u32[]{:S(2)}) %collective-permute-start.8) | collective-permute-done | bytes 524320 | tf_op jit(solution)/shard_map/ppermute | solution.py:357
  24.4 2.7 %shard_map.105 = (bf16[512,128]{1,0:T(8,128)(2,1)}, bf16[512,128]{1,0:T(8,128)(2,1)}, bf16[512,128]{1,0:T(8,128)(2,1)}, bf16[512,128]{1,0:T(8,128)(2,1)}) custom-call(s32[3]{0:T(128)} %pad_add_fusion.meta_ref, bf16[1024,256]{1,0:T(8,128)(2,1)} %x_ref.5), custom_call_target="tpu_custom_call" | custom-call | tf_op jit(solution)/shard_map/pallas_call | solution.py:36
  27.1 1.7 collective-permute-start.13
  30.6 3.2 %shard_map.102 = (bf16[512,128]{1,0:T(8,128)(2,1)}, bf16[512,128]{1,0:T(8,128)(2,1)}, bf16[512,128]{1,0:T(8,128)(2,1)}, bf16[512,128]{1,0:T(8,128)(2,1)}, bf16[5...) custom-call(s32[3]{0:T(128)} %pad_add_fusion.meta_ref, ...), custom_call_target="tpu_custom_call" | custom-call | tf_op jit(solution)/shard_map/pallas_call | solution.py:36
  34.2 2.3 %collective-permute-start = (bf16[512,128]{1,0:T(8,128)(2,1)}, bf16[512,128]{1,0:T(8,128)(2,1)S(1)}, u32[]{:S(2)}, u32[]{:S(2)}) collective-permute-start(bf16[512,128]{1,0:T(8,128)(2,1)} %get-tuple-element.34), channel_id=1, source_target_pairs={{0,4},{4,0},{8,12},{12,8},{16,20},{20,16},{24,28},{28,24},{1,5},{5... | collective-permute-start | bytes 393224 | tf_op jit(solution)/shard_map/ppermute | solution.py:373
  36.6 2.2 %collective-permute-done.14.refs_2_.refs_10_ = bf16[512,128]{1,0:T(8,128)(2,1)S(1)} collective-permute-done((bf16[512,128]{1,0:T(8,128)(2,1)}, bf16[512,128]{1,0:T(8,128)(2,1)S(1)}, u32[]{:S(2)}, u32[]{:S(2)}) %collective-permute-start.14) | collective-permute-done | bytes 131104 | tf_op jit(solution)/shard_map/ppermute | solution.py:373
  41.7 3.2 %collective-permute-start.3 = (bf16[512,128]{1,0:T(8,128)(2,1)}, bf16[512,128]{1,0:T(8,128)(2,1)S(1)}, u32[]{:S(2)}, u32[]{:S(2)}) collective-permute-start(bf16[512,128]{1,0:T(8,128)(2,1)} %get-tuple-element.37), channel_id=1, source_target_pairs={{0,16},{4,20},{8,24},{12,28},{16,0},{20,4},{24,8},{28,12},{1,17},{... | collective-permute-start | bytes 393224 | tf_op jit(solution)/shard_map/ppermute | solution.py:373
  46.1 4.1 %shard_map.103 = (bf16[512,128]{1,0:T(8,128)(2,1)}, bf16[512,128]{1,0:T(8,128)(2,1)}, bf16[512,128]{1,0:T(8,128)(2,1)}, bf16[512,128]{1,0:T(8,128)(2,1)}) custom-call(s32[3]{0:T(128)} %pad_add_fusion.meta_ref, bf16[1024,256]{1,0:T(8,128)(2,1)} %own_ref.1, bf16[1024,256]{1,0:T(8,128)(2,1)} %copy-done.3, bf16[1024,256]{1,0:T(8,128)(2,1)} %copy-done.2, ...), custom_call_target="tpu_custom_call" | custom-call | tf_op jit(solution)/shard_map/pallas_call | solution.py:36
  50.2 2.2 %collective-permute-start.5 = (bf16[512,128]{1,0:T(8,128)(2,1)}, bf16[512,128]{1,0:T(8,128)(2,1)S(1)}, u32[]{:S(2)}, u32[]{:S(2)}) collective-permute-start(bf16[512,128]{1,0:T(8,128)(2,1)} %get-tuple-element.39), channel_id=1, source_target_pairs={{0,24},{4,28},{8,16},{12,20},{16,8},{20,12},{24,0},{28,4},{1,25},{... | collective-permute-start | bytes 393224 | tf_op jit(solution)/shard_map/ppermute | solution.py:373
  52.5 2.0 collective-permute-start.6
  55.6 4.1 %collective-permute-start.11 = (bf16[512,128]{1,0:T(8,128)(2,1)}, bf16[512,128]{1,0:T(8,128)(2,1)S(1)}, u32[]{:S(2)}, u32[]{:S(2)}) collective-permute-start(bf16[512,128]{1,0:T(8,128)(2,1)} %get-tuple-element.43), channel_id=1, source_target_pairs={{0,8},{4,12},{8,0},{12,4},{16,24},{20,28},{24,16},{28,20},{1,9},{5... | collective-permute-start | bytes 393224 | tf_op jit(solution)/shard_map/ppermute | solution.py:373
  59.7 5.1 %collective-permute-done.4.refs_5_ = bf16[512,128]{1,0:T(8,128)(2,1)S(1)} collective-permute-done((bf16[512,128]{1,0:T(8,128)(2,1)}, bf16[512,128]{1,0:T(8,128)(2,1)S(1)}, u32[]{:S(2)}, u32[]{:S(2)}) %collective-permute-start.4) | collective-permute-done | bytes 131104 | tf_op jit(solution)/shard_map/ppermute | solution.py:373
  65.9 16.6 %shard_map.106 = (bf16[4,2,2048,512]{3,2,1,0:T(8,128)(2,1)}, f32[4,2,1,512]{3,2,1,0:T(1,128)}) custom-call(s32[8,16]{1,0:T(8,128)} %sv_ref.5, s32[8,16]{1,0:T(8,128)} %sb_ref.5, s32[3]{0:T(128)} %pad_add_fusion.meta_ref, bf16[8,512,128]{2,1,0:T(8,128)(2,1)} %copy-done.1, bf16[512,128]{1,0:T(8,128)(2,1)} %get-tuple-element.45.refs_0_.refs_8_, ...), custom_call_target="tpu_custom_call" | custom-call | flops 4294967296 | tf_op jit(solution)/shard_map/pallas_call | solution.py:36
  83.3 16.6 %shard_map.107 = (bf16[512,128]{1,0:T(8,128)(2,1)}, bf16[512,128]{1,0:T(8,128)(2,1)}, bf16[512,128]{1,0:T(8,128)(2,1)}, bf16[512,128]{1,0:T(8,128)(2,1)}, f32[4,...) custom-call(s32[8,16]{1,0:T(8,128)} %sv_ref.5, s32[8,16]{1,0:T(8,128)} %sb_ref.5, s32[3]{0:T(128)} %pad_add_fusion.meta_ref, ...), custom_call_target="tpu_custom_call" | custom-call | flops 3221225472 | tf_op jit(solution)/shard_map/pallas_call | solution.py:36
  99.9 21.0 %shard_map.110 = (bf16[512,128]{1,0:T(8,128)(2,1)}, bf16[512,128]{1,0:T(8,128)(2,1)}, bf16[512,128]{1,0:T(8,128)(2,1)}, bf16[512,128]{1,0:T(8,128)(2,1)}, bf16[8,512,128]{2,1,0:T(8,128)(2,1)}) custom-call(s32[8,16]{1,0:T(8,128)} %sv_ref.5, s32[8,16]{1,0:T(8,128)} %sb_ref.5, s32[3]{0:T(128)} %pad_add_fusion.meta_ref, bf16[8,512,128]{2,1,0:T(8,128)(2,1)} %copy-done.1, ...), custom_call_target="tpu_custom_call" | custom-call | flops 8589934592 | tf_op jit(solution)/shard_map/pallas_call | solution.py:36
  120.9 28.7 %all_to_all.15 = bf16[8,512,128]{2,1,0:T(8,128)(2,1)} all-to-all(bf16[8,512,128]{2,1,0:T(8,128)(2,1)} %get-tuple-element.60), channel_id=1, replica_groups=mesh['view'=8,'head'=4] {'view'}, dimensions={0} | all-to-all | bytes 2097152 | tf_op jit(solution)/shard_map/all_to_all | solution.py:369
  149.6 3.6 %all-to-all-start.2 = ((bf16[8,512,128]{2,1,0:T(8,128)(2,1)}), bf16[8,512,128]{2,1,0:T(8,128)(2,1)S(1)}, u32[]{:S(2)}, u32[]{:S(2)}) async-start(bf16[8,512,128]{2,1,0:T(8,128)(2,1)} %get-tuple-element.61), calls=%async_computation.2 | async-start | bytes 2097152 | tf_op jit(solution)/shard_map/all_to_all | solution.py:369
  153.2 2.0 collective-permute-start.16
  156.8 8.9 %collective-permute-done.16.refs_1_ = bf16[512,128]{1,0:T(8,128)(2,1)S(1)} collective-permute-done((bf16[512,128]{1,0:T(8,128)(2,1)S(1)}, bf16[512,128]{1,0:T(8,128)(2,1)S(1)}, u32[]{:S(2)}, u32[]{:S(2)}) %collective-permute-start.16) | collective-permute-done | bytes 131104 | tf_op jit(solution)/shard_map/ppermute | solution.py:373
  165.7 8.3 %collective-permute-done.17.refs_2_ = bf16[512,128]{1,0:T(8,128)(2,1)S(1)} collective-permute-done((bf16[512,128]{1,0:T(8,128)(2,1)S(1)}, bf16[512,128]{1,0:T(8,128)(2,1)S(1)}, u32[]{:S(2)}, u32[]{:S(2)}) %collective-permute-start.17) | collective-permute-done | bytes 131104 | tf_op jit(solution)/shard_map/ppermute | solution.py:373
  174.0 2.0 collective-permute-done.18.refs_3_
  176.7 2.8 %shard_map.108.refs_0_ = bf16[1024,256]{1,0:T(8,128)(2,1)} custom-call(s32[3]{0:T(128)} %pad_add_fusion.meta_ref, bf16[512,128]{1,0:T(8,128)(2,1)} %get-tuple-element.51.refs_0_, bf16[512,128]{1,0:T(8,128)(2,1)} %copy-done.18, bf16[512,128]{1,0:T(8,128)(2,1)} %copy-done.20, bf16[512,128]{1,0:T(8,128)(2,1)} %copy-done.22), custom_call_target="tpu_custom_call" | custom-call | tf_op jit(solution)/shard_map/pallas_call | solution.py:36
  181.1 11.3 %collective-permute-done.20.refs_2_ = bf16[1024,256]{1,0:T(8,128)(2,1)S(1)} collective-permute-done((bf16[1024,256]{1,0:T(8,128)(2,1)}, bf16[1024,256]{1,0:T(8,128)(2,1)S(1)}, u32[]{:S(2)}, u32[]{:S(2)}) %collective-permute-start.20) | collective-permute-done | bytes 524320 | tf_op jit(solution)/shard_map/ppermute | solution.py:357
  193.1 2.3 %collective-permute-start.23 = (bf16[512,128]{1,0:T(8,128)(2,1)}, bf16[512,128]{1,0:T(8,128)(2,1)S(1)}, u32[]{:S(2)}, u32[]{:S(2)}) collective-permute-start(bf16[512,128]{1,0:T(8,128)(2,1)} %get-tuple-element.58), channel_id=1, source_target_pairs={{0,8},{4,12},{8,0},{12,4},{16,24},{20,28},{24,16},{28,20},{1,9},{5... | collective-permute-start | bytes 393224 | tf_op jit(solution)/shard_map/ppermute | solution.py:373
  196.5 2.1 collective-permute-done.22.refs_1_
  199.7 3.7 %collective-permute-done.24.refs_3_ = bf16[512,128]{1,0:T(8,128)(2,1)S(1)} collective-permute-done((bf16[512,128]{1,0:T(8,128)(2,1)}, bf16[512,128]{1,0:T(8,128)(2,1)S(1)}, u32[]{:S(2)}, u32[]{:S(2)}) %collective-permute-start.24) | collective-permute-done | bytes 131104 | tf_op jit(solution)/shard_map/ppermute | solution.py:373
  204.0 2.8 %shard_map.111 = bf16[1024,256]{1,0:T(8,128)(2,1)} custom-call(s32[3]{0:T(128)} %pad_add_fusion.meta_ref, bf16[512,128]{1,0:T(8,128)(2,1)} %get-tuple-element.56.refs_0_, bf16[512,128]{1,0:T(8,128)(2,1)} %copy-done.19, bf16[512,128]{1,0:T(8,128)(2,1)} %copy-done.21, bf16[512,128]{1,0:T(8,128)(2,1)} %copy-done.23), custom_call_target="tpu_custom_call" | custom-call | tf_op jit(solution)/shard_map/pallas_call | solution.py:36
  208.4 3.8 %shard_map.109 = bf16[1024,256]{1,0:T(8,128)(2,1)} custom-call(s32[3]{0:T(128)} %pad_add_fusion.meta_ref, bf16[1024,256]{1,0:T(8,128)(2,1)} %shard_map.108.refs_0_, bf16[1024,256]{1,0:T(8,128)(2,1)} %copy-done.6, bf16[1024,256]{1,0:T(8,128)(2,1)} %copy-done.5, bf16[1024,256]{1,0:T(8,128)(2,1)} %copy-done.7, bf16[1024,1024]{1,0:T(8,128)(2,1)} %refs_4_.1), custom_call_target="tpu_custom_call" | custom-call | tf_op jit(solution)/shard_map/pallas_call | solution.py:36
  212.3 2.0 shard_map.112
  215.4 2.0 shard_map.113
  (96 shorter events, 21.5 us)
Async XLA Ops:
  2.8 62.1 %all-to-all-start = ((bf16[8,512,128]{2,1,0:T(8,128)(2,1)}), bf16[8,512,128]{2,1,0:T(8,128)(2,1)S(1)}, u32[]{:S(2)}, u32[]{:S(2)}) async-start(bf16[8,512,128]{2,1,0:T(8,128)(2,1)} %bitcast.6), calls=%async_computation | async-start | bytes 2097152 | tf_op jit(solution)/shard_map/all_to_all | solution.py:369
  10.1 13.6 %collective-permute-start.8 = (bf16[1024,256]{1,0:T(8,128)(2,1)}, bf16[1024,256]{1,0:T(8,128)(2,1)S(1)}, u32[]{:S(2)}, u32[]{:S(2)}) collective-permute-start(bf16[1024,256]{1,0:T(8,128)(2,1)} %own_ref.1), channel_id=1, source_target_pairs={{0,2},{1,3},{2,0},{3,1},{4,6},{5,7},{6,4},{7,5},{8,10},{9,11},{10,... | collective-permute-start | bytes 1572872 | tf_op jit(solution)/shard_map/ppermute | solution.py:357
  11.6 30.1 %collective-permute-start.7 = (bf16[1024,256]{1,0:T(8,128)(2,1)}, bf16[1024,256]{1,0:T(8,128)(2,1)S(1)}, u32[]{:S(2)}, u32[]{:S(2)}) collective-permute-start(bf16[1024,256]{1,0:T(8,128)(2,1)} %own_ref.1), channel_id=1, source_target_pairs={{0,1},{1,0},{2,3},{3,2},{4,5},{5,4},{6,7},{7,6},{8,9},{9,8},{10,11... | collective-permute-start | bytes 1572872 | tf_op jit(solution)/shard_map/ppermute | solution.py:357
  23.7 21.2 %collective-permute-start.9 = (bf16[1024,256]{1,0:T(8,128)(2,1)S(1)}, bf16[1024,256]{1,0:T(8,128)(2,1)S(1)}, u32[]{:S(2)}, u32[]{:S(2)}) collective-permute-start(bf16[1024,256]{1,0:T(8,128)(2,1)S(1)} %collective-permute-done.8.refs_1_), channel_id=1, source_target_pairs={{0,1},{1,0},{2,3},{3,2},{4,5},{5,4},{6,7},{7,6},{8,9},{9,8},{10,11... | collective-permute-start | bytes 1572872 | tf_op jit(solution)/shard_map/ppermute | solution.py:357
  27.1 7.1 %collective-permute-start.13 = (bf16[512,128]{1,0:T(8,128)(2,1)}, bf16[512,128]{1,0:T(8,128)(2,1)S(1)}, u32[]{:S(2)}, u32[]{:S(2)}) collective-permute-start(bf16[512,128]{1,0:T(8,128)(2,1)} %get-tuple-element.46), channel_id=1, source_target_pairs={{0,4},{4,0},{8,12},{12,8},{16,20},{20,16},{24,28},{28,24},{1,5},{5... | collective-permute-start | bytes 393224 | tf_op jit(solution)/shard_map/ppermute | solution.py:373
  28.9 9.9 %collective-permute-start.14 = (bf16[512,128]{1,0:T(8,128)(2,1)}, bf16[512,128]{1,0:T(8,128)(2,1)S(1)}, u32[]{:S(2)}, u32[]{:S(2)}) collective-permute-start(bf16[512,128]{1,0:T(8,128)(2,1)} %get-tuple-element.47), channel_id=1, source_target_pairs={{0,8},{4,12},{8,0},{12,4},{16,24},{20,28},{24,16},{28,20},{1,9},{5... | collective-permute-start | bytes 393224 | tf_op jit(solution)/shard_map/ppermute | solution.py:373
  30.3 9.7 %collective-permute-start.15 = (bf16[512,128]{1,0:T(8,128)(2,1)}, bf16[512,128]{1,0:T(8,128)(2,1)S(1)}, u32[]{:S(2)}, u32[]{:S(2)}) collective-permute-start(bf16[512,128]{1,0:T(8,128)(2,1)} %get-tuple-element.48), channel_id=1, source_target_pairs={{0,12},{4,8},{8,4},{12,0},{16,28},{20,24},{24,20},{28,16},{1,13},{... | collective-permute-start | bytes 393224 | tf_op jit(solution)/shard_map/ppermute | solution.py:373
  34.2 30.6 %copy-start.24 = (bf16[512,128]{1,0:T(8,128)(2,1)}, bf16[512,128]{1,0:T(8,128)(2,1)S(1)}, u32[]{:S(2)}) copy-start(bf16[512,128]{1,0:T(8,128)(2,1)S(1)} %collective-permute-done.13.refs_1_.refs_9_) | copy-start | bytes 393220
  34.2 16.0 %collective-permute-start = (bf16[512,128]{1,0:T(8,128)(2,1)}, bf16[512,128]{1,0:T(8,128)(2,1)S(1)}, u32[]{:S(2)}, u32[]{:S(2)}) collective-permute-start(bf16[512,128]{1,0:T(8,128)(2,1)} %get-tuple-element.34), channel_id=1, source_target_pairs={{0,4},{4,0},{8,12},{12,8},{16,20},{20,16},{24,28},{28,24},{1,5},{5... | collective-permute-start | bytes 393224 | tf_op jit(solution)/shard_map/ppermute | solution.py:373
  38.7 13.7 %collective-permute-start.1 = (bf16[512,128]{1,0:T(8,128)(2,1)}, bf16[512,128]{1,0:T(8,128)(2,1)S(1)}, u32[]{:S(2)}, u32[]{:S(2)}) collective-permute-start(bf16[512,128]{1,0:T(8,128)(2,1)} %get-tuple-element.35), channel_id=1, source_target_pairs={{0,8},{4,12},{8,0},{12,4},{16,24},{20,28},{24,16},{28,20},{1,9},{5... | collective-permute-start | bytes 393224 | tf_op jit(solution)/shard_map/ppermute | solution.py:373
  40.7 13.8 %collective-permute-start.2 = (bf16[512,128]{1,0:T(8,128)(2,1)}, bf16[512,128]{1,0:T(8,128)(2,1)S(1)}, u32[]{:S(2)}, u32[]{:S(2)}) collective-permute-start(bf16[512,128]{1,0:T(8,128)(2,1)} %get-tuple-element.36), channel_id=1, source_target_pairs={{0,12},{4,8},{8,4},{12,0},{16,28},{20,24},{24,20},{28,16},{1,13},{... | collective-permute-start | bytes 393224 | tf_op jit(solution)/shard_map/ppermute | solution.py:373
  41.7 13.9 %collective-permute-start.3 = (bf16[512,128]{1,0:T(8,128)(2,1)}, bf16[512,128]{1,0:T(8,128)(2,1)S(1)}, u32[]{:S(2)}, u32[]{:S(2)}) collective-permute-start(bf16[512,128]{1,0:T(8,128)(2,1)} %get-tuple-element.37), channel_id=1, source_target_pairs={{0,16},{4,20},{8,24},{12,28},{16,0},{20,4},{24,8},{28,12},{1,17},{... | collective-permute-start | bytes 393224 | tf_op jit(solution)/shard_map/ppermute | solution.py:373
  44.9 19.9 %collective-permute-start.4 = (bf16[512,128]{1,0:T(8,128)(2,1)}, bf16[512,128]{1,0:T(8,128)(2,1)S(1)}, u32[]{:S(2)}, u32[]{:S(2)}) collective-permute-start(bf16[512,128]{1,0:T(8,128)(2,1)} %get-tuple-element.38), channel_id=1, source_target_pairs={{0,20},{4,16},{8,28},{12,24},{16,4},{20,0},{24,12},{28,8},{1,21},{... | collective-permute-start | bytes 393224 | tf_op jit(solution)/shard_map/ppermute | solution.py:373
  50.2 32.3 %copy-start.8 = (bf16[512,128]{1,0:T(8,128)(2,1)}, bf16[512,128]{1,0:T(8,128)(2,1)S(1)}, u32[]{:S(2)}) copy-start(bf16[512,128]{1,0:T(8,128)(2,1)S(1)} %collective-permute-done.refs_1_) | copy-start | bytes 393220
  50.2 32.2 %collective-permute-start.5 = (bf16[512,128]{1,0:T(8,128)(2,1)}, bf16[512,128]{1,0:T(8,128)(2,1)S(1)}, u32[]{:S(2)}, u32[]{:S(2)}) collective-permute-start(bf16[512,128]{1,0:T(8,128)(2,1)} %get-tuple-element.39), channel_id=1, source_target_pairs={{0,24},{4,28},{8,16},{12,20},{16,8},{20,12},{24,0},{28,4},{1,25},{... | collective-permute-start | bytes 393224 | tf_op jit(solution)/shard_map/ppermute | solution.py:373
  52.5 30.0 %collective-permute-start.6 = (bf16[512,128]{1,0:T(8,128)(2,1)}, bf16[512,128]{1,0:T(8,128)(2,1)S(1)}, u32[]{:S(2)}, u32[]{:S(2)}) collective-permute-start(bf16[512,128]{1,0:T(8,128)(2,1)} %get-tuple-element.40), channel_id=1, source_target_pairs={{0,28},{4,24},{8,20},{12,16},{16,12},{20,8},{24,4},{28,0},{1,29},{... | collective-permute-start | bytes 393224 | tf_op jit(solution)/shard_map/ppermute | solution.py:373
  54.5 28.0 %collective-permute-start.10 = (bf16[512,128]{1,0:T(8,128)(2,1)}, bf16[512,128]{1,0:T(8,128)(2,1)S(1)}, u32[]{:S(2)}, u32[]{:S(2)}) collective-permute-start(bf16[512,128]{1,0:T(8,128)(2,1)} %get-tuple-element.42), channel_id=1, source_target_pairs={{0,4},{4,0},{8,12},{12,8},{16,20},{20,16},{24,28},{28,24},{1,5},{5... | collective-permute-start | bytes 393224 | tf_op jit(solution)/shard_map/ppermute | solution.py:373
  55.6 26.9 %collective-permute-start.11 = (bf16[512,128]{1,0:T(8,128)(2,1)}, bf16[512,128]{1,0:T(8,128)(2,1)S(1)}, u32[]{:S(2)}, u32[]{:S(2)}) collective-permute-start(bf16[512,128]{1,0:T(8,128)(2,1)} %get-tuple-element.43), channel_id=1, source_target_pairs={{0,8},{4,12},{8,0},{12,4},{16,24},{20,28},{24,16},{28,20},{1,9},{5... | collective-permute-start | bytes 393224 | tf_op jit(solution)/shard_map/ppermute | solution.py:373
  64.8 17.7 %collective-permute-start.12 = (bf16[512,128]{1,0:T(8,128)(2,1)}, bf16[512,128]{1,0:T(8,128)(2,1)S(1)}, u32[]{:S(2)}, u32[]{:S(2)}) collective-permute-start(bf16[512,128]{1,0:T(8,128)(2,1)} %get-tuple-element.44), channel_id=1, source_target_pairs={{0,12},{4,8},{8,4},{12,0},{16,28},{20,24},{24,20},{28,16},{1,13},{... | collective-permute-start | bytes 393224 | tf_op jit(solution)/shard_map/ppermute | solution.py:373
  99.9 53.3 %copy-start.29 = (bf16[512,128]{1,0:T(8,128)(2,1)S(1)}, bf16[512,128]{1,0:T(8,128)(2,1)}, u32[]{:S(2)}) copy-start(bf16[512,128]{1,0:T(8,128)(2,1)} %get-tuple-element.52) | copy-start | bytes 393220
  99.9 55.4 %copy-start.28 = (bf16[512,128]{1,0:T(8,128)(2,1)S(1)}, bf16[512,128]{1,0:T(8,128)(2,1)}, u32[]{:S(2)}) copy-start(bf16[512,128]{1,0:T(8,128)(2,1)} %get-tuple-element.53) | copy-start | bytes 393220
  99.9 56.8 %copy-start.27 = (bf16[512,128]{1,0:T(8,128)(2,1)S(1)}, bf16[512,128]{1,0:T(8,128)(2,1)}, u32[]{:S(2)}) copy-start(bf16[512,128]{1,0:T(8,128)(2,1)} %get-tuple-element.54) | copy-start | bytes 393220
  149.6 64.7 %all-to-all-start.2 = ((bf16[8,512,128]{2,1,0:T(8,128)(2,1)}), bf16[8,512,128]{2,1,0:T(8,128)(2,1)S(1)}, u32[]{:S(2)}, u32[]{:S(2)}) async-start(bf16[8,512,128]{2,1,0:T(8,128)(2,1)} %get-tuple-element.61), calls=%async_computation.2 | async-start | bytes 2097152 | tf_op jit(solution)/shard_map/all_to_all | solution.py:369
  153.2 12.5 %collective-permute-start.16 = (bf16[512,128]{1,0:T(8,128)(2,1)S(1)}, bf16[512,128]{1,0:T(8,128)(2,1)S(1)}, u32[]{:S(2)}, u32[]{:S(2)}) collective-permute-start(bf16[512,128]{1,0:T(8,128)(2,1)S(1)} %copy-done.29), channel_id=1, source_target_pairs={{0,4},{4,0},{8,12},{12,8},{16,20},{20,16},{24,28},{28,24},{1,5},{5... | collective-permute-start | bytes 393224 | tf_op jit(solution)/shard_map/ppermute | solution.py:373
  155.3 18.8 %collective-permute-start.17 = (bf16[512,128]{1,0:T(8,128)(2,1)S(1)}, bf16[512,128]{1,0:T(8,128)(2,1)S(1)}, u32[]{:S(2)}, u32[]{:S(2)}) collective-permute-start(bf16[512,128]{1,0:T(8,128)(2,1)S(1)} %copy-done.28), channel_id=1, source_target_pairs={{0,8},{4,12},{8,0},{12,4},{16,24},{20,28},{24,16},{28,20},{1,9},{5... | collective-permute-start | bytes 393224 | tf_op jit(solution)/shard_map/ppermute | solution.py:373
  156.7 19.3 %collective-permute-start.18 = (bf16[512,128]{1,0:T(8,128)(2,1)S(1)}, bf16[512,128]{1,0:T(8,128)(2,1)S(1)}, u32[]{:S(2)}, u32[]{:S(2)}) collective-permute-start(bf16[512,128]{1,0:T(8,128)(2,1)S(1)} %copy-done.27), channel_id=1, source_target_pairs={{0,12},{4,8},{8,4},{12,0},{16,28},{20,24},{24,20},{28,16},{1,13},{... | collective-permute-start | bytes 393224 | tf_op jit(solution)/shard_map/ppermute | solution.py:373
  179.5 12.9 %collective-permute-start.20 = (bf16[1024,256]{1,0:T(8,128)(2,1)}, bf16[1024,256]{1,0:T(8,128)(2,1)S(1)}, u32[]{:S(2)}, u32[]{:S(2)}) collective-permute-start(bf16[1024,256]{1,0:T(8,128)(2,1)} %shard_map.108.refs_0_), channel_id=1, source_target_pairs={{0,2},{1,3},{2,0},{3,1},{4,6},{5,7},{6,4},{7,5},{8,10},{9,11},{10,... | collective-permute-start | bytes 1572872 | tf_op jit(solution)/shard_map/ppermute | solution.py:357
  181.1 25.7 %collective-permute-start.19 = (bf16[1024,256]{1,0:T(8,128)(2,1)}, bf16[1024,256]{1,0:T(8,128)(2,1)S(1)}, u32[]{:S(2)}, u32[]{:S(2)}) collective-permute-start(bf16[1024,256]{1,0:T(8,128)(2,1)} %shard_map.108.refs_0_), channel_id=1, source_target_pairs={{0,1},{1,0},{2,3},{3,2},{4,5},{5,4},{6,7},{7,6},{8,9},{9,8},{10,11... | collective-permute-start | bytes 1572872 | tf_op jit(solution)/shard_map/ppermute | solution.py:357
  192.4 14.4 %collective-permute-start.21 = (bf16[1024,256]{1,0:T(8,128)(2,1)S(1)}, bf16[1024,256]{1,0:T(8,128)(2,1)S(1)}, u32[]{:S(2)}, u32[]{:S(2)}) collective-permute-start(bf16[1024,256]{1,0:T(8,128)(2,1)S(1)} %collective-permute-done.20.refs_2_), channel_id=1, source_target_pairs={{0,1},{1,0},{2,3},{3,2},{4,5},{5,4},{6,7},{7,6},{8,9},{9,8},{10,11... | collective-permute-start | bytes 1572872 | tf_op jit(solution)/shard_map/ppermute | solution.py:357
  192.4 6.1 %collective-permute-start.22 = (bf16[512,128]{1,0:T(8,128)(2,1)}, bf16[512,128]{1,0:T(8,128)(2,1)S(1)}, u32[]{:S(2)}, u32[]{:S(2)}) collective-permute-start(bf16[512,128]{1,0:T(8,128)(2,1)} %get-tuple-element.57), channel_id=1, source_target_pairs={{0,4},{4,0},{8,12},{12,8},{16,20},{20,16},{24,28},{28,24},{1,5},{5... | collective-permute-start | bytes 393224 | tf_op jit(solution)/shard_map/ppermute | solution.py:373
  193.1 6.6 %collective-permute-start.23 = (bf16[512,128]{1,0:T(8,128)(2,1)}, bf16[512,128]{1,0:T(8,128)(2,1)S(1)}, u32[]{:S(2)}, u32[]{:S(2)}) collective-permute-start(bf16[512,128]{1,0:T(8,128)(2,1)} %get-tuple-element.58), channel_id=1, source_target_pairs={{0,8},{4,12},{8,0},{12,4},{16,24},{20,28},{24,16},{28,20},{1,9},{5... | collective-permute-start | bytes 393224 | tf_op jit(solution)/shard_map/ppermute | solution.py:373
  195.4 8.0 %collective-permute-start.24 = (bf16[512,128]{1,0:T(8,128)(2,1)}, bf16[512,128]{1,0:T(8,128)(2,1)S(1)}, u32[]{:S(2)}, u32[]{:S(2)}) collective-permute-start(bf16[512,128]{1,0:T(8,128)(2,1)} %get-tuple-element.59), channel_id=1, source_target_pairs={{0,12},{4,8},{8,4},{12,0},{16,28},{20,24},{24,20},{28,16},{1,13},{... | collective-permute-start | bytes 393224 | tf_op jit(solution)/shard_map/ppermute | solution.py:373
  (25 other events, 201.9 us)

commit v5 on v4

--- a/solution.py
+++ b/solution.py
@@ -216,10 +216,12 @@
 
 
 def scores(sv_ref, sb_ref, meta_ref, k_ref, *refs):
-    count = len(refs) - 8
-    parts = refs[:count]
-    e_ref, l_ref, k_scr, q_scr, rows_scr, s0, s1, sem = refs[count:]
+    e_ref, l_ref, k_scr, q_scr, rows_scr, top_scr, s0, s1, sem = refs[-9:]
+    parts = refs[:-9]
+    count = len(parts)
     step = pl.program_id(0)
+    keys, queries = s0.shape
+    chunk = 128
 
     @pl.when(step == 0)
     def _():
@@ -228,36 +230,46 @@
             *(pltpu.make_async_copy(p, q_scr.at[n], sem.at[n]) for n, p in enumerate(parts)),
         )
 
-    view = meta_ref[1] * count + (meta_ref[0] ^ step)
-    gather(sv_ref, sb_ref, view, k_scr, rows_scr=rows_scr)
-    keys, queries = s0.shape
-    tops = []
-    for t, s_scr in zip(halves(q_scr[step]), (s0, s1)):
-        q = padded(t * jnp.asarray(SCALE, BF16))
+    def phase(old, new, q, n):
         top = None
-        for i in range(0, keys, STEP):
-            s = dot(rows_scr[i : i + STEP, :], q)
-            s_scr[i : i + STEP, :] = s
-            m = jnp.max(s.reshape(STEP // 8, 8, queries), axis=0)
-            top = m if top is None else jnp.maximum(top, m)
-        tops.append(jnp.max(top, axis=0, keepdims=True))
-    for n, (top, s_scr) in enumerate(zip(tops, (s0, s1))):
         total = None
-        for i in range(0, keys, STEP):
-            e = jnp.exp2((s_scr[i : i + STEP, :] - top) * LOG2E)
-            m = jnp.sum(e.reshape(STEP // 8, 8, queries), axis=0)
+        old_top = top_scr[...]
+        for i in range(0, keys, chunk):
+            rows = slice(i, i + chunk)
+            if q is not None:
+                s = dot(rows_scr[rows, :], q)
+                new[rows, :] = s
+                m = jnp.max(s.reshape(chunk // 8, 8, queries), axis=0)
+                top = m if top is None else jnp.maximum(top, m)
+            e = jnp.exp2((old[rows, :] - old_top) * LOG2E)
+            m = jnp.sum(e.reshape(chunk // 8, 8, queries), axis=0)
             total = m if total is None else total + m
-            e_ref[0, n, i : i + STEP, :] = e.astype(BF16)
+            e_ref[0, n, rows, :] = e.astype(BF16)
         l_ref[0, n] = jnp.sum(total, axis=0, keepdims=True)
+        if q is not None:
+            top_scr[...] = jnp.max(top, axis=0, keepdims=True)
+
+    @pl.when(step < count)
+    def _():
+        view = meta_ref[1] * count + (meta_ref[0] ^ step)
+        gather(sv_ref, sb_ref, view, k_scr, rows_scr=rows_scr)
+        first, second = [padded(t * jnp.asarray(SCALE, BF16)) for t in halves(q_scr[step])]
+        phase(s1, s0, first, 0)
+        phase(s0, s1, second, 1)
+
+    @pl.when(step == count)
+    def _():
+        phase(s1, None, None, 0)
 
 
 def attend(sv_ref, sb_ref, meta_ref, *refs):
     v_scr, g_scr, turned_scr, acc, sem = refs[-5:]
     count, views = g_scr.shape[0], v_scr.shape[0]
     v_parts, parts = refs[:views], refs[views : views + count]
-    e_ref, l_ref = refs[views + count : views + count + 2]
-    outs = refs[views + count + 2 : views + 2 * count + 2]
-    delta_ref, dv_ref = refs[views + 2 * count + 2 : -5]
+    e_refs = refs[views + count : views + count + 2]
+    l_refs = refs[views + count + 2 : views + count + 4]
+    outs = refs[views + count + 4 : views + 2 * count + 4]
+    delta_ref, dv_ref = refs[views + 2 * count + 4 : -5]
     step = pl.program_id(0)
 
     @pl.when(step == 0)
@@ -272,8 +284,9 @@
     gather(sv_ref, sb_ref, view, v_scr, turned_scr=turned_scr)
     out, grads = [], []
     for n, g in enumerate(halves(g_scr[step])):
-        o = (dot(turned_scr[...], e_ref[0, n]) / l_ref[0, n]).astype(BF16)
-        g = (g.astype(F32) / l_ref[0, n]).astype(BF16)
+        l = l_refs[n][0, 0]
+        o = (dot(turned_scr[...], e_refs[n][0, 0]) / l).astype(BF16)
+        g = (g.astype(F32) / l).astype(BF16)
         delta_ref[0, n] = jnp.sum(o.astype(F32) * g.astype(F32), axis=0, keepdims=True)
         out.append(o)
         grads.append(padded(g).T)
@@ -284,7 +297,7 @@
         def _():
             ref[...] = out
 
-    scatter(sv_ref, sb_ref, view, acc, (e_ref.at[0, 0], e_ref.at[0, 1]), grads)
+    scatter(sv_ref, sb_ref, view, acc, [e.at[0, 0] for e in e_refs], grads)
 
     @pl.when(step == count - 1)
     def _():
@@ -296,9 +309,10 @@
     count, views = q_scr.shape[0], v_scr.shape[0]
     v_parts, refs = refs[:views], refs[views:]
     q_parts, g_parts = refs[:count], refs[count : 2 * count]
-    e_ref, l_ref, delta_ref = refs[2 * count : 2 * count + 3]
-    outs = refs[2 * count + 3 : 3 * count + 3]
-    dk_ref = refs[3 * count + 3]
+    e_refs, l_refs = refs[2 * count : 2 * count + 2], refs[2 * count + 2 : 2 * count + 4]
+    delta_ref = refs[2 * count + 4]
+    outs = refs[2 * count + 5 : 3 * count + 5]
+    dk_ref = refs[3 * count + 5]
     step = pl.program_id(0)
 
     @pl.when(step == 0)
@@ -322,10 +336,10 @@
     keys = rows_scr.shape[0]
     queries = [padded(t * jnp.asarray(SCALE, BF16)).T for t in halves(q_scr[step])]
     for n, (g, ds_scr) in enumerate(zip(halves(g_scr[step]), (ds0, ds1))):
-        g = padded((g.astype(F32) / l_ref[0, n]).astype(BF16))
+        g = padded((g.astype(F32) / l_refs[n][0, 0]).astype(BF16))
         for i in range(0, keys, STEP):
             dp = dot(rows_scr[i : i + STEP, :], g)
-            e = e_ref[0, n, i : i + STEP, :].astype(F32)
+            e = e_refs[n][0, 0, i : i + STEP, :].astype(F32)
             ds_scr[i : i + STEP, :] = (e * (dp - delta_ref[0, n])).astype(BF16)
     scatter(sv_ref, sb_ref, view, acc, (ds0, ds1), queries)
     dq = [(dot(turned_scr[...], ds[...]) * SCALE).astype(BF16) for ds in (ds0, ds1)]
@@ -409,6 +423,14 @@
     )
     g = send(g)
     e_spec = pl.BlockSpec((1, 2, keys, half), lambda i, *_: (i, 0, 0, 0))
+    e_specs = [
+        pl.BlockSpec((1, 1, keys, half), lambda i, *_: (i, 1, 0, 0)),
+        pl.BlockSpec((1, 1, keys, half), lambda i, *_: (i + 1, 0, 0, 0)),
+    ]
+    l_specs = [
+        pl.BlockSpec((1, 1, 1, half), lambda i, *_: (i, 1, 0, 0)),
+        pl.BlockSpec((1, 1, 1, half), lambda i, *_: (i + 1, 0, 0, 0)),
+    ]
     row_spec = pl.BlockSpec((1, 2, 1, half), lambda i, *_: (i, 0, 0, 0))
     row_shape = shape_of(count, 2, 1, half, dtype=F32)
     unit = 2 * count * keys * tokens * HEAD_DIM
@@ -423,10 +445,10 @@
         (k, *q),
         [HBM] * (1 + count),
         [e_spec, row_spec],
-        [shape_of(count, 2, keys, half), row_shape],
-        grid=(count,),
+        [shape_of(count + 1, 2, keys, half), shape_of(count + 1, 2, 1, half, dtype=F32)],
+        grid=(count + 1,),
         scratch=[
-            held, mine, rows_scr, pltpu.VMEM((keys, half), F32), pltpu.VMEM((keys, half), F32),
+            held, mine, rows_scr, pltpu.VMEM((1, half), F32), pltpu.VMEM((keys, half), F32), pltpu.VMEM((keys, half), F32),
             pltpu.SemaphoreType.DMA((count + 1,)),
         ],
         flops=unit * 4,
@@ -434,8 +456,8 @@
     *o, delta, dv = call(
         attend,
         routes,
-        (*v, *g, e, l),
-        [HBM] * (views + count) + [e_spec, row_spec],
+        (*v, *g, e, e, l, l),
+        [HBM] * (views + count) + e_specs + l_specs,
         [one] * count + [row_spec, every],
         [one_shape] * count + [row_shape, every_shape],
         grid=(count,),
@@ -447,8 +469,8 @@
     *dq, dk = call(
         backward,
         routes,
-        (k, *v, *q, *g, e, l, delta),
-        [HBM] * (1 + views + 2 * count) + [e_spec, row_spec, row_spec],
+        (k, *v, *q, *g, e, e, l, l, delta),
+        [HBM] * (1 + views + 2 * count) + e_specs + l_specs + [row_spec],
         [one] * count + [every],
         [one_shape] * count + [every_shape],
         grid=(count,),

time: 218 us -> 217 us (level)
  no operation moved by 1% of the time
where the time goes in v5:
time: 217 us
  Pallas kernels  79 us (36%)
  waiting for transfers between devices  57.7 us (27%)
  starting transfers between devices  43.2 us (20%)
  blocking collectives  28.7 us (13%)
  local copies, waits for them, and re-layouts  6.35 us (3%)
    pallas_call x12, Pallas kernels, call(): pl.pallas_call(kernel, grid_spec=pltpu.PrefetchScalarGridSpec(num_scalar_...  79 us
    ppermute x19, waiting for transfers between devices, send(): lax.ppermute(part, 'view', [(n, n ^ bits) for n in range(views)])  34.3 us
    ppermute x19, starting transfers between devices, send(): lax.ppermute(part, 'view', [(n, n ^ bits) for n in range(views)])  29.2 us
    all_to_all x1, blocking collectives, view_swap(): return lax.all_to_all(x, 'view', split_axis=0, concat_axis=0, tiled=True)  28.7 us
    ppermute x6, waiting for transfers between devices, flip(): return lax.ppermute(x, 'head', [(n, n ^ bits) for n in range(group)])  23.4 us
    all_to_all x2, starting transfers between devices, view_swap(): return lax.all_to_all(x, 'view', split_axis=0, concat_axis=0, tiled=True)  10.9 us
    unnamed x60, local copies, waits for them, and re-layouts  6.35 us
  transfers between devices with their start and end apart: 27, of which 12 were waited for; matrix products, arithmetic and copies ran while one was open for 0% of the time, Pallas kernels for 17%

profile of v5, /device:TPU:0, one launch (start us, length us, event | category | flops | bytes accessed | tf_op | source)
XLA Modules:
  0.0 216.7 jit_solution(17610149452224767195)
XLA Ops:
  0.6 2.1 shard_map.104
  2.8 7.3 %all-to-all-start = ((bf16[8,512,128]{2,1,0:T(8,128)(2,1)}), bf16[8,512,128]{2,1,0:T(8,128)(2,1)S(1)}, u32[]{:S(2)}, u32[]{:S(2)}) async-start(bf16[8,512,128]{2,1,0:T(8,128)(2,1)} %bitcast.6), calls=%async_computation | async-start | bytes 2097152 | tf_op jit(solution)/shard_map/all_to_all | solution.py:383
  11.6 12.1 %collective-permute-done.8.refs_1_ = bf16[1024,256]{1,0:T(8,128)(2,1)S(1)} collective-permute-done((bf16[1024,256]{1,0:T(8,128)(2,1)}, bf16[1024,256]{1,0:T(8,128)(2,1)S(1)}, u32[]{:S(2)}, u32[]{:S(2)}) %collective-permute-start.8) | collective-permute-done | bytes 524320 | tf_op jit(solution)/shard_map/ppermute | solution.py:371
  24.4 2.7 %shard_map.105 = (bf16[512,128]{1,0:T(8,128)(2,1)}, bf16[512,128]{1,0:T(8,128)(2,1)}, bf16[512,128]{1,0:T(8,128)(2,1)}, bf16[512,128]{1,0:T(8,128)(2,1)}) custom-call(s32[3]{0:T(128)} %pad_add_fusion.meta_ref, bf16[1024,256]{1,0:T(8,128)(2,1)} %x_ref.5), custom_call_target="tpu_custom_call" | custom-call | tf_op jit(solution)/shard_map/pallas_call | solution.py:36
  27.1 1.7 collective-permute-start.13
  30.6 3.2 %shard_map.102 = (bf16[512,128]{1,0:T(8,128)(2,1)}, bf16[512,128]{1,0:T(8,128)(2,1)}, bf16[512,128]{1,0:T(8,128)(2,1)}, bf16[512,128]{1,0:T(8,128)(2,1)}, bf16[5...) custom-call(s32[3]{0:T(128)} %pad_add_fusion.meta_ref, ...), custom_call_target="tpu_custom_call" | custom-call | tf_op jit(solution)/shard_map/pallas_call | solution.py:36
  34.2 2.3 %collective-permute-start = (bf16[512,128]{1,0:T(8,128)(2,1)}, bf16[512,128]{1,0:T(8,128)(2,1)S(1)}, u32[]{:S(2)}, u32[]{:S(2)}) collective-permute-start(bf16[512,128]{1,0:T(8,128)(2,1)} %get-tuple-element.34), channel_id=1, source_target_pairs={{0,4},{4,0},{8,12},{12,8},{16,20},{20,16},{24,28},{28,24},{1,5},{5... | collective-permute-start | bytes 393224 | tf_op jit(solution)/shard_map/ppermute | solution.py:387
  36.5 2.2 %collective-permute-done.14.refs_2_.refs_10_ = bf16[512,128]{1,0:T(8,128)(2,1)S(1)} collective-permute-done((bf16[512,128]{1,0:T(8,128)(2,1)}, bf16[512,128]{1,0:T(8,128)(2,1)S(1)}, u32[]{:S(2)}, u32[]{:S(2)}) %collective-permute-start.14) | collective-permute-done | bytes 131104 | tf_op jit(solution)/shard_map/ppermute | solution.py:387
  41.7 3.2 %collective-permute-start.3 = (bf16[512,128]{1,0:T(8,128)(2,1)}, bf16[512,128]{1,0:T(8,128)(2,1)S(1)}, u32[]{:S(2)}, u32[]{:S(2)}) collective-permute-start(bf16[512,128]{1,0:T(8,128)(2,1)} %get-tuple-element.37), channel_id=1, source_target_pairs={{0,16},{4,20},{8,24},{12,28},{16,0},{20,4},{24,8},{28,12},{1,17},{... | collective-permute-start | bytes 393224 | tf_op jit(solution)/shard_map/ppermute | solution.py:387
  46.1 4.1 %shard_map.103 = (bf16[512,128]{1,0:T(8,128)(2,1)}, bf16[512,128]{1,0:T(8,128)(2,1)}, bf16[512,128]{1,0:T(8,128)(2,1)}, bf16[512,128]{1,0:T(8,128)(2,1)}) custom-call(s32[3]{0:T(128)} %pad_add_fusion.meta_ref, bf16[1024,256]{1,0:T(8,128)(2,1)} %own_ref.1, bf16[1024,256]{1,0:T(8,128)(2,1)} %copy-done.13, bf16[1024,256]{1,0:T(8,128)(2,1)} %copy-done.12, ...), custom_call_target="tpu_custom_call" | custom-call | tf_op jit(solution)/shard_map/pallas_call | solution.py:36
  50.2 2.2 %collective-permute-start.5 = (bf16[512,128]{1,0:T(8,128)(2,1)}, bf16[512,128]{1,0:T(8,128)(2,1)S(1)}, u32[]{:S(2)}, u32[]{:S(2)}) collective-permute-start(bf16[512,128]{1,0:T(8,128)(2,1)} %get-tuple-element.39), channel_id=1, source_target_pairs={{0,24},{4,28},{8,16},{12,20},{16,8},{20,12},{24,0},{28,4},{1,25},{... | collective-permute-start | bytes 393224 | tf_op jit(solution)/shard_map/ppermute | solution.py:387
  52.5 2.0 collective-permute-start.6
  55.6 4.1 %collective-permute-start.11 = (bf16[512,128]{1,0:T(8,128)(2,1)}, bf16[512,128]{1,0:T(8,128)(2,1)S(1)}, u32[]{:S(2)}, u32[]{:S(2)}) collective-permute-start(bf16[512,128]{1,0:T(8,128)(2,1)} %get-tuple-element.43), channel_id=1, source_target_pairs={{0,8},{4,12},{8,0},{12,4},{16,24},{20,28},{24,16},{28,20},{1,9},{5... | collective-permute-start | bytes 393224 | tf_op jit(solution)/shard_map/ppermute | solution.py:387
  59.7 5.1 %collective-permute-done.4.refs_5_ = bf16[512,128]{1,0:T(8,128)(2,1)S(1)} collective-permute-done((bf16[512,128]{1,0:T(8,128)(2,1)}, bf16[512,128]{1,0:T(8,128)(2,1)S(1)}, u32[]{:S(2)}, u32[]{:S(2)}) %collective-permute-start.4) | collective-permute-done | bytes 131104 | tf_op jit(solution)/shard_map/ppermute | solution.py:387
  65.8 15.4 %shard_map.106 = (bf16[5,2,2048,512]{3,2,1,0:T(8,128)(2,1)}, f32[5,2,1,512]{3,2,1,0:T(1,128)}) custom-call(s32[8,16]{1,0:T(8,128)} %sv_ref.5, s32[8,16]{1,0:T(8,128)} %sb_ref.5, s32[3]{0:T(128)} %pad_add_fusion.meta_ref, bf16[8,512,128]{2,1,0:T(8,128)(2,1)} %copy-done, bf16[512,128]{1,0:T(8,128)(2,1)} %get-tuple-element.45.refs_0_.refs_8_, ...), custom_call_target="tpu_custom_call" | custom-call | flops 4294967296 | tf_op jit(solution)/shard_map/pallas_call | solution.py:36
  82.2 16.7 %shard_map.107 = (bf16[512,128]{1,0:T(8,128)(2,1)}, bf16[512,128]{1,0:T(8,128)(2,1)}, bf16[512,128]{1,0:T(8,128)(2,1)}, bf16[512,128]{1,0:T(8,128)(2,1)}, f32[4,...) custom-call(s32[8,16]{1,0:T(8,128)} %sv_ref.5, s32[8,16]{1,0:T(8,128)} %sb_ref.5, s32[3]{0:T(128)} %pad_add_fusion.meta_ref, ...), custom_call_target="tpu_custom_call" | custom-call | flops 3221225472 | tf_op jit(solution)/shard_map/pallas_call | solution.py:36
  98.9 21.2 %shard_map.110 = (bf16[512,128]{1,0:T(8,128)(2,1)}, bf16[512,128]{1,0:T(8,128)(2,1)}, bf16[512,128]{1,0:T(8,128)(2,1)}, bf16[512,128]{1,0:T(8,128)(2,1)}, bf16[8,512,128]{2,1,0:T(8,128)(2,1)}) custom-call(s32[8,16]{1,0:T(8,128)} %sv_ref.5, s32[8,16]{1,0:T(8,128)} %sb_ref.5, s32[3]{0:T(128)} %pad_add_fusion.meta_ref, bf16[8,512,128]{2,1,0:T(8,128)(2,1)} %copy-done, ...), custom_call_target="tpu_custom_call" | custom-call | flops 8589934592 | tf_op jit(solution)/shard_map/pallas_call | solution.py:36
  120.2 28.7 %all_to_all.15 = bf16[8,512,128]{2,1,0:T(8,128)(2,1)} all-to-all(bf16[8,512,128]{2,1,0:T(8,128)(2,1)} %get-tuple-element.60), channel_id=1, replica_groups=mesh['view'=8,'head'=4] {'view'}, dimensions={0} | all-to-all | bytes 2097152 | tf_op jit(solution)/shard_map/all_to_all | solution.py:383
  148.9 3.6 %all-to-all-start.2 = ((bf16[8,512,128]{2,1,0:T(8,128)(2,1)}), bf16[8,512,128]{2,1,0:T(8,128)(2,1)S(1)}, u32[]{:S(2)}, u32[]{:S(2)}) async-start(bf16[8,512,128]{2,1,0:T(8,128)(2,1)} %get-tuple-element.61), calls=%async_computation.2 | async-start | bytes 2097152 | tf_op jit(solution)/shard_map/all_to_all | solution.py:383
  152.5 2.0 collective-permute-start.16
  156.0 8.9 %collective-permute-done.16.refs_1_ = bf16[512,128]{1,0:T(8,128)(2,1)S(1)} collective-permute-done((bf16[512,128]{1,0:T(8,128)(2,1)S(1)}, bf16[512,128]{1,0:T(8,128)(2,1)S(1)}, u32[]{:S(2)}, u32[]{:S(2)}) %collective-permute-start.16) | collective-permute-done | bytes 131104 | tf_op jit(solution)/shard_map/ppermute | solution.py:387
  165.0 8.3 %collective-permute-done.17.refs_2_ = bf16[512,128]{1,0:T(8,128)(2,1)S(1)} collective-permute-done((bf16[512,128]{1,0:T(8,128)(2,1)S(1)}, bf16[512,128]{1,0:T(8,128)(2,1)S(1)}, u32[]{:S(2)}, u32[]{:S(2)}) %collective-permute-start.17) | collective-permute-done | bytes 131104 | tf_op jit(solution)/shard_map/ppermute | solution.py:387
  173.3 2.0 collective-permute-done.18.refs_3_
  176.0 2.8 %shard_map.108.refs_0_ = bf16[1024,256]{1,0:T(8,128)(2,1)} custom-call(s32[3]{0:T(128)} %pad_add_fusion.meta_ref, bf16[512,128]{1,0:T(8,128)(2,1)} %get-tuple-element.51.refs_0_, bf16[512,128]{1,0:T(8,128)(2,1)} %copy-done.21, bf16[512,128]{1,0:T(8,128)(2,1)} %copy-done.23, bf16[512,128]{1,0:T(8,128)(2,1)} %copy-done.25), custom_call_target="tpu_custom_call" | custom-call | tf_op jit(solution)/shard_map/pallas_call | solution.py:36
  180.3 11.3 %collective-permute-done.20.refs_2_ = bf16[1024,256]{1,0:T(8,128)(2,1)S(1)} collective-permute-done((bf16[1024,256]{1,0:T(8,128)(2,1)}, bf16[1024,256]{1,0:T(8,128)(2,1)S(1)}, u32[]{:S(2)}, u32[]{:S(2)}) %collective-permute-start.20) | collective-permute-done | bytes 524320 | tf_op jit(solution)/shard_map/ppermute | solution.py:371
  192.3 2.3 %collective-permute-start.23 = (bf16[512,128]{1,0:T(8,128)(2,1)}, bf16[512,128]{1,0:T(8,128)(2,1)S(1)}, u32[]{:S(2)}, u32[]{:S(2)}) collective-permute-start(bf16[512,128]{1,0:T(8,128)(2,1)} %get-tuple-element.58), channel_id=1, source_target_pairs={{0,8},{4,12},{8,0},{12,4},{16,24},{20,28},{24,16},{28,20},{1,9},{5... | collective-permute-start | bytes 393224 | tf_op jit(solution)/shard_map/ppermute | solution.py:387
  195.7 2.1 collective-permute-done.22.refs_1_
  198.9 3.7 %collective-permute-done.24.refs_3_ = bf16[512,128]{1,0:T(8,128)(2,1)S(1)} collective-permute-done((bf16[512,128]{1,0:T(8,128)(2,1)}, bf16[512,128]{1,0:T(8,128)(2,1)S(1)}, u32[]{:S(2)}, u32[]{:S(2)}) %collective-permute-start.24) | collective-permute-done | bytes 131104 | tf_op jit(solution)/shard_map/ppermute | solution.py:387
  203.3 2.8 %shard_map.111 = bf16[1024,256]{1,0:T(8,128)(2,1)} custom-call(s32[3]{0:T(128)} %pad_add_fusion.meta_ref, bf16[512,128]{1,0:T(8,128)(2,1)} %get-tuple-element.56.refs_0_, bf16[512,128]{1,0:T(8,128)(2,1)} %copy-done.22, bf16[512,128]{1,0:T(8,128)(2,1)} %copy-done.24, bf16[512,128]{1,0:T(8,128)(2,1)} %copy-done.26), custom_call_target="tpu_custom_call" | custom-call | tf_op jit(solution)/shard_map/pallas_call | solution.py:36
  207.7 3.8 %shard_map.109 = bf16[1024,256]{1,0:T(8,128)(2,1)} custom-call(s32[3]{0:T(128)} %pad_add_fusion.meta_ref, bf16[1024,256]{1,0:T(8,128)(2,1)} %shard_map.108.refs_0_, bf16[1024,256]{1,0:T(8,128)(2,1)} %copy-done.16, bf16[1024,256]{1,0:T(8,128)(2,1)} %copy-done.15, bf16[1024,256]{1,0:T(8,128)(2,1)} %copy-done.17, bf16[1024,1024]{1,0:T(8,128)(2,1)} %refs_4_.1), custom_call_target="tpu_custom_call" | custom-call | tf_op jit(solution)/shard_map/pallas_call | solution.py:36
  211.5 2.0 shard_map.112
  214.6 2.0 shard_map.113
  (96 shorter events, 21.5 us)
Async XLA Ops:
  2.8 62.0 %all-to-all-start = ((bf16[8,512,128]{2,1,0:T(8,128)(2,1)}), bf16[8,512,128]{2,1,0:T(8,128)(2,1)S(1)}, u32[]{:S(2)}, u32[]{:S(2)}) async-start(bf16[8,512,128]{2,1,0:T(8,128)(2,1)} %bitcast.6), calls=%async_computation | async-start | bytes 2097152 | tf_op jit(solution)/shard_map/all_to_all | solution.py:383
  10.1 13.6 %collective-permute-start.8 = (bf16[1024,256]{1,0:T(8,128)(2,1)}, bf16[1024,256]{1,0:T(8,128)(2,1)S(1)}, u32[]{:S(2)}, u32[]{:S(2)}) collective-permute-start(bf16[1024,256]{1,0:T(8,128)(2,1)} %own_ref.1), channel_id=1, source_target_pairs={{0,2},{1,3},{2,0},{3,1},{4,6},{5,7},{6,4},{7,5},{8,10},{9,11},{10,... | collective-permute-start | bytes 1572872 | tf_op jit(solution)/shard_map/ppermute | solution.py:371
  11.6 30.1 %collective-permute-start.7 = (bf16[1024,256]{1,0:T(8,128)(2,1)}, bf16[1024,256]{1,0:T(8,128)(2,1)S(1)}, u32[]{:S(2)}, u32[]{:S(2)}) collective-permute-start(bf16[1024,256]{1,0:T(8,128)(2,1)} %own_ref.1), channel_id=1, source_target_pairs={{0,1},{1,0},{2,3},{3,2},{4,5},{5,4},{6,7},{7,6},{8,9},{9,8},{10,11... | collective-permute-start | bytes 1572872 | tf_op jit(solution)/shard_map/ppermute | solution.py:371
  23.7 21.2 %collective-permute-start.9 = (bf16[1024,256]{1,0:T(8,128)(2,1)S(1)}, bf16[1024,256]{1,0:T(8,128)(2,1)S(1)}, u32[]{:S(2)}, u32[]{:S(2)}) collective-permute-start(bf16[1024,256]{1,0:T(8,128)(2,1)S(1)} %collective-permute-done.8.refs_1_), channel_id=1, source_target_pairs={{0,1},{1,0},{2,3},{3,2},{4,5},{5,4},{6,7},{7,6},{8,9},{9,8},{10,11... | collective-permute-start | bytes 1572872 | tf_op jit(solution)/shard_map/ppermute | solution.py:371
  27.1 7.1 %collective-permute-start.13 = (bf16[512,128]{1,0:T(8,128)(2,1)}, bf16[512,128]{1,0:T(8,128)(2,1)S(1)}, u32[]{:S(2)}, u32[]{:S(2)}) collective-permute-start(bf16[512,128]{1,0:T(8,128)(2,1)} %get-tuple-element.46), channel_id=1, source_target_pairs={{0,4},{4,0},{8,12},{12,8},{16,20},{20,16},{24,28},{28,24},{1,5},{5... | collective-permute-start | bytes 393224 | tf_op jit(solution)/shard_map/ppermute | solution.py:387
  28.8 9.9 %collective-permute-start.14 = (bf16[512,128]{1,0:T(8,128)(2,1)}, bf16[512,128]{1,0:T(8,128)(2,1)S(1)}, u32[]{:S(2)}, u32[]{:S(2)}) collective-permute-start(bf16[512,128]{1,0:T(8,128)(2,1)} %get-tuple-element.47), channel_id=1, source_target_pairs={{0,8},{4,12},{8,0},{12,4},{16,24},{20,28},{24,16},{28,20},{1,9},{5... | collective-permute-start | bytes 393224 | tf_op jit(solution)/shard_map/ppermute | solution.py:387
  30.3 9.7 %collective-permute-start.15 = (bf16[512,128]{1,0:T(8,128)(2,1)}, bf16[512,128]{1,0:T(8,128)(2,1)S(1)}, u32[]{:S(2)}, u32[]{:S(2)}) collective-permute-start(bf16[512,128]{1,0:T(8,128)(2,1)} %get-tuple-element.48), channel_id=1, source_target_pairs={{0,12},{4,8},{8,4},{12,0},{16,28},{20,24},{24,20},{28,16},{1,13},{... | collective-permute-start | bytes 393224 | tf_op jit(solution)/shard_map/ppermute | solution.py:387
  34.2 30.6 %copy-start.18 = (bf16[512,128]{1,0:T(8,128)(2,1)}, bf16[512,128]{1,0:T(8,128)(2,1)S(1)}, u32[]{:S(2)}) copy-start(bf16[512,128]{1,0:T(8,128)(2,1)S(1)} %collective-permute-done.13.refs_1_.refs_9_) | copy-start | bytes 393220
  34.2 16.0 %collective-permute-start = (bf16[512,128]{1,0:T(8,128)(2,1)}, bf16[512,128]{1,0:T(8,128)(2,1)S(1)}, u32[]{:S(2)}, u32[]{:S(2)}) collective-permute-start(bf16[512,128]{1,0:T(8,128)(2,1)} %get-tuple-element.34), channel_id=1, source_target_pairs={{0,4},{4,0},{8,12},{12,8},{16,20},{20,16},{24,28},{28,24},{1,5},{5... | collective-permute-start | bytes 393224 | tf_op jit(solution)/shard_map/ppermute | solution.py:387
  38.7 13.7 %collective-permute-start.1 = (bf16[512,128]{1,0:T(8,128)(2,1)}, bf16[512,128]{1,0:T(8,128)(2,1)S(1)}, u32[]{:S(2)}, u32[]{:S(2)}) collective-permute-start(bf16[512,128]{1,0:T(8,128)(2,1)} %get-tuple-element.35), channel_id=1, source_target_pairs={{0,8},{4,12},{8,0},{12,4},{16,24},{20,28},{24,16},{28,20},{1,9},{5... | collective-permute-start | bytes 393224 | tf_op jit(solution)/shard_map/ppermute | solution.py:387
  40.7 13.8 %collective-permute-start.2 = (bf16[512,128]{1,0:T(8,128)(2,1)}, bf16[512,128]{1,0:T(8,128)(2,1)S(1)}, u32[]{:S(2)}, u32[]{:S(2)}) collective-permute-start(bf16[512,128]{1,0:T(8,128)(2,1)} %get-tuple-element.36), channel_id=1, source_target_pairs={{0,12},{4,8},{8,4},{12,0},{16,28},{20,24},{24,20},{28,16},{1,13},{... | collective-permute-start | bytes 393224 | tf_op jit(solution)/shard_map/ppermute | solution.py:387
  41.7 13.9 %collective-permute-start.3 = (bf16[512,128]{1,0:T(8,128)(2,1)}, bf16[512,128]{1,0:T(8,128)(2,1)S(1)}, u32[]{:S(2)}, u32[]{:S(2)}) collective-permute-start(bf16[512,128]{1,0:T(8,128)(2,1)} %get-tuple-element.37), channel_id=1, source_target_pairs={{0,16},{4,20},{8,24},{12,28},{16,0},{20,4},{24,8},{28,12},{1,17},{... | collective-permute-start | bytes 393224 | tf_op jit(solution)/shard_map/ppermute | solution.py:387
  44.9 19.9 %collective-permute-start.4 = (bf16[512,128]{1,0:T(8,128)(2,1)}, bf16[512,128]{1,0:T(8,128)(2,1)S(1)}, u32[]{:S(2)}, u32[]{:S(2)}) collective-permute-start(bf16[512,128]{1,0:T(8,128)(2,1)} %get-tuple-element.38), channel_id=1, source_target_pairs={{0,20},{4,16},{8,28},{12,24},{16,4},{20,0},{24,12},{28,8},{1,21},{... | collective-permute-start | bytes 393224 | tf_op jit(solution)/shard_map/ppermute | solution.py:387
  50.2 31.2 %copy-start.2 = (bf16[512,128]{1,0:T(8,128)(2,1)}, bf16[512,128]{1,0:T(8,128)(2,1)S(1)}, u32[]{:S(2)}) copy-start(bf16[512,128]{1,0:T(8,128)(2,1)S(1)} %collective-permute-done.refs_1_) | copy-start | bytes 393220
  50.2 31.1 %collective-permute-start.5 = (bf16[512,128]{1,0:T(8,128)(2,1)}, bf16[512,128]{1,0:T(8,128)(2,1)S(1)}, u32[]{:S(2)}, u32[]{:S(2)}) collective-permute-start(bf16[512,128]{1,0:T(8,128)(2,1)} %get-tuple-element.39), channel_id=1, source_target_pairs={{0,24},{4,28},{8,16},{12,20},{16,8},{20,12},{24,0},{28,4},{1,25},{... | collective-permute-start | bytes 393224 | tf_op jit(solution)/shard_map/ppermute | solution.py:387
  52.5 28.8 %collective-permute-start.6 = (bf16[512,128]{1,0:T(8,128)(2,1)}, bf16[512,128]{1,0:T(8,128)(2,1)S(1)}, u32[]{:S(2)}, u32[]{:S(2)}) collective-permute-start(bf16[512,128]{1,0:T(8,128)(2,1)} %get-tuple-element.40), channel_id=1, source_target_pairs={{0,28},{4,24},{8,20},{12,16},{16,12},{20,8},{24,4},{28,0},{1,29},{... | collective-permute-start | bytes 393224 | tf_op jit(solution)/shard_map/ppermute | solution.py:387
  54.5 26.9 %collective-permute-start.10 = (bf16[512,128]{1,0:T(8,128)(2,1)}, bf16[512,128]{1,0:T(8,128)(2,1)S(1)}, u32[]{:S(2)}, u32[]{:S(2)}) collective-permute-start(bf16[512,128]{1,0:T(8,128)(2,1)} %get-tuple-element.42), channel_id=1, source_target_pairs={{0,4},{4,0},{8,12},{12,8},{16,20},{20,16},{24,28},{28,24},{1,5},{5... | collective-permute-start | bytes 393224 | tf_op jit(solution)/shard_map/ppermute | solution.py:387
  55.6 25.8 %collective-permute-start.11 = (bf16[512,128]{1,0:T(8,128)(2,1)}, bf16[512,128]{1,0:T(8,128)(2,1)S(1)}, u32[]{:S(2)}, u32[]{:S(2)}) collective-permute-start(bf16[512,128]{1,0:T(8,128)(2,1)} %get-tuple-element.43), channel_id=1, source_target_pairs={{0,8},{4,12},{8,0},{12,4},{16,24},{20,28},{24,16},{28,20},{1,9},{5... | collective-permute-start | bytes 393224 | tf_op jit(solution)/shard_map/ppermute | solution.py:387
  64.8 16.6 %collective-permute-start.12 = (bf16[512,128]{1,0:T(8,128)(2,1)}, bf16[512,128]{1,0:T(8,128)(2,1)S(1)}, u32[]{:S(2)}, u32[]{:S(2)}) collective-permute-start(bf16[512,128]{1,0:T(8,128)(2,1)} %get-tuple-element.44), channel_id=1, source_target_pairs={{0,12},{4,8},{8,4},{12,0},{16,28},{20,24},{24,20},{28,16},{1,13},{... | collective-permute-start | bytes 393224 | tf_op jit(solution)/shard_map/ppermute | solution.py:387
  98.9 53.6 %copy-start.29 = (bf16[512,128]{1,0:T(8,128)(2,1)S(1)}, bf16[512,128]{1,0:T(8,128)(2,1)}, u32[]{:S(2)}) copy-start(bf16[512,128]{1,0:T(8,128)(2,1)} %get-tuple-element.52) | copy-start | bytes 393220
  98.9 55.6 %copy-start.28 = (bf16[512,128]{1,0:T(8,128)(2,1)S(1)}, bf16[512,128]{1,0:T(8,128)(2,1)}, u32[]{:S(2)}) copy-start(bf16[512,128]{1,0:T(8,128)(2,1)} %get-tuple-element.53) | copy-start | bytes 393220
  98.9 57.1 %copy-start.27 = (bf16[512,128]{1,0:T(8,128)(2,1)S(1)}, bf16[512,128]{1,0:T(8,128)(2,1)}, u32[]{:S(2)}) copy-start(bf16[512,128]{1,0:T(8,128)(2,1)} %get-tuple-element.54) | copy-start | bytes 393220
  148.9 64.7 %all-to-all-start.2 = ((bf16[8,512,128]{2,1,0:T(8,128)(2,1)}), bf16[8,512,128]{2,1,0:T(8,128)(2,1)S(1)}, u32[]{:S(2)}, u32[]{:S(2)}) async-start(bf16[8,512,128]{2,1,0:T(8,128)(2,1)} %get-tuple-element.61), calls=%async_computation.2 | async-start | bytes 2097152 | tf_op jit(solution)/shard_map/all_to_all | solution.py:383
  152.5 12.5 %collective-permute-start.16 = (bf16[512,128]{1,0:T(8,128)(2,1)S(1)}, bf16[512,128]{1,0:T(8,128)(2,1)S(1)}, u32[]{:S(2)}, u32[]{:S(2)}) collective-permute-start(bf16[512,128]{1,0:T(8,128)(2,1)S(1)} %copy-done.29), channel_id=1, source_target_pairs={{0,4},{4,0},{8,12},{12,8},{16,20},{20,16},{24,28},{28,24},{1,5},{5... | collective-permute-start | bytes 393224 | tf_op jit(solution)/shard_map/ppermute | solution.py:387
  154.5 18.8 %collective-permute-start.17 = (bf16[512,128]{1,0:T(8,128)(2,1)S(1)}, bf16[512,128]{1,0:T(8,128)(2,1)S(1)}, u32[]{:S(2)}, u32[]{:S(2)}) collective-permute-start(bf16[512,128]{1,0:T(8,128)(2,1)S(1)} %copy-done.28), channel_id=1, source_target_pairs={{0,8},{4,12},{8,0},{12,4},{16,24},{20,28},{24,16},{28,20},{1,9},{5... | collective-permute-start | bytes 393224 | tf_op jit(solution)/shard_map/ppermute | solution.py:387
  156.0 19.3 %collective-permute-start.18 = (bf16[512,128]{1,0:T(8,128)(2,1)S(1)}, bf16[512,128]{1,0:T(8,128)(2,1)S(1)}, u32[]{:S(2)}, u32[]{:S(2)}) collective-permute-start(bf16[512,128]{1,0:T(8,128)(2,1)S(1)} %copy-done.27), channel_id=1, source_target_pairs={{0,12},{4,8},{8,4},{12,0},{16,28},{20,24},{24,20},{28,16},{1,13},{... | collective-permute-start | bytes 393224 | tf_op jit(solution)/shard_map/ppermute | solution.py:387
  178.8 12.9 %collective-permute-start.20 = (bf16[1024,256]{1,0:T(8,128)(2,1)}, bf16[1024,256]{1,0:T(8,128)(2,1)S(1)}, u32[]{:S(2)}, u32[]{:S(2)}) collective-permute-start(bf16[1024,256]{1,0:T(8,128)(2,1)} %shard_map.108.refs_0_), channel_id=1, source_target_pairs={{0,2},{1,3},{2,0},{3,1},{4,6},{5,7},{6,4},{7,5},{8,10},{9,11},{10,... | collective-permute-start | bytes 1572872 | tf_op jit(solution)/shard_map/ppermute | solution.py:371
  180.3 25.8 %collective-permute-start.19 = (bf16[1024,256]{1,0:T(8,128)(2,1)}, bf16[1024,256]{1,0:T(8,128)(2,1)S(1)}, u32[]{:S(2)}, u32[]{:S(2)}) collective-permute-start(bf16[1024,256]{1,0:T(8,128)(2,1)} %shard_map.108.refs_0_), channel_id=1, source_target_pairs={{0,1},{1,0},{2,3},{3,2},{4,5},{5,4},{6,7},{7,6},{8,9},{9,8},{10,11... | collective-permute-start | bytes 1572872 | tf_op jit(solution)/shard_map/ppermute | solution.py:371
  191.7 14.5 %collective-permute-start.21 = (bf16[1024,256]{1,0:T(8,128)(2,1)S(1)}, bf16[1024,256]{1,0:T(8,128)(2,1)S(1)}, u32[]{:S(2)}, u32[]{:S(2)}) collective-permute-start(bf16[1024,256]{1,0:T(8,128)(2,1)S(1)} %collective-permute-done.20.refs_2_), channel_id=1, source_target_pairs={{0,1},{1,0},{2,3},{3,2},{4,5},{5,4},{6,7},{7,6},{8,9},{9,8},{10,11... | collective-permute-start | bytes 1572872 | tf_op jit(solution)/shard_map/ppermute | solution.py:371
  191.7 6.1 %collective-permute-start.22 = (bf16[512,128]{1,0:T(8,128)(2,1)}, bf16[512,128]{1,0:T(8,128)(2,1)S(1)}, u32[]{:S(2)}, u32[]{:S(2)}) collective-permute-start(bf16[512,128]{1,0:T(8,128)(2,1)} %get-tuple-element.57), channel_id=1, source_target_pairs={{0,4},{4,0},{8,12},{12,8},{16,20},{20,16},{24,28},{28,24},{1,5},{5... | collective-permute-start | bytes 393224 | tf_op jit(solution)/shard_map/ppermute | solution.py:387
  192.3 6.6 %collective-permute-start.23 = (bf16[512,128]{1,0:T(8,128)(2,1)}, bf16[512,128]{1,0:T(8,128)(2,1)S(1)}, u32[]{:S(2)}, u32[]{:S(2)}) collective-permute-start(bf16[512,128]{1,0:T(8,128)(2,1)} %get-tuple-element.58), channel_id=1, source_target_pairs={{0,8},{4,12},{8,0},{12,4},{16,24},{20,28},{24,16},{28,20},{1,9},{5... | collective-permute-start | bytes 393224 | tf_op jit(solution)/shard_map/ppermute | solution.py:387
  194.6 8.0 %collective-permute-start.24 = (bf16[512,128]{1,0:T(8,128)(2,1)}, bf16[512,128]{1,0:T(8,128)(2,1)S(1)}, u32[]{:S(2)}, u32[]{:S(2)}) collective-permute-start(bf16[512,128]{1,0:T(8,128)(2,1)} %get-tuple-element.59), channel_id=1, source_target_pairs={{0,12},{4,8},{8,4},{12,0},{16,28},{20,24},{24,20},{28,16},{1,13},{... | collective-permute-start | bytes 393224 | tf_op jit(solution)/shard_map/ppermute | solution.py:387
  (25 other events, 197.3 us)

commit v6 on v5

--- a/solution.py
+++ b/solution.py
@@ -76,11 +76,13 @@
 def fold_each(meta_ref, x_ref, outs):
     rows = x_ref.shape[0]
     count = x_ref.shape[1] // HEAD_DIM
-    for n, out in enumerate(outs):
-        head = meta_ref[0] ^ (n % count)
+    for n in range(count):
+        head = meta_ref[0] ^ n
         pair = aligned(head // 2, 128)
         top, low = x_ref[: rows // 2, pair], x_ref[rows // 2 :, pair]
-        out[...] = jnp.where(head % 2 == 1, join_high(top, low), join(top, low))
+        folded = jnp.where(head % 2 == 1, join_high(top, low), join(top, low))
+        for out in outs[n::count]:
+            out[...] = folded
 
 
 def pack_k(x_ref, out_ref):

time: 217 us -> 217 us (level)
  no operation moved by 1% of the time
where the time goes in v6:
time: 217 us
  Pallas kernels  78.7 us (36%)
  waiting for transfers between devices  58.1 us (27%)
  starting transfers between devices  43.2 us (20%)
  blocking collectives  28.7 us (13%)
  local copies, waits for them, and re-layouts  6.35 us (3%)
    pallas_call x12, Pallas kernels, call(): pl.pallas_call(kernel, grid_spec=pltpu.PrefetchScalarGridSpec(num_scalar_...  78.7 us
    ppermute x19, waiting for transfers between devices, send(): lax.ppermute(part, 'view', [(n, n ^ bits) for n in range(views)])  34.6 us
    ppermute x19, starting transfers between devices, send(): lax.ppermute(part, 'view', [(n, n ^ bits) for n in range(views)])  29.2 us
    all_to_all x1, blocking collectives, view_swap(): return lax.all_to_all(x, 'view', split_axis=0, concat_axis=0, tiled=True)  28.7 us
    ppermute x6, waiting for transfers between devices, flip(): return lax.ppermute(x, 'head', [(n, n ^ bits) for n in range(group)])  23.4 us
    all_to_all x2, starting transfers between devices, view_swap(): return lax.all_to_all(x, 'view', split_axis=0, concat_axis=0, tiled=True)  10.9 us
    unnamed x60, local copies, waits for them, and re-layouts  6.35 us
  transfers between devices with their start and end apart: 27, of which 12 were waited for; matrix products, arithmetic and copies ran while one was open for 0% of the time, Pallas kernels for 17%

profile of v6, /device:TPU:0, one launch (start us, length us, event | category | flops | bytes accessed | tf_op | source)
XLA Modules:
  0.0 216.7 jit_solution(14610390173643621202)
XLA Ops:
  0.6 2.1 shard_map.104
  2.8 7.3 %all-to-all-start = ((bf16[8,512,128]{2,1,0:T(8,128)(2,1)}), bf16[8,512,128]{2,1,0:T(8,128)(2,1)S(1)}, u32[]{:S(2)}, u32[]{:S(2)}) async-start(bf16[8,512,128]{2,1,0:T(8,128)(2,1)} %bitcast.6), calls=%async_computation | async-start | bytes 2097152 | tf_op jit(solution)/shard_map/all_to_all | solution.py:385
  11.6 12.1 %collective-permute-done.8.refs_1_ = bf16[1024,256]{1,0:T(8,128)(2,1)S(1)} collective-permute-done((bf16[1024,256]{1,0:T(8,128)(2,1)}, bf16[1024,256]{1,0:T(8,128)(2,1)S(1)}, u32[]{:S(2)}, u32[]{:S(2)}) %collective-permute-start.8) | collective-permute-done | bytes 524320 | tf_op jit(solution)/shard_map/ppermute | solution.py:373
  24.4 2.7 %shard_map.105 = (bf16[512,128]{1,0:T(8,128)(2,1)}, bf16[512,128]{1,0:T(8,128)(2,1)}, bf16[512,128]{1,0:T(8,128)(2,1)}, bf16[512,128]{1,0:T(8,128)(2,1)}) custom-call(s32[3]{0:T(128)} %pad_add_fusion.meta_ref, bf16[1024,256]{1,0:T(8,128)(2,1)} %x_ref.5), custom_call_target="tpu_custom_call" | custom-call | tf_op jit(solution)/shard_map/pallas_call | solution.py:36
  27.1 1.7 collective-permute-start.13
  30.6 2.9 %shard_map.102 = (bf16[512,128]{1,0:T(8,128)(2,1)}, bf16[512,128]{1,0:T(8,128)(2,1)}, bf16[512,128]{1,0:T(8,128)(2,1)}, bf16[512,128]{1,0:T(8,128)(2,1)}, bf16[5...) custom-call(s32[3]{0:T(128)} %pad_add_fusion.meta_ref, ...), custom_call_target="tpu_custom_call" | custom-call | tf_op jit(solution)/shard_map/pallas_call | solution.py:36
  34.2 2.3 %collective-permute-start = (bf16[512,128]{1,0:T(8,128)(2,1)}, bf16[512,128]{1,0:T(8,128)(2,1)S(1)}, u32[]{:S(2)}, u32[]{:S(2)}) collective-permute-start(bf16[512,128]{1,0:T(8,128)(2,1)} %get-tuple-element.34), channel_id=1, source_target_pairs={{0,4},{4,0},{8,12},{12,8},{16,20},{20,16},{24,28},{28,24},{1,5},{5... | collective-permute-start | bytes 393224 | tf_op jit(solution)/shard_map/ppermute | solution.py:389
  36.5 2.2 %collective-permute-done.14.refs_2_.refs_10_ = bf16[512,128]{1,0:T(8,128)(2,1)S(1)} collective-permute-done((bf16[512,128]{1,0:T(8,128)(2,1)}, bf16[512,128]{1,0:T(8,128)(2,1)S(1)}, u32[]{:S(2)}, u32[]{:S(2)}) %collective-permute-start.14) | collective-permute-done | bytes 131104 | tf_op jit(solution)/shard_map/ppermute | solution.py:389
  41.7 3.2 %collective-permute-start.3 = (bf16[512,128]{1,0:T(8,128)(2,1)}, bf16[512,128]{1,0:T(8,128)(2,1)S(1)}, u32[]{:S(2)}, u32[]{:S(2)}) collective-permute-start(bf16[512,128]{1,0:T(8,128)(2,1)} %get-tuple-element.37), channel_id=1, source_target_pairs={{0,16},{4,20},{8,24},{12,28},{16,0},{20,4},{24,8},{28,12},{1,17},{... | collective-permute-start | bytes 393224 | tf_op jit(solution)/shard_map/ppermute | solution.py:389
  46.1 4.1 %shard_map.103 = (bf16[512,128]{1,0:T(8,128)(2,1)}, bf16[512,128]{1,0:T(8,128)(2,1)}, bf16[512,128]{1,0:T(8,128)(2,1)}, bf16[512,128]{1,0:T(8,128)(2,1)}) custom-call(s32[3]{0:T(128)} %pad_add_fusion.meta_ref, bf16[1024,256]{1,0:T(8,128)(2,1)} %own_ref.1, bf16[1024,256]{1,0:T(8,128)(2,1)} %copy-done.13, bf16[1024,256]{1,0:T(8,128)(2,1)} %copy-done.12, ...), custom_call_target="tpu_custom_call" | custom-call | tf_op jit(solution)/shard_map/pallas_call | solution.py:36
  50.2 2.2 %collective-permute-start.5 = (bf16[512,128]{1,0:T(8,128)(2,1)}, bf16[512,128]{1,0:T(8,128)(2,1)S(1)}, u32[]{:S(2)}, u32[]{:S(2)}) collective-permute-start(bf16[512,128]{1,0:T(8,128)(2,1)} %get-tuple-element.39), channel_id=1, source_target_pairs={{0,24},{4,28},{8,16},{12,20},{16,8},{20,12},{24,0},{28,4},{1,25},{... | collective-permute-start | bytes 393224 | tf_op jit(solution)/shard_map/ppermute | solution.py:389
  52.5 2.0 collective-permute-start.6
  55.6 4.1 %collective-permute-start.11 = (bf16[512,128]{1,0:T(8,128)(2,1)}, bf16[512,128]{1,0:T(8,128)(2,1)S(1)}, u32[]{:S(2)}, u32[]{:S(2)}) collective-permute-start(bf16[512,128]{1,0:T(8,128)(2,1)} %get-tuple-element.43), channel_id=1, source_target_pairs={{0,8},{4,12},{8,0},{12,4},{16,24},{20,28},{24,16},{28,20},{1,9},{5... | collective-permute-start | bytes 393224 | tf_op jit(solution)/shard_map/ppermute | solution.py:389
  59.7 5.1 %collective-permute-done.4.refs_5_ = bf16[512,128]{1,0:T(8,128)(2,1)S(1)} collective-permute-done((bf16[512,128]{1,0:T(8,128)(2,1)}, bf16[512,128]{1,0:T(8,128)(2,1)S(1)}, u32[]{:S(2)}, u32[]{:S(2)}) %collective-permute-start.4) | collective-permute-done | bytes 131104 | tf_op jit(solution)/shard_map/ppermute | solution.py:389
  65.8 15.4 %shard_map.106 = (bf16[5,2,2048,512]{3,2,1,0:T(8,128)(2,1)}, f32[5,2,1,512]{3,2,1,0:T(1,128)}) custom-call(s32[8,16]{1,0:T(8,128)} %sv_ref.5, s32[8,16]{1,0:T(8,128)} %sb_ref.5, s32[3]{0:T(128)} %pad_add_fusion.meta_ref, bf16[8,512,128]{2,1,0:T(8,128)(2,1)} %copy-done, bf16[512,128]{1,0:T(8,128)(2,1)} %get-tuple-element.45.refs_0_.refs_8_, ...), custom_call_target="tpu_custom_call" | custom-call | flops 4294967296 | tf_op jit(solution)/shard_map/pallas_call | solution.py:36
  82.2 16.7 %shard_map.107 = (bf16[512,128]{1,0:T(8,128)(2,1)}, bf16[512,128]{1,0:T(8,128)(2,1)}, bf16[512,128]{1,0:T(8,128)(2,1)}, bf16[512,128]{1,0:T(8,128)(2,1)}, f32[4,...) custom-call(s32[8,16]{1,0:T(8,128)} %sv_ref.5, s32[8,16]{1,0:T(8,128)} %sb_ref.5, s32[3]{0:T(128)} %pad_add_fusion.meta_ref, ...), custom_call_target="tpu_custom_call" | custom-call | flops 3221225472 | tf_op jit(solution)/shard_map/pallas_call | solution.py:36
  98.9 21.2 %shard_map.110 = (bf16[512,128]{1,0:T(8,128)(2,1)}, bf16[512,128]{1,0:T(8,128)(2,1)}, bf16[512,128]{1,0:T(8,128)(2,1)}, bf16[512,128]{1,0:T(8,128)(2,1)}, bf16[8,512,128]{2,1,0:T(8,128)(2,1)}) custom-call(s32[8,16]{1,0:T(8,128)} %sv_ref.5, s32[8,16]{1,0:T(8,128)} %sb_ref.5, s32[3]{0:T(128)} %pad_add_fusion.meta_ref, bf16[8,512,128]{2,1,0:T(8,128)(2,1)} %copy-done, ...), custom_call_target="tpu_custom_call" | custom-call | flops 8589934592 | tf_op jit(solution)/shard_map/pallas_call | solution.py:36
  120.2 28.7 %all_to_all.15 = bf16[8,512,128]{2,1,0:T(8,128)(2,1)} all-to-all(bf16[8,512,128]{2,1,0:T(8,128)(2,1)} %get-tuple-element.60), channel_id=1, replica_groups=mesh['view'=8,'head'=4] {'view'}, dimensions={0} | all-to-all | bytes 2097152 | tf_op jit(solution)/shard_map/all_to_all | solution.py:385
  148.9 3.6 %all-to-all-start.2 = ((bf16[8,512,128]{2,1,0:T(8,128)(2,1)}), bf16[8,512,128]{2,1,0:T(8,128)(2,1)S(1)}, u32[]{:S(2)}, u32[]{:S(2)}) async-start(bf16[8,512,128]{2,1,0:T(8,128)(2,1)} %get-tuple-element.61), calls=%async_computation.2 | async-start | bytes 2097152 | tf_op jit(solution)/shard_map/all_to_all | solution.py:385
  152.5 2.0 collective-permute-start.16
  156.0 8.9 %collective-permute-done.16.refs_1_ = bf16[512,128]{1,0:T(8,128)(2,1)S(1)} collective-permute-done((bf16[512,128]{1,0:T(8,128)(2,1)S(1)}, bf16[512,128]{1,0:T(8,128)(2,1)S(1)}, u32[]{:S(2)}, u32[]{:S(2)}) %collective-permute-start.16) | collective-permute-done | bytes 131104 | tf_op jit(solution)/shard_map/ppermute | solution.py:389
  165.0 8.3 %collective-permute-done.17.refs_2_ = bf16[512,128]{1,0:T(8,128)(2,1)S(1)} collective-permute-done((bf16[512,128]{1,0:T(8,128)(2,1)S(1)}, bf16[512,128]{1,0:T(8,128)(2,1)S(1)}, u32[]{:S(2)}, u32[]{:S(2)}) %collective-permute-start.17) | collective-permute-done | bytes 131104 | tf_op jit(solution)/shard_map/ppermute | solution.py:389
  173.3 2.0 collective-permute-done.18.refs_3_
  176.0 2.8 %shard_map.108.refs_0_ = bf16[1024,256]{1,0:T(8,128)(2,1)} custom-call(s32[3]{0:T(128)} %pad_add_fusion.meta_ref, bf16[512,128]{1,0:T(8,128)(2,1)} %get-tuple-element.51.refs_0_, bf16[512,128]{1,0:T(8,128)(2,1)} %copy-done.21, bf16[512,128]{1,0:T(8,128)(2,1)} %copy-done.23, bf16[512,128]{1,0:T(8,128)(2,1)} %copy-done.25), custom_call_target="tpu_custom_call" | custom-call | tf_op jit(solution)/shard_map/pallas_call | solution.py:36
  180.3 11.3 %collective-permute-done.20.refs_2_ = bf16[1024,256]{1,0:T(8,128)(2,1)S(1)} collective-permute-done((bf16[1024,256]{1,0:T(8,128)(2,1)}, bf16[1024,256]{1,0:T(8,128)(2,1)S(1)}, u32[]{:S(2)}, u32[]{:S(2)}) %collective-permute-start.20) | collective-permute-done | bytes 524320 | tf_op jit(solution)/shard_map/ppermute | solution.py:373
  192.3 2.3 %collective-permute-start.23 = (bf16[512,128]{1,0:T(8,128)(2,1)}, bf16[512,128]{1,0:T(8,128)(2,1)S(1)}, u32[]{:S(2)}, u32[]{:S(2)}) collective-permute-start(bf16[512,128]{1,0:T(8,128)(2,1)} %get-tuple-element.58), channel_id=1, source_target_pairs={{0,8},{4,12},{8,0},{12,4},{16,24},{20,28},{24,16},{28,20},{1,9},{5... | collective-permute-start | bytes 393224 | tf_op jit(solution)/shard_map/ppermute | solution.py:389
  195.7 2.1 collective-permute-done.22.refs_1_
  198.9 3.7 %collective-permute-done.24.refs_3_ = bf16[512,128]{1,0:T(8,128)(2,1)S(1)} collective-permute-done((bf16[512,128]{1,0:T(8,128)(2,1)}, bf16[512,128]{1,0:T(8,128)(2,1)S(1)}, u32[]{:S(2)}, u32[]{:S(2)}) %collective-permute-start.24) | collective-permute-done | bytes 131104 | tf_op jit(solution)/shard_map/ppermute | solution.py:389
  203.3 2.8 %shard_map.111 = bf16[1024,256]{1,0:T(8,128)(2,1)} custom-call(s32[3]{0:T(128)} %pad_add_fusion.meta_ref, bf16[512,128]{1,0:T(8,128)(2,1)} %get-tuple-element.56.refs_0_, bf16[512,128]{1,0:T(8,128)(2,1)} %copy-done.22, bf16[512,128]{1,0:T(8,128)(2,1)} %copy-done.24, bf16[512,128]{1,0:T(8,128)(2,1)} %copy-done.26), custom_call_target="tpu_custom_call" | custom-call | tf_op jit(solution)/shard_map/pallas_call | solution.py:36
  207.7 3.8 %shard_map.109 = bf16[1024,256]{1,0:T(8,128)(2,1)} custom-call(s32[3]{0:T(128)} %pad_add_fusion.meta_ref, bf16[1024,256]{1,0:T(8,128)(2,1)} %shard_map.108.refs_0_, bf16[1024,256]{1,0:T(8,128)(2,1)} %copy-done.16, bf16[1024,256]{1,0:T(8,128)(2,1)} %copy-done.15, bf16[1024,256]{1,0:T(8,128)(2,1)} %copy-done.17, bf16[1024,1024]{1,0:T(8,128)(2,1)} %refs_4_.1), custom_call_target="tpu_custom_call" | custom-call | tf_op jit(solution)/shard_map/pallas_call | solution.py:36
  211.5 2.0 shard_map.112
  214.6 2.0 shard_map.113
  (96 shorter events, 21.8 us)
Async XLA Ops:
  2.8 62.0 %all-to-all-start = ((bf16[8,512,128]{2,1,0:T(8,128)(2,1)}), bf16[8,512,128]{2,1,0:T(8,128)(2,1)S(1)}, u32[]{:S(2)}, u32[]{:S(2)}) async-start(bf16[8,512,128]{2,1,0:T(8,128)(2,1)} %bitcast.6), calls=%async_computation | async-start | bytes 2097152 | tf_op jit(solution)/shard_map/all_to_all | solution.py:385
  10.1 13.6 %collective-permute-start.8 = (bf16[1024,256]{1,0:T(8,128)(2,1)}, bf16[1024,256]{1,0:T(8,128)(2,1)S(1)}, u32[]{:S(2)}, u32[]{:S(2)}) collective-permute-start(bf16[1024,256]{1,0:T(8,128)(2,1)} %own_ref.1), channel_id=1, source_target_pairs={{0,2},{1,3},{2,0},{3,1},{4,6},{5,7},{6,4},{7,5},{8,10},{9,11},{10,... | collective-permute-start | bytes 1572872 | tf_op jit(solution)/shard_map/ppermute | solution.py:373
  11.6 30.1 %collective-permute-start.7 = (bf16[1024,256]{1,0:T(8,128)(2,1)}, bf16[1024,256]{1,0:T(8,128)(2,1)S(1)}, u32[]{:S(2)}, u32[]{:S(2)}) collective-permute-start(bf16[1024,256]{1,0:T(8,128)(2,1)} %own_ref.1), channel_id=1, source_target_pairs={{0,1},{1,0},{2,3},{3,2},{4,5},{5,4},{6,7},{7,6},{8,9},{9,8},{10,11... | collective-permute-start | bytes 1572872 | tf_op jit(solution)/shard_map/ppermute | solution.py:373
  23.7 21.2 %collective-permute-start.9 = (bf16[1024,256]{1,0:T(8,128)(2,1)S(1)}, bf16[1024,256]{1,0:T(8,128)(2,1)S(1)}, u32[]{:S(2)}, u32[]{:S(2)}) collective-permute-start(bf16[1024,256]{1,0:T(8,128)(2,1)S(1)} %collective-permute-done.8.refs_1_), channel_id=1, source_target_pairs={{0,1},{1,0},{2,3},{3,2},{4,5},{5,4},{6,7},{7,6},{8,9},{9,8},{10,11... | collective-permute-start | bytes 1572872 | tf_op jit(solution)/shard_map/ppermute | solution.py:373
  27.1 7.1 %collective-permute-start.13 = (bf16[512,128]{1,0:T(8,128)(2,1)}, bf16[512,128]{1,0:T(8,128)(2,1)S(1)}, u32[]{:S(2)}, u32[]{:S(2)}) collective-permute-start(bf16[512,128]{1,0:T(8,128)(2,1)} %get-tuple-element.46), channel_id=1, source_target_pairs={{0,4},{4,0},{8,12},{12,8},{16,20},{20,16},{24,28},{28,24},{1,5},{5... | collective-permute-start | bytes 393224 | tf_op jit(solution)/shard_map/ppermute | solution.py:389
  28.8 9.9 %collective-permute-start.14 = (bf16[512,128]{1,0:T(8,128)(2,1)}, bf16[512,128]{1,0:T(8,128)(2,1)S(1)}, u32[]{:S(2)}, u32[]{:S(2)}) collective-permute-start(bf16[512,128]{1,0:T(8,128)(2,1)} %get-tuple-element.47), channel_id=1, source_target_pairs={{0,8},{4,12},{8,0},{12,4},{16,24},{20,28},{24,16},{28,20},{1,9},{5... | collective-permute-start | bytes 393224 | tf_op jit(solution)/shard_map/ppermute | solution.py:389
  30.3 9.7 %collective-permute-start.15 = (bf16[512,128]{1,0:T(8,128)(2,1)}, bf16[512,128]{1,0:T(8,128)(2,1)S(1)}, u32[]{:S(2)}, u32[]{:S(2)}) collective-permute-start(bf16[512,128]{1,0:T(8,128)(2,1)} %get-tuple-element.48), channel_id=1, source_target_pairs={{0,12},{4,8},{8,4},{12,0},{16,28},{20,24},{24,20},{28,16},{1,13},{... | collective-permute-start | bytes 393224 | tf_op jit(solution)/shard_map/ppermute | solution.py:389
  34.2 30.6 %copy-start.18 = (bf16[512,128]{1,0:T(8,128)(2,1)}, bf16[512,128]{1,0:T(8,128)(2,1)S(1)}, u32[]{:S(2)}) copy-start(bf16[512,128]{1,0:T(8,128)(2,1)S(1)} %collective-permute-done.13.refs_1_.refs_9_) | copy-start | bytes 393220
  34.2 16.0 %collective-permute-start = (bf16[512,128]{1,0:T(8,128)(2,1)}, bf16[512,128]{1,0:T(8,128)(2,1)S(1)}, u32[]{:S(2)}, u32[]{:S(2)}) collective-permute-start(bf16[512,128]{1,0:T(8,128)(2,1)} %get-tuple-element.34), channel_id=1, source_target_pairs={{0,4},{4,0},{8,12},{12,8},{16,20},{20,16},{24,28},{28,24},{1,5},{5... | collective-permute-start | bytes 393224 | tf_op jit(solution)/shard_map/ppermute | solution.py:389
  38.7 13.7 %collective-permute-start.1 = (bf16[512,128]{1,0:T(8,128)(2,1)}, bf16[512,128]{1,0:T(8,128)(2,1)S(1)}, u32[]{:S(2)}, u32[]{:S(2)}) collective-permute-start(bf16[512,128]{1,0:T(8,128)(2,1)} %get-tuple-element.35), channel_id=1, source_target_pairs={{0,8},{4,12},{8,0},{12,4},{16,24},{20,28},{24,16},{28,20},{1,9},{5... | collective-permute-start | bytes 393224 | tf_op jit(solution)/shard_map/ppermute | solution.py:389
  40.7 13.8 %collective-permute-start.2 = (bf16[512,128]{1,0:T(8,128)(2,1)}, bf16[512,128]{1,0:T(8,128)(2,1)S(1)}, u32[]{:S(2)}, u32[]{:S(2)}) collective-permute-start(bf16[512,128]{1,0:T(8,128)(2,1)} %get-tuple-element.36), channel_id=1, source_target_pairs={{0,12},{4,8},{8,4},{12,0},{16,28},{20,24},{24,20},{28,16},{1,13},{... | collective-permute-start | bytes 393224 | tf_op jit(solution)/shard_map/ppermute | solution.py:389
  41.7 13.9 %collective-permute-start.3 = (bf16[512,128]{1,0:T(8,128)(2,1)}, bf16[512,128]{1,0:T(8,128)(2,1)S(1)}, u32[]{:S(2)}, u32[]{:S(2)}) collective-permute-start(bf16[512,128]{1,0:T(8,128)(2,1)} %get-tuple-element.37), channel_id=1, source_target_pairs={{0,16},{4,20},{8,24},{12,28},{16,0},{20,4},{24,8},{28,12},{1,17},{... | collective-permute-start | bytes 393224 | tf_op jit(solution)/shard_map/ppermute | solution.py:389
  44.9 19.9 %collective-permute-start.4 = (bf16[512,128]{1,0:T(8,128)(2,1)}, bf16[512,128]{1,0:T(8,128)(2,1)S(1)}, u32[]{:S(2)}, u32[]{:S(2)}) collective-permute-start(bf16[512,128]{1,0:T(8,128)(2,1)} %get-tuple-element.38), channel_id=1, source_target_pairs={{0,20},{4,16},{8,28},{12,24},{16,4},{20,0},{24,12},{28,8},{1,21},{... | collective-permute-start | bytes 393224 | tf_op jit(solution)/shard_map/ppermute | solution.py:389
  50.2 31.2 %copy-start.2 = (bf16[512,128]{1,0:T(8,128)(2,1)}, bf16[512,128]{1,0:T(8,128)(2,1)S(1)}, u32[]{:S(2)}) copy-start(bf16[512,128]{1,0:T(8,128)(2,1)S(1)} %collective-permute-done.refs_1_) | copy-start | bytes 393220
  50.2 31.1 %collective-permute-start.5 = (bf16[512,128]{1,0:T(8,128)(2,1)}, bf16[512,128]{1,0:T(8,128)(2,1)S(1)}, u32[]{:S(2)}, u32[]{:S(2)}) collective-permute-start(bf16[512,128]{1,0:T(8,128)(2,1)} %get-tuple-element.39), channel_id=1, source_target_pairs={{0,24},{4,28},{8,16},{12,20},{16,8},{20,12},{24,0},{28,4},{1,25},{... | collective-permute-start | bytes 393224 | tf_op jit(solution)/shard_map/ppermute | solution.py:389
  52.5 28.8 %collective-permute-start.6 = (bf16[512,128]{1,0:T(8,128)(2,1)}, bf16[512,128]{1,0:T(8,128)(2,1)S(1)}, u32[]{:S(2)}, u32[]{:S(2)}) collective-permute-start(bf16[512,128]{1,0:T(8,128)(2,1)} %get-tuple-element.40), channel_id=1, source_target_pairs={{0,28},{4,24},{8,20},{12,16},{16,12},{20,8},{24,4},{28,0},{1,29},{... | collective-permute-start | bytes 393224 | tf_op jit(solution)/shard_map/ppermute | solution.py:389
  54.5 26.9 %collective-permute-start.10 = (bf16[512,128]{1,0:T(8,128)(2,1)}, bf16[512,128]{1,0:T(8,128)(2,1)S(1)}, u32[]{:S(2)}, u32[]{:S(2)}) collective-permute-start(bf16[512,128]{1,0:T(8,128)(2,1)} %get-tuple-element.42), channel_id=1, source_target_pairs={{0,4},{4,0},{8,12},{12,8},{16,20},{20,16},{24,28},{28,24},{1,5},{5... | collective-permute-start | bytes 393224 | tf_op jit(solution)/shard_map/ppermute | solution.py:389
  55.6 25.8 %collective-permute-start.11 = (bf16[512,128]{1,0:T(8,128)(2,1)}, bf16[512,128]{1,0:T(8,128)(2,1)S(1)}, u32[]{:S(2)}, u32[]{:S(2)}) collective-permute-start(bf16[512,128]{1,0:T(8,128)(2,1)} %get-tuple-element.43), channel_id=1, source_target_pairs={{0,8},{4,12},{8,0},{12,4},{16,24},{20,28},{24,16},{28,20},{1,9},{5... | collective-permute-start | bytes 393224 | tf_op jit(solution)/shard_map/ppermute | solution.py:389
  64.8 16.6 %collective-permute-start.12 = (bf16[512,128]{1,0:T(8,128)(2,1)}, bf16[512,128]{1,0:T(8,128)(2,1)S(1)}, u32[]{:S(2)}, u32[]{:S(2)}) collective-permute-start(bf16[512,128]{1,0:T(8,128)(2,1)} %get-tuple-element.44), channel_id=1, source_target_pairs={{0,12},{4,8},{8,4},{12,0},{16,28},{20,24},{24,20},{28,16},{1,13},{... | collective-permute-start | bytes 393224 | tf_op jit(solution)/shard_map/ppermute | solution.py:389
  98.9 53.6 %copy-start.29 = (bf16[512,128]{1,0:T(8,128)(2,1)S(1)}, bf16[512,128]{1,0:T(8,128)(2,1)}, u32[]{:S(2)}) copy-start(bf16[512,128]{1,0:T(8,128)(2,1)} %get-tuple-element.52) | copy-start | bytes 393220
  98.9 55.6 %copy-start.28 = (bf16[512,128]{1,0:T(8,128)(2,1)S(1)}, bf16[512,128]{1,0:T(8,128)(2,1)}, u32[]{:S(2)}) copy-start(bf16[512,128]{1,0:T(8,128)(2,1)} %get-tuple-element.53) | copy-start | bytes 393220
  98.9 57.1 %copy-start.27 = (bf16[512,128]{1,0:T(8,128)(2,1)S(1)}, bf16[512,128]{1,0:T(8,128)(2,1)}, u32[]{:S(2)}) copy-start(bf16[512,128]{1,0:T(8,128)(2,1)} %get-tuple-element.54) | copy-start | bytes 393220
  148.9 64.7 %all-to-all-start.2 = ((bf16[8,512,128]{2,1,0:T(8,128)(2,1)}), bf16[8,512,128]{2,1,0:T(8,128)(2,1)S(1)}, u32[]{:S(2)}, u32[]{:S(2)}) async-start(bf16[8,512,128]{2,1,0:T(8,128)(2,1)} %get-tuple-element.61), calls=%async_computation.2 | async-start | bytes 2097152 | tf_op jit(solution)/shard_map/all_to_all | solution.py:385
  152.5 12.5 %collective-permute-start.16 = (bf16[512,128]{1,0:T(8,128)(2,1)S(1)}, bf16[512,128]{1,0:T(8,128)(2,1)S(1)}, u32[]{:S(2)}, u32[]{:S(2)}) collective-permute-start(bf16[512,128]{1,0:T(8,128)(2,1)S(1)} %copy-done.29), channel_id=1, source_target_pairs={{0,4},{4,0},{8,12},{12,8},{16,20},{20,16},{24,28},{28,24},{1,5},{5... | collective-permute-start | bytes 393224 | tf_op jit(solution)/shard_map/ppermute | solution.py:389
  154.5 18.8 %collective-permute-start.17 = (bf16[512,128]{1,0:T(8,128)(2,1)S(1)}, bf16[512,128]{1,0:T(8,128)(2,1)S(1)}, u32[]{:S(2)}, u32[]{:S(2)}) collective-permute-start(bf16[512,128]{1,0:T(8,128)(2,1)S(1)} %copy-done.28), channel_id=1, source_target_pairs={{0,8},{4,12},{8,0},{12,4},{16,24},{20,28},{24,16},{28,20},{1,9},{5... | collective-permute-start | bytes 393224 | tf_op jit(solution)/shard_map/ppermute | solution.py:389
  156.0 19.3 %collective-permute-start.18 = (bf16[512,128]{1,0:T(8,128)(2,1)S(1)}, bf16[512,128]{1,0:T(8,128)(2,1)S(1)}, u32[]{:S(2)}, u32[]{:S(2)}) collective-permute-start(bf16[512,128]{1,0:T(8,128)(2,1)S(1)} %copy-done.27), channel_id=1, source_target_pairs={{0,12},{4,8},{8,4},{12,0},{16,28},{20,24},{24,20},{28,16},{1,13},{... | collective-permute-start | bytes 393224 | tf_op jit(solution)/shard_map/ppermute | solution.py:389
  178.8 12.9 %collective-permute-start.20 = (bf16[1024,256]{1,0:T(8,128)(2,1)}, bf16[1024,256]{1,0:T(8,128)(2,1)S(1)}, u32[]{:S(2)}, u32[]{:S(2)}) collective-permute-start(bf16[1024,256]{1,0:T(8,128)(2,1)} %shard_map.108.refs_0_), channel_id=1, source_target_pairs={{0,2},{1,3},{2,0},{3,1},{4,6},{5,7},{6,4},{7,5},{8,10},{9,11},{10,... | collective-permute-start | bytes 1572872 | tf_op jit(solution)/shard_map/ppermute | solution.py:373
  180.3 25.8 %collective-permute-start.19 = (bf16[1024,256]{1,0:T(8,128)(2,1)}, bf16[1024,256]{1,0:T(8,128)(2,1)S(1)}, u32[]{:S(2)}, u32[]{:S(2)}) collective-permute-start(bf16[1024,256]{1,0:T(8,128)(2,1)} %shard_map.108.refs_0_), channel_id=1, source_target_pairs={{0,1},{1,0},{2,3},{3,2},{4,5},{5,4},{6,7},{7,6},{8,9},{9,8},{10,11... | collective-permute-start | bytes 1572872 | tf_op jit(solution)/shard_map/ppermute | solution.py:373
  191.7 14.5 %collective-permute-start.21 = (bf16[1024,256]{1,0:T(8,128)(2,1)S(1)}, bf16[1024,256]{1,0:T(8,128)(2,1)S(1)}, u32[]{:S(2)}, u32[]{:S(2)}) collective-permute-start(bf16[1024,256]{1,0:T(8,128)(2,1)S(1)} %collective-permute-done.20.refs_2_), channel_id=1, source_target_pairs={{0,1},{1,0},{2,3},{3,2},{4,5},{5,4},{6,7},{7,6},{8,9},{9,8},{10,11... | collective-permute-start | bytes 1572872 | tf_op jit(solution)/shard_map/ppermute | solution.py:373
  191.7 6.1 %collective-permute-start.22 = (bf16[512,128]{1,0:T(8,128)(2,1)}, bf16[512,128]{1,0:T(8,128)(2,1)S(1)}, u32[]{:S(2)}, u32[]{:S(2)}) collective-permute-start(bf16[512,128]{1,0:T(8,128)(2,1)} %get-tuple-element.57), channel_id=1, source_target_pairs={{0,4},{4,0},{8,12},{12,8},{16,20},{20,16},{24,28},{28,24},{1,5},{5... | collective-permute-start | bytes 393224 | tf_op jit(solution)/shard_map/ppermute | solution.py:389
  192.3 6.6 %collective-permute-start.23 = (bf16[512,128]{1,0:T(8,128)(2,1)}, bf16[512,128]{1,0:T(8,128)(2,1)S(1)}, u32[]{:S(2)}, u32[]{:S(2)}) collective-permute-start(bf16[512,128]{1,0:T(8,128)(2,1)} %get-tuple-element.58), channel_id=1, source_target_pairs={{0,8},{4,12},{8,0},{12,4},{16,24},{20,28},{24,16},{28,20},{1,9},{5... | collective-permute-start | bytes 393224 | tf_op jit(solution)/shard_map/ppermute | solution.py:389
  194.6 8.0 %collective-permute-start.24 = (bf16[512,128]{1,0:T(8,128)(2,1)}, bf16[512,128]{1,0:T(8,128)(2,1)S(1)}, u32[]{:S(2)}, u32[]{:S(2)}) collective-permute-start(bf16[512,128]{1,0:T(8,128)(2,1)} %get-tuple-element.59), channel_id=1, source_target_pairs={{0,12},{4,8},{8,4},{12,0},{16,28},{20,24},{24,20},{28,16},{1,13},{... | collective-permute-start | bytes 393224 | tf_op jit(solution)/shard_map/ppermute | solution.py:389
  (25 other events, 197.3 us)
